TPU v7x, 32 devices: a whole 2x2x4 slice. The times are simulated.
32 devices in a mesh: lat: 4 (over y, x), lon: 8 (over z, core).
Axes of the slice: x: 2, y: 2, z: 4, core: 2. Of those that a mesh axis runs over, the one named last changes fastest.
Arguments:
- grid_latent: float32 [64, 360, 512], P('lat', 'lon'), may hold values from -6 to 6
- mesh_latent: float32 [20480, 512], P(('lat', 'lon')), may hold values from -6 to 6
- grid_senders: int32 [32, 32, 8], P(('lat', 'lon')), may hold values from 0 to 719
- grid_targets: int32 [32, 256], P(('lat', 'lon')), may hold values from -1 to 639, as said below
- grid_geometry: float32 [4, 32, 256], P(None, ('lat', 'lon')), may hold values from -6 to 6
- mesh_senders: int32 [32, 32, 8], P(('lat', 'lon')), may hold values from 0 to 639
- mesh_targets: int32 [32, 256], P(('lat', 'lon')), may hold values from -1 to 639, as said below
- mesh_geometry: float32 [4, 32, 256], P(None, ('lat', 'lon')), may hold values from -6 to 6
- encoder_sender: float32 [512, 512], replicated, may hold values from -0.25 to 0.25
- encoder_receiver: float32 [512, 512], replicated, may hold values from -0.25 to 0.25
- encoder_geometry: float32 [4, 512], replicated, may hold values from -3 to 3
- encoder_bias: float32 [512], replicated, may hold values from -3 to 3
- encoder_output: float32 [512, 512], replicated, may hold values from -0.25 to 0.25
- encoder_outbias: float32 [512], replicated, may hold values from -3 to 3
- update_self: float32 [512, 512], replicated, may hold values from -0.25 to 0.25
- update_summed: float32 [512, 512], replicated, may hold values from -0.25 to 0.25
- update_bias: float32 [512], replicated, may hold values from -3 to 3
- update_output: float32 [512, 512], replicated, may hold values from -0.25 to 0.25
- update_outbias: float32 [512], replicated, may hold values from -3 to 3
- process_sender: float32 [512, 512], replicated, may hold values from -0.25 to 0.25
- process_receiver: float32 [512, 512], replicated, may hold values from -0.25 to 0.25
- process_geometry: float32 [4, 512], replicated, may hold values from -3 to 3
- process_bias: float32 [512], replicated, may hold values from -3 to 3
- process_output: float32 [512, 512], replicated, may hold values from -0.25 to 0.25
- process_outbias: float32 [512], replicated, may hold values from -3 to 3
- refine_self: float32 [512, 512], replicated, may hold values from -0.25 to 0.25
- refine_summed: float32 [512, 512], replicated, may hold values from -0.25 to 0.25
- refine_bias: float32 [512], replicated, may hold values from -3 to 3
- refine_output: float32 [512, 512], replicated, may hold values from -0.25 to 0.25
- refine_outbias: float32 [512], replicated, may hold values from -3 to 3
Outputs:
- mesh_output: float32 [20480, 512], P(('lat', 'lon'))
Inputs may be any that keep to these rules, and one draw needn't show every extreme that they name: `grid_targets`: entry [q, p * 8 + c] is the index among patch q's 640 nodes of the mesh node that receives grid edge slot c from patch p, or -1 for an empty slot; the live slots of a pair come first, and every patch's slots from itself are all live. `grid_senders`: entry [p, q, c] is the index of the sending cell among patch p's tile cells; entries of empty slots are ignored. `mesh_targets`: entry [q, p * 8 + c] is the index among patch q's 640 nodes of the mesh node that receives mesh edge slot c from patch p, or -1 for an empty slot; the live slots of a pair come first, and every patch's slots from itself are all live. `mesh_senders`: entry [p, q, c] is the index of the sending node among patch p's 640 nodes; entries of empty slots are ignored.
All inputs are finite; a program needn't handle non-finite values.
Results may differ from a plain program's by a relative error of at most 0.0003.
Values sent between devices are 32-bit elements; how exact they have to be, the bound alone decides.
No kernel may reach another device: no remote copies, remote signals or barrier semaphores. Data moves between devices by JAX's collectives and lax.ppermute only.
A program may use at most 128 MiB of HBM per device.

v0:
```python
import jax
import jax.numpy as jnp
from jax import lax
from jax.sharding import PartitionSpec as P

PRECISE = lax.Precision.HIGHEST


def matmul(left, right):
    return jnp.dot(left, right, precision=PRECISE, preferred_element_type=jnp.float32)


def norm_rows(values):
    average = jnp.mean(values, axis=-1, keepdims=True)
    centred = values - average
    spread = jnp.mean(centred * centred, axis=-1, keepdims=True)
    return centred * lax.rsqrt(spread + 1e-05)


def edge_block(
    sender_rows, receiver_rows, geometry, weight_geometry, bias_hidden, weight_output, bias_output
):
    geometric = lax.dot_general(
        geometry,
        weight_geometry,
        (((0,), (0,)), ((), ())),
        precision=PRECISE,
        preferred_element_type=jnp.float32,
    )
    hidden = jax.nn.silu(sender_rows + receiver_rows + geometric + bias_hidden)
    return norm_rows(matmul(hidden, weight_output) + bias_output)


def aggregate(messages, targets, number):
    one_hot = (jnp.arange(number, dtype=jnp.int32)[:, None] == targets[None, :]).astype(jnp.float32)
    return matmul(one_hot, messages)


def node_block(latent, summed, weight_self, weight_summed, bias_hidden, weight_output, bias_output):
    hidden = jax.nn.silu(matmul(latent, weight_self) + matmul(summed, weight_summed) + bias_hidden)
    return latent + norm_rows(matmul(hidden, weight_output) + bias_output)


def finish_patch(
    nodes,
    sender_rows,
    targets,
    geometry,
    weight_receiver,
    weight_geometry,
    edge_bias,
    edge_output,
    edge_outbias,
    weight_self,
    weight_summed,
    node_bias,
    node_output,
    node_outbias,
):
    receiver_rows = matmul(nodes, weight_receiver)[jnp.maximum(targets, 0)]
    messages = edge_block(
        sender_rows, receiver_rows, geometry, weight_geometry, edge_bias, edge_output, edge_outbias
    )
    summed = aggregate(messages, targets, nodes.shape[0])
    return node_block(
        nodes, summed, weight_self, weight_summed, node_bias, node_output, node_outbias
    )


def per_device(
    grid_latent,
    mesh_latent,
    grid_senders,
    grid_targets,
    grid_geometry,
    mesh_senders,
    mesh_targets,
    mesh_geometry,
    encoder_sender,
    encoder_receiver,
    encoder_geometry,
    encoder_bias,
    encoder_output,
    encoder_outbias,
    update_self,
    update_summed,
    update_bias,
    update_output,
    update_outbias,
    process_sender,
    process_receiver,
    process_geometry,
    process_bias,
    process_output,
    process_outbias,
    refine_self,
    refine_summed,
    refine_bias,
    refine_output,
    refine_outbias,
):
    width = mesh_latent.shape[1]
    lat_count = lax.axis_size("lat")
    lon_count = lax.axis_size("lon")
    local_grid = grid_latent.reshape(-1, width)
    grid_capacity = grid_senders.shape[2]
    mesh_capacity = mesh_senders.shape[2]
    grid_index = grid_senders.reshape(-1)
    grid_rows = local_grid[grid_index]
    grid_out = grid_rows.reshape(lat_count, lon_count, grid_capacity, width)
    grid_in = lax.all_to_all(
        grid_out.reshape(lat_count * lon_count, grid_capacity, width),
        ("lat", "lon"),
        split_axis=0,
        concat_axis=0,
        tiled=True,
    )
    grid_in = grid_in.reshape(-1, width)
    grid_sent = matmul(grid_in, encoder_sender)
    encoded = finish_patch(
        mesh_latent,
        grid_sent,
        grid_targets.reshape(-1),
        grid_geometry[:, 0, :],
        encoder_receiver,
        encoder_geometry,
        encoder_bias,
        encoder_output,
        encoder_outbias,
        update_self,
        update_summed,
        update_bias,
        update_output,
        update_outbias,
    )
    mesh_index = mesh_senders.reshape(-1)
    mesh_rows = encoded[mesh_index]
    mesh_out = mesh_rows.reshape(lat_count, lon_count, mesh_capacity, width)
    mesh_in = lax.all_to_all(
        mesh_out.reshape(lat_count * lon_count, mesh_capacity, width),
        ("lat", "lon"),
        split_axis=0,
        concat_axis=0,
        tiled=True,
    )
    mesh_in = mesh_in.reshape(-1, width)
    mesh_sent = matmul(mesh_in, process_sender)
    return finish_patch(
        encoded,
        mesh_sent,
        mesh_targets.reshape(-1),
        mesh_geometry[:, 0, :],
        process_receiver,
        process_geometry,
        process_bias,
        process_output,
        process_outbias,
        refine_self,
        refine_summed,
        refine_bias,
        refine_output,
        refine_outbias,
    )


def solution(mesh):
    return jax.shard_map(
        per_device,
        mesh=mesh,
        in_specs=(
            P("lat", "lon", None),
            P(("lat", "lon"), None),
            P(("lat", "lon"), None, None),
            P(("lat", "lon"), None),
            P(None, ("lat", "lon"), None),
            P(("lat", "lon"), None, None),
            P(("lat", "lon"), None),
            P(None, ("lat", "lon"), None),
            P(),
            P(),
            P(),
            P(),
            P(),
            P(),
            P(),
            P(),
            P(),
            P(),
            P(),
            P(),
            P(),
            P(),
            P(),
            P(),
            P(),
            P(),
            P(),
            P(),
            P(),
            P(),
        ),
        out_specs=P(("lat", "lon"), None),
        check_vma=False,
    )
```

profile of v0, /device:TPU:0, one launch (start us, length us, event | category | flops | bytes accessed | tf_op | source)
XLA Modules:
  0.0 81.7 jit_solution(14086365279048289807)
XLA Ops:
  0.0 0.0 copy-start
  0.0 3.5 %copy.35 = f32[16,45,512]{2,1,0:T(8,128)} copy(f32[16,45,512]{2,0,1:T(8,128)} %param.30) | data formatting | bytes 2949120 | tf_op args[0]
  3.5 1.6 %reshape.153 = f32[720,512]{1,0:T(8,128)S(1)} reshape(f32[16,45,512]{2,1,0:T(8,128)} %copy.35) | data formatting | bytes 2949120 | tf_op jit(solution)/shard_map/reshape | solution.py:105
  5.1 0.0 copy-done.11
  5.1 0.1 copy.36
  5.2 0.1 reshape.154
  5.3 1.8 %gather_fusion = f32[256,512]{1,0:T(8,128)} fusion(f32[720,512]{1,0:T(8,128)S(1)} %reshape.153, s32[1024]{0:T(1024)S(1)} %pad_clamp_fusion.3), kind=kCustom, calls=%fused_computation | custom fusion | bytes 1049600 | tf_op jit(solution)/shard_map/gather | solution.py:109
  7.0 7.3 %all-to-all-start = ((f32[32,8,512]{2,1,0:T(8,128)}), f32[32,8,512]{2,1,0:T(8,128)S(1)}, u32[]{:S(2)}, u32[]{:S(2)}) async-start(f32[32,8,512]{2,1,0:T(8,128)} %bitcast.2), calls=%async_computation | async-start | bytes 1048576 | tf_op jit(solution)/shard_map/all_to_all | solution.py:111
  14.4 0.0 copy-start.9
  14.4 3.9 %fusion.59 = f32[640,512]{1,0:T(8,128)S(1)} fusion(f32[640,512]{1,0:T(8,128)} %param.31, f32[512,512]{1,0:T(8,128)} %param.39), kind=kOutput, calls=%fused_computation.95 | convolution fusion | flops 2013265920 | bytes 3670016 | tf_op jit(solution)/shard_map/dot_general | solution.py:10
  18.3 0.0 copy-done.9
  18.3 0.0 copy-start.12
  18.3 2.8 %copy.37 = f32[640,512]{0,1:T(8,128)} copy(f32[640,512]{1,0:T(8,128)} %param.31) | data formatting | bytes 2621440 | tf_op args[1]
  21.1 0.0 copy-done.12
  21.1 0.1 copy.38
  21.2 0.1 reshape.156
  21.3 0.0 copy-start.5
  21.3 0.0 copy-start.7
  21.3 1.0 %gather_fusion.1 = f32[256,512]{1,0:T(8,128)S(1)} fusion(f32[640,512]{1,0:T(8,128)S(1)} %fusion.59, s32[1024]{0:T(1024)S(1)} %pad_clamp_fusion.2), kind=kCustom, calls=%fused_computation.1 | custom fusion | bytes 1049600 | tf_op jit(solution)/shard_map/gather | solution.py:60
  22.3 0.0 copy-done.5
  22.3 0.0 copy-done.7
  22.3 1.4 %fusion.47 = f32[256,512]{1,0:T(8,128)} fusion(f32[4,512]{1,0:T(4,128)S(1)} %copy-done.5, f32[4,1,256]{2,1,0:T(1,128)S(1)} %copy-done.7), kind=kOutput, calls=%fused_computation.73 | convolution fusion | flops 6291456 | bytes 536576 | tf_op jit(solution)/shard_map/dot_general | solution.py:23
  23.7 3.9 %fusion.58 = f32[640,512]{1,0:T(8,128)S(1)} fusion(f32[640,512]{1,0:T(8,128)} %param.31, f32[512,512]{1,0:T(8,128)} %param.44), kind=kOutput, calls=%fused_computation.94 | convolution fusion | flops 2013265920 | bytes 3670016 | tf_op jit(solution)/shard_map/dot_general | solution.py:10
  27.6 0.0 copy-start.20
  27.6 3.0 %all-to-all-done = f32[32,8,512]{2,1,0:T(8,128)S(1)} async-done(((f32[32,8,512]{2,1,0:T(8,128)}), f32[32,8,512]{2,1,0:T(8,128)S(1)}, u32[]{:S(2)}, u32[]{:S(2)}) %all-to-all-start) | async-done | bytes 524320 | tf_op jit(solution)/shard_map/all_to_all | solution.py:111
  30.6 0.0 copy-done.15
  30.6 2.5 %fusion.15 = f32[256,512]{1,0:T(8,128)S(1)} fusion(f32[256,512]{1,0:T(8,128)} %fusion.47, f32[256,512]{1,0:T(8,128)S(1)} %gather_fusion.1, f32[512,512]{1,0:T(8,128)} %param.38, f32[32,8,512]{2,1,0:T(8,128)S(1)} %all-to-all-done, f32[512]{0:T(512)S(1)} %copy-done.15), kind=kOutput, calls=%fused_computation.31 | convolution fusion | flops 805699584 | bytes 3147776 | tf_op jit(solution)/shard_map/dot_general | solution.py:10
  33.1 0.0 copy-done.20
  33.1 0.0 copy-done.17
  33.2 1.2 %fusion.54 = (f32[256]{0:T(256)S(1)}, f32[256,512]{1,0:T(8,128)S(1)}) fusion(f32[512]{0:T(512)S(1)} %copy-done.20, f32[512,512]{1,0:T(8,128)S(1)} %copy-done.17, f32[256,512]{1,0:T(8,128)S(1)} %fusion.15), kind=kOutput, calls=%fused_computation.90 | convolution fusion | flops 806092544 | bytes 2100224 | tf_op jit(solution)/shard_map/dot_general | solution.py:10
  34.4 0.0 copy-start.13
  34.4 0.2 multiply_reduce_fusion.3
  34.6 0.9 %fusion.18 = f32[640,512]{1,0:T(8,128)S(1)} fusion(f32[256,512]{1,0:T(8,128)S(1)} %get-tuple-element.6, s32[256]{0:T(256)S(1)} %bitcast.40, f32[256]{0:T(256)S(1)} %add_rsqrt_fusion.3, f32[256]{0:T(256)S(1)} %broadcast_multiply_fusion.3), kind=kOutput, calls=%fused_computation.36 | convolution fusion | flops 1007058944 | bytes 1838080 | tf_op jit(solution)/shard_map/dot_general | solution.py:10
  35.5 0.1 copy-done.3
  35.6 2.3 %fusion.1 = f32[640,512]{1,0:T(8,128)S(1)} fusion(f32[640,512]{1,0:T(8,128)S(1)} %fusion.58, f32[640,512]{1,0:T(8,128)S(1)} %fusion.18, f32[512,512]{1,0:T(8,128)S(1)} %copy-done.3, f32[512]{0:T(512)S(1)} %copy-done.13), kind=kOutput, calls=%fused_computation.9 | convolution fusion | flops 2013921280 | bytes 4982784 | tf_op jit(solution)/shard_map/dot_general | solution.py:10
  37.9 3.2 %fusion.55 = (f32[640]{0:T(1024)S(1)}, f32[640,512]{0,1:T(8,128)S(1)}) fusion(f32[512]{0:T(512)S(1)} %copy-done.21, f32[512,512]{1,0:T(8,128)S(1)} %copy-done, f32[640,512]{1,0:T(8,128)S(1)} %fusion.1), kind=kOutput, calls=%fused_computation.91 | convolution fusion | flops 2015231360 | bytes 3674624 | tf_op jit(solution)/shard_map/dot_general | solution.py:10
  41.1 0.2 multiply_reduce_fusion.1
  41.3 1.1 %copy-done.2 = f32[640,512]{0,1:T(8,128)S(1)} copy-done((f32[640,512]{0,1:T(8,128)S(1)}, f32[640,512]{0,1:T(8,128)}, u32[]{:S(2)}) %copy-start.2) | copy-done | bytes 1310744
  42.4 0.1 multiply_add_fusion.1
  42.6 1.5 %copy.39 = f32[640,512]{1,0:T(8,128)} copy(f32[640,512]{0,1:T(8,128)S(1)} %multiply_add_fusion.1) | data formatting | bytes 2621440 | tf_op jit(solution)/shard_map/add | solution.py:41
  44.0 3.4 %gather_fusion.2 = f32[256,512]{1,0:T(8,128)} fusion(f32[640,512]{1,0:T(8,128)} %copy.39, s32[1024]{0:T(1024)S(1)} %pad_clamp_fusion.1), kind=kCustom, calls=%fused_computation.2 | custom fusion | bytes 1049600 | tf_op jit(solution)/shard_map/gather | solution.py:137
  47.4 2.9 %all-to-all-start.1 = ((f32[32,8,512]{2,1,0:T(8,128)}), f32[32,8,512]{2,1,0:T(8,128)S(1)}, u32[]{:S(2)}, u32[]{:S(2)}) async-start(f32[32,8,512]{2,1,0:T(8,128)} %bitcast.7), calls=%async_computation.1 | async-start | bytes 1048576 | tf_op jit(solution)/shard_map/all_to_all | solution.py:139
  50.3 1.4 %fusion.44 = f32[256,512]{1,0:T(8,128)} fusion(f32[4,512]{1,0:T(4,128)S(1)} %copy-done.6, f32[4,1,256]{2,1,0:T(1,128)S(1)} %copy-done.8), kind=kOutput, calls=%fused_computation.70 | convolution fusion | flops 6291456 | bytes 536576 | tf_op jit(solution)/shard_map/dot_general | solution.py:23
  51.8 4.5 %fusion.61 = f32[640,512]{1,0:T(8,128)} fusion(f32[640,512]{0,1:T(8,128)S(1)} %multiply_add_fusion.1, f32[512,512]{1,0:T(8,128)} %param.50), kind=kOutput, calls=%fused_computation.97 | convolution fusion | flops 2013265920 | bytes 3670016 | tf_op jit(solution)/shard_map/dot_general | solution.py:10
  56.3 2.5 %gather_fusion.3 = f32[256,512]{1,0:T(8,128)S(1)} fusion(f32[640,512]{1,0:T(8,128)} %fusion.61, s32[1024]{0:T(1024)S(1)} %pad_clamp_fusion), kind=kCustom, calls=%fused_computation.3 | custom fusion | bytes 1049600 | tf_op jit(solution)/shard_map/gather | solution.py:60
  58.8 0.0 copy-start.16
  58.8 4.5 %fusion.60 = f32[640,512]{1,0:T(8,128)} fusion(f32[640,512]{0,1:T(8,128)S(1)} %multiply_add_fusion.1, f32[512,512]{1,0:T(8,128)} %param.55), kind=kOutput, calls=%fused_computation.96 | convolution fusion | flops 2013265920 | bytes 3670016 | tf_op jit(solution)/shard_map/dot_general | solution.py:10
  63.4 3.1 %all-to-all-done.1 = f32[32,8,512]{2,1,0:T(8,128)S(1)} async-done(((f32[32,8,512]{2,1,0:T(8,128)}), f32[32,8,512]{2,1,0:T(8,128)S(1)}, u32[]{:S(2)}, u32[]{:S(2)}) %all-to-all-start.1) | async-done | bytes 524320 | tf_op jit(solution)/shard_map/all_to_all | solution.py:139
  66.5 2.5 %fusion.14 = f32[256,512]{1,0:T(8,128)S(1)} fusion(f32[256,512]{1,0:T(8,128)} %fusion.44, f32[256,512]{1,0:T(8,128)S(1)} %gather_fusion.3, f32[512,512]{1,0:T(8,128)} %param.49, f32[32,8,512]{2,1,0:T(8,128)S(1)} %all-to-all-done.1, f32[512]{0:T(512)S(1)} %copy-done.16), kind=kOutput, calls=%fused_computation.30 | convolution fusion | flops 805699584 | bytes 3147776 | tf_op jit(solution)/shard_map/dot_general | solution.py:10
  69.0 0.0 copy-done.22
  69.0 0.0 copy-done.18
  69.0 1.2 %fusion.56 = (f32[256]{0:T(256)S(1)}, f32[256,512]{1,0:T(8,128)S(1)}) fusion(f32[512]{0:T(512)S(1)} %copy-done.22, f32[512,512]{1,0:T(8,128)S(1)} %copy-done.18, f32[256,512]{1,0:T(8,128)S(1)} %fusion.14), kind=kOutput, calls=%fused_computation.92 | convolution fusion | flops 806092544 | bytes 2100224 | tf_op jit(solution)/shard_map/dot_general | solution.py:10
  70.3 0.0 copy-start.4
  70.3 0.0 copy-start.14
  70.3 0.2 multiply_reduce_fusion.2
  70.5 0.9 %fusion.19 = f32[640,512]{1,0:T(8,128)S(1)} fusion(f32[256,512]{1,0:T(8,128)S(1)} %get-tuple-element.10, s32[256]{0:T(256)S(1)} %bitcast.41, f32[256]{0:T(256)S(1)} %add_rsqrt_fusion.2, f32[256]{0:T(256)S(1)} %broadcast_multiply_fusion.2), kind=kOutput, calls=%fused_computation.37 | convolution fusion | flops 1007058944 | bytes 1838080 | tf_op jit(solution)/shard_map/dot_general | solution.py:10
  71.4 0.2 copy-done.1
  71.6 0.3 copy-done.4
  71.9 0.0 copy-done.14
  71.9 2.3 %fusion = f32[640,512]{1,0:T(8,128)S(1)} fusion(f32[640,512]{1,0:T(8,128)S(1)} %copy-done.1, f32[640,512]{1,0:T(8,128)S(1)} %fusion.19, f32[512,512]{1,0:T(8,128)S(1)} %copy-done.4, f32[512]{0:T(512)S(1)} %copy-done.14), kind=kOutput, calls=%fused_computation.6 | convolution fusion | flops 2013921280 | bytes 4982784 | tf_op jit(solution)/shard_map/dot_general | solution.py:10
  74.2 3.3 %fusion.57 = (f32[640]{0:T(1024)S(1)}, f32[640,512]{0,1:T(8,128)S(1)}) fusion(f32[512]{0:T(512)S(1)} %copy-done.23, f32[512,512]{1,0:T(8,128)S(1)} %copy-done.19, f32[640,512]{1,0:T(8,128)S(1)} %fusion), kind=kOutput, calls=%fused_computation.93 | convolution fusion | flops 2015231360 | bytes 3674624 | tf_op jit(solution)/shard_map/dot_general | solution.py:10
  77.5 0.2 multiply_reduce_fusion
  77.7 1.3 %multiply_add_fusion = f32[640,512]{0,1:T(8,128)} fusion(f32[640,512]{0,1:T(8,128)S(1)} %multiply_add_fusion.1, f32[640,512]{0,1:T(8,128)S(1)} %get-tuple-element.12, f32[640]{0:T(1024)S(1)} %add_rsqrt_fusion, f32[640]{0:T(1024)S(1)} %broadcast_multiply_fusion), kind=kLoop, calls=%fused_computation.10 | loop fusion | flops 983040 | bytes 3937280 | tf_op jit(solution)/shard_map/add | solution.py:41
  79.0 2.8 %copy.40 = f32[640,512]{1,0:T(8,128)} copy(f32[640,512]{0,1:T(8,128)} %multiply_add_fusion) | data formatting | bytes 2621440 | tf_op jit(solution)/shard_map/add | solution.py:41
  (39 shorter events, 0.1 us)
Async XLA Ops:
  0.0 37.9 %copy-start = (f32[512,512]{1,0:T(8,128)S(1)}, f32[512,512]{1,0:T(8,128)}, u32[]{:S(2)}) copy-start(f32[512,512]{1,0:T(8,128)} %param.47) | copy-start | bytes 3145732
  3.5 1.6 %copy-start.11 = (s32[1,32,8]{1,2,0:T(8,128)S(1)}, s32[1,32,8]{1,2,0:T(8,128)}, u32[]{:S(2)}) copy-start(s32[1,32,8]{1,2,0:T(8,128)} %param.32) | copy-start | bytes 3076
  7.0 23.6 %all-to-all-start = ((f32[32,8,512]{2,1,0:T(8,128)}), f32[32,8,512]{2,1,0:T(8,128)S(1)}, u32[]{:S(2)}, u32[]{:S(2)}) async-start(f32[32,8,512]{2,1,0:T(8,128)} %bitcast.2), calls=%async_computation | async-start | bytes 1048576 | tf_op jit(solution)/shard_map/all_to_all | solution.py:111
  14.4 3.9 %copy-start.9 = (s32[1,256]{1,0:T(1,128)S(1)}, s32[1,256]{1,0:T(1,128)}, u32[]{:S(2)}) copy-start(s32[1,256]{1,0:T(1,128)} %param.33) | copy-start | bytes 3076
  18.3 2.8 %copy-start.12 = (s32[1,32,8]{1,2,0:T(8,128)S(1)}, s32[1,32,8]{1,2,0:T(8,128)}, u32[]{:S(2)}) copy-start(s32[1,32,8]{1,2,0:T(8,128)} %param.35) | copy-start | bytes 3076
  21.3 1.0 %copy-start.5 = (f32[4,512]{1,0:T(4,128)S(1)}, f32[4,512]{1,0:T(4,128)}, u32[]{:S(2)}) copy-start(f32[4,512]{1,0:T(4,128)} %param.40) | copy-start | bytes 24580
  21.3 1.0 %copy-start.7 = (f32[4,1,256]{2,1,0:T(1,128)S(1)}, f32[4,1,256]{2,1,0:T(1,128)}, u32[]{:S(2)}) copy-start(f32[4,1,256]{2,1,0:T(1,128)} %param.34) | copy-start | bytes 12292
  23.7 6.9 %copy-start.15 = (f32[512]{0:T(512)S(1)}, f32[512]{0:T(512)}, u32[]{:S(2)}) copy-start(f32[512]{0:T(512)} %param.41) | copy-start | bytes 6148
  27.6 5.5 %copy-start.20 = (f32[512]{0:T(512)S(1)}, f32[512]{0:T(512)}, u32[]{:S(2)}) copy-start(f32[512]{0:T(512)} %param.43) | copy-start | bytes 6148
  30.6 2.5 %copy-start.17 = (f32[512,512]{1,0:T(8,128)S(1)}, f32[512,512]{1,0:T(8,128)}, u32[]{:S(2)}) copy-start(f32[512,512]{1,0:T(8,128)} %param.42) | copy-start | bytes 3145732
  34.4 1.2 %copy-start.3 = (f32[512,512]{1,0:T(8,128)S(1)}, f32[512,512]{1,0:T(8,128)}, u32[]{:S(2)}) copy-start(f32[512,512]{1,0:T(8,128)} %param.45) | copy-start | bytes 3145732
  34.4 1.2 %copy-start.13 = (f32[512]{0:T(512)S(1)}, f32[512]{0:T(512)}, u32[]{:S(2)}) copy-start(f32[512]{0:T(512)} %param.46) | copy-start | bytes 6148
  35.6 2.3 %copy-start.21 = (f32[512]{0:T(512)S(1)}, f32[512]{0:T(512)}, u32[]{:S(2)}) copy-start(f32[512]{0:T(512)} %param.48) | copy-start | bytes 6148
  41.1 1.3 %copy-start.2 = (f32[640,512]{0,1:T(8,128)S(1)}, f32[640,512]{0,1:T(8,128)}, u32[]{:S(2)}) copy-start(f32[640,512]{0,1:T(8,128)} %copy.37) | copy-start | bytes 3932164
  44.0 6.2 %copy-start.10 = (s32[1,256]{1,0:T(1,128)S(1)}, s32[1,256]{1,0:T(1,128)}, u32[]{:S(2)}) copy-start(s32[1,256]{1,0:T(1,128)} %param.36) | copy-start | bytes 3076
  44.0 6.3 %copy-start.6 = (f32[4,512]{1,0:T(4,128)S(1)}, f32[4,512]{1,0:T(4,128)}, u32[]{:S(2)}) copy-start(f32[4,512]{1,0:T(4,128)} %param.51) | copy-start | bytes 24580
  44.0 6.3 %copy-start.8 = (f32[4,1,256]{2,1,0:T(1,128)S(1)}, f32[4,1,256]{2,1,0:T(1,128)}, u32[]{:S(2)}) copy-start(f32[4,1,256]{2,1,0:T(1,128)} %param.37) | copy-start | bytes 12292
  47.4 19.1 %all-to-all-start.1 = ((f32[32,8,512]{2,1,0:T(8,128)}), f32[32,8,512]{2,1,0:T(8,128)S(1)}, u32[]{:S(2)}, u32[]{:S(2)}) async-start(f32[32,8,512]{2,1,0:T(8,128)} %bitcast.7), calls=%async_computation.1 | async-start | bytes 1048576 | tf_op jit(solution)/shard_map/all_to_all | solution.py:139
  58.8 7.7 %copy-start.16 = (f32[512]{0:T(512)S(1)}, f32[512]{0:T(512)}, u32[]{:S(2)}) copy-start(f32[512]{0:T(512)} %param.52) | copy-start | bytes 6148
  63.4 5.7 %copy-start.22 = (f32[512]{0:T(512)S(1)}, f32[512]{0:T(512)}, u32[]{:S(2)}) copy-start(f32[512]{0:T(512)} %param.54) | copy-start | bytes 6148
  66.5 2.5 %copy-start.18 = (f32[512,512]{1,0:T(8,128)S(1)}, f32[512,512]{1,0:T(8,128)}, u32[]{:S(2)}) copy-start(f32[512,512]{1,0:T(8,128)} %param.53) | copy-start | bytes 3145732
  70.3 1.3 %copy-start.1 = (f32[640,512]{1,0:T(8,128)S(1)}, f32[640,512]{1,0:T(8,128)}, u32[]{:S(2)}) copy-start(f32[640,512]{1,0:T(8,128)} %fusion.60) | copy-start | bytes 3932164
  70.3 1.6 %copy-start.4 = (f32[512,512]{1,0:T(8,128)S(1)}, f32[512,512]{1,0:T(8,128)}, u32[]{:S(2)}) copy-start(f32[512,512]{1,0:T(8,128)} %param.56) | copy-start | bytes 3145732
  70.3 1.6 %copy-start.14 = (f32[512]{0:T(512)S(1)}, f32[512]{0:T(512)}, u32[]{:S(2)}) copy-start(f32[512]{0:T(512)} %param.57) | copy-start | bytes 6148
  71.9 2.3 %copy-start.19 = (f32[512,512]{1,0:T(8,128)S(1)}, f32[512,512]{1,0:T(8,128)}, u32[]{:S(2)}) copy-start(f32[512,512]{1,0:T(8,128)} %param.58) | copy-start | bytes 3145732
  71.9 2.3 %copy-start.23 = (f32[512]{0:T(512)S(1)}, f32[512]{0:T(512)}, u32[]{:S(2)}) copy-start(f32[512]{0:T(512)} %param.59) | copy-start | bytes 6148
where the time goes:
time: 82.4 us; the launch traced here: 81.7 us
  matrix products  39.9 us (48%)
  local copies, waits for them, and re-layouts  22.9 us (28%)
  starting transfers between devices  10.2 us (12%)
  waiting for transfers between devices  6.13 us (7%)
  other arithmetic  2.23 us (3%)
    dot_general x14, matrix products, matmul(): jnp.dot(left, right, precision=PRECISE, preferred_element_type=jnp.float32)  37 us
    unnamed x52, local copies, waits for them, and re-layouts  8.24 us
    all_to_all x1, starting transfers between devices, per_device(): lax.all_to_all(grid_out.reshape(lat_count * lon_count, grid_capacity, wid...  7.33 us
    add x2, local copies, waits for them, and re-layouts, node_block(): return latent + norm_rows(matmul(hidden, weight_output) + bias_output)  4.24 us
    gather x2, local copies, waits for them, and re-layouts, finish_patch(): receiver_rows = matmul(nodes, weight_receiver)[jnp.maximum(targets, 0)]  3.5 us
    gather x1, local copies, waits for them, and re-layouts, per_device(): mesh_rows = encoded[mesh_index]  3.36 us
    all_to_all x1, waiting for transfers between devices, per_device(): lax.all_to_all(mesh_out.reshape(lat_count * lon_count, mesh_capacity, wid...  3.13 us
    all_to_all x1, waiting for transfers between devices, per_device(): lax.all_to_all(grid_out.reshape(lat_count * lon_count, grid_capacity, wid...  3 us
  transfers between devices with their start and end apart: 2, of which 2 were waited for; matrix products, arithmetic and copies ran while one was open for 32% of the time, Pallas kernels for 0%

commit v1 on v0

v1 whole, which is shorter than its diff:
```python
import functools

import jax
import jax.numpy as jnp
from jax import lax
from jax.experimental import pallas as pl
from jax.experimental.pallas import tpu as pltpu
from jax.sharding import PartitionSpec as P

F32 = jnp.float32
BF16 = jnp.bfloat16
VMEM = pl.BlockSpec(memory_space=pltpu.VMEM)
SMEM = pl.BlockSpec(memory_space=pltpu.SMEM)


def split(values):
    high = values.astype(BF16)
    low = (values - high.astype(F32)).astype(BF16)
    return high, low


def dot(left, right):
    return jnp.dot(left, right, preferred_element_type=F32)


def dot3(left, high, low):
    left_high, left_low = split(left)
    return dot(left_high, high) + (dot(left_low, high) + dot(left_high, low))


def pick(one_hot, values):
    high, low = split(values)
    return dot(one_hot, high) + dot(one_hot, low)


def silu(values):
    return values * (1.0 / (1.0 + jnp.exp(-values)))


def norm_rows(values):
    average = jnp.mean(values, axis=-1, keepdims=True)
    centred = values - average
    spread = jnp.mean(centred * centred, axis=-1, keepdims=True)
    return centred * lax.rsqrt(spread + 1e-05)


def gather_rows(count, row_of, pairs, unroll=8):
    def step(i, carry):
        row = row_of(i)
        for source, target in pairs:
            target[pl.ds(i, 1), :] = source[pl.ds(row, 1), :]
        return carry

    lax.fori_loop(0, count, step, 0, unroll=unroll)


def geometry_rows(geometry_ref, weight_ref):
    features, _, slots = geometry_ref.shape
    rows = jnp.concatenate([geometry_ref[k] for k in range(features)], axis=0)
    padded = jnp.concatenate([rows, jnp.zeros((8 - features % 8, slots), F32)], axis=0)
    columns = padded.T
    total = columns[:, 0:1] * weight_ref[0:1, :]
    for k in range(1, features):
        total += columns[:, k : k + 1] * weight_ref[k : k + 1, :]
    return total


def target_matrix(number, targets_ref):
    slots = targets_ref.shape[1]
    nodes = lax.broadcasted_iota(jnp.int32, (number, slots), 0)
    return jnp.where(nodes == targets_ref[...], 1.0, 0.0).astype(F32)


def slot_order(index_ref):
    capacity = index_ref.shape[0]
    bits = capacity.bit_length() - 1
    assert capacity == 1 << bits
    return lambda i: index_ref[i & (capacity - 1), i >> bits]


def pack_kernel(rows_in, columns_in, index_ref, grid_ref, out_ref):
    shift = 20
    factor = -(-(1 << shift) // columns_in)
    assert all((i * factor) >> shift == i // columns_in for i in range(rows_in * columns_in))
    order = slot_order(index_ref)

    def row_of(i):
        cell = order(i)
        row = (cell * factor) >> shift
        return (cell - row * columns_in) * rows_in + row

    gather_rows(out_ref.shape[0], row_of, [(grid_ref, out_ref)])


def before_kernel(
    grid_targets_s,
    mesh_senders_s,
    grid_targets,
    geometry,
    nodes,
    weight_receiver,
    weight_geometry,
    edge_bias,
    weight_self,
    node_bias,
    *refs,
):
    count = (len(refs) - 8) // 3
    weights = refs[:count]
    received, self_all, self_sent, nodes_sent, match = refs[count : count + 5]
    splits = refs[count + 5 : 3 * count + 5]
    near, table, chosen = refs[3 * count + 5 :]
    for k, weight in enumerate(weights):
        splits[2 * k][...], splits[2 * k + 1][...] = split(weight[...])
    self_all[...] = dot3(nodes[...], *split(weight_self[...])) + node_bias[...]
    gather_rows(
        received.shape[0], lambda i: jnp.maximum(grid_targets_s[0, i], 0), [(nodes, near)]
    )
    received[...] = (
        dot3(near[...], *split(weight_receiver[...]))
        + geometry_rows(geometry, weight_geometry)
        + edge_bias[...]
    )
    table[...] = target_matrix(nodes.shape[0], grid_targets)
    gather_rows(
        nodes_sent.shape[0],
        slot_order(mesh_senders_s),
        [(nodes, nodes_sent), (self_all, self_sent), (table, chosen)],
    )
    match[...] = chosen[...].astype(BF16)


def edges(arrived, received, sender, output, bias, summed):
    hidden = silu(dot3(arrived[...], *sender) + received[...])
    messages = norm_rows(dot3(hidden, *output) + bias[...])
    return dot3(messages, *summed)


def encode_kernel(
    arrived,
    received,
    self_sent,
    nodes_sent,
    match,
    sender_high,
    sender_low,
    output_high,
    output_low,
    output_bias,
    summed_high,
    summed_low,
    update_high,
    update_low,
    update_bias,
    sent,
    parts,
):
    part = edges(
        arrived,
        received,
        (sender_high[...], sender_low[...]),
        (output_high[...], output_low[...]),
        output_bias,
        (summed_high[...], summed_low[...]),
    )
    parts[...] = part
    hidden = silu(self_sent[...] + pick(match[...], part))
    sent[...] = nodes_sent[...] + norm_rows(
        dot3(hidden, update_high[...], update_low[...]) + update_bias[...]
    )


def between_kernel(
    mesh_targets_s,
    grid_targets,
    mesh_targets,
    geometry,
    nodes,
    self_all,
    parts,
    update_high,
    update_low,
    update_bias,
    weight_receiver,
    weight_geometry,
    edge_bias,
    weight_self,
    node_bias,
    refine_high,
    refine_low,
    refine_bias,
    received,
    self_near,
    near,
    match,
    base,
    encoded,
    self_next,
    table,
    chosen,
):
    one_hot = target_matrix(nodes.shape[0], grid_targets).astype(BF16)
    hidden = silu(self_all[...] + pick(one_hot, parts[...]))
    encoded[...] = nodes[...] + norm_rows(
        dot3(hidden, update_high[...], update_low[...]) + update_bias[...]
    )
    self_next[...] = dot3(encoded[...], *split(weight_self[...])) + node_bias[...]
    table[...] = target_matrix(nodes.shape[0], mesh_targets)
    gather_rows(
        near.shape[0],
        lambda i: jnp.maximum(mesh_targets_s[0, i], 0),
        [(encoded, near), (self_next, self_near), (table, chosen)],
    )
    match[...] = chosen[...].astype(BF16)
    received[...] = (
        dot3(near[...], *split(weight_receiver[...]))
        + geometry_rows(geometry, weight_geometry)
        + edge_bias[...]
    )
    base[...] = encoded[...] + norm_rows(
        dot3(silu(self_next[...]), refine_high[...], refine_low[...]) + refine_bias[...]
    )


def refine_kernel(
    mesh_targets_s,
    arrived,
    received,
    self_near,
    near,
    match,
    base,
    sender_high,
    sender_low,
    output_high,
    output_low,
    output_bias,
    summed_high,
    summed_low,
    refine_high,
    refine_low,
    refine_bias,
    out,
    rows,
):
    part = edges(
        arrived,
        received,
        (sender_high[...], sender_low[...]),
        (output_high[...], output_low[...]),
        output_bias,
        (summed_high[...], summed_low[...]),
    )
    hidden = silu(self_near[...] + pick(match[...], part))
    rows[...] = near[...] + norm_rows(
        dot3(hidden, refine_high[...], refine_low[...]) + refine_bias[...]
    )
    out[...] = base[...]

    def place(i, carry):
        target = mesh_targets_s[0, i]

        @pl.when(target >= 0)
        def _():
            out[pl.ds(target, 1), :] = rows[pl.ds(i, 1), :]

        return carry

    lax.fori_loop(0, rows.shape[0], place, 0, unroll=8)


def shape(dims, kind=F32):
    return jax.ShapeDtypeStruct(dims, kind)


def call(kernel, out_shape, scalars, arrays, scratch=(), flops=0, name=None):
    return pl.pallas_call(
        kernel,
        out_shape=out_shape,
        in_specs=[SMEM] * len(scalars) + [VMEM] * len(arrays),
        out_specs=jax.tree.map(lambda _: VMEM, out_shape),
        scratch_shapes=list(scratch),
        cost_estimate=pl.CostEstimate(flops=flops, bytes_accessed=4 * 2**20, transcendentals=0),
        compiler_params=pltpu.CompilerParams(vmem_limit_bytes=56 * 2**20),
        name=name,
    )(*scalars, *arrays)


def exchange(rows, patches):
    blocks = rows.reshape(patches, -1, rows.shape[1])
    blocks = lax.all_to_all(blocks, ("lat", "lon"), split_axis=0, concat_axis=0, tiled=True)
    return blocks.reshape(rows.shape)


def per_device(
    grid_latent,
    mesh_latent,
    grid_senders,
    grid_targets,
    grid_geometry,
    mesh_senders,
    mesh_targets,
    mesh_geometry,
    encoder_sender,
    encoder_receiver,
    encoder_geometry,
    encoder_bias,
    encoder_output,
    encoder_outbias,
    update_self,
    update_summed,
    update_bias,
    update_output,
    update_outbias,
    process_sender,
    process_receiver,
    process_geometry,
    process_bias,
    process_output,
    process_outbias,
    refine_self,
    refine_summed,
    refine_bias,
    refine_output,
    refine_outbias,
):
    number, width = mesh_latent.shape
    patches = grid_senders.shape[1]
    grid_slots = grid_targets.shape[1]
    mesh_slots = mesh_targets.shape[1]
    rows_in, columns_in = grid_latent.shape[:2]
    square = 2 * width * width
    row = lambda bias: bias.reshape(1, width)

    cells = grid_latent.transpose(1, 0, 2).reshape(rows_in * columns_in, width)
    packed = call(
        functools.partial(pack_kernel, rows_in, columns_in),
        shape((grid_slots, width)),
        [grid_senders[0].T],
        [cells],
        flops=1000,
        name="pack",
    )
    grid_in = exchange(packed, patches)

    weights = [
        encoder_sender,
        encoder_output,
        update_summed,
        update_output,
        process_sender,
        process_output,
        refine_summed,
        refine_output,
    ]
    senders = mesh_senders[0].T
    received, self_all, self_sent, nodes_sent, match, *splits = call(
        before_kernel,
        [
            shape((grid_slots, width)),
            shape((number, width)),
            shape((mesh_slots, width)),
            shape((mesh_slots, width)),
            shape((mesh_slots, grid_slots), BF16),
        ]
        + [shape((width, width), BF16)] * (2 * len(weights)),
        [grid_targets, senders],
        [
            grid_targets,
            grid_geometry,
            mesh_latent,
            encoder_receiver,
            encoder_geometry,
            row(encoder_bias),
            update_self,
            row(update_bias),
        ]
        + weights,
        [
            pltpu.VMEM((grid_slots, width), F32),
            pltpu.VMEM((number, grid_slots), F32),
            pltpu.VMEM((mesh_slots, grid_slots), F32),
        ],
        flops=(number + grid_slots) * square * 3,
        name="before",
    )
    sent, parts = call(
        encode_kernel,
        [shape((mesh_slots, width)), shape((grid_slots, width))],
        [],
        [grid_in, received, self_sent, nodes_sent, match]
        + splits[0:4]
        + [row(encoder_outbias)]
        + splits[4:8]
        + [row(update_outbias)],
        flops=(3 * grid_slots + mesh_slots) * square * 3,
        name="encode",
    )
    mesh_in = exchange(sent, patches)
    received, self_near, near, match, base = call(
        between_kernel,
        [
            shape((mesh_slots, width)),
            shape((mesh_slots, width)),
            shape((mesh_slots, width)),
            shape((mesh_slots, mesh_slots), BF16),
            shape((number, width)),
        ],
        [mesh_targets],
        [
            grid_targets,
            mesh_targets,
            mesh_geometry,
            mesh_latent,
            self_all,
            parts,
            splits[6],
            splits[7],
            row(update_outbias),
            process_receiver,
            process_geometry,
            row(process_bias),
            refine_self,
            row(refine_bias),
            splits[14],
            splits[15],
            row(refine_outbias),
        ],
        [
            pltpu.VMEM((number, width), F32),
            pltpu.VMEM((number, width), F32),
            pltpu.VMEM((number, mesh_slots), F32),
            pltpu.VMEM((mesh_slots, mesh_slots), F32),
        ],
        flops=(3 * number + mesh_slots) * square * 3,
        name="between",
    )
    return call(
        refine_kernel,
        shape((number, width)),
        [mesh_targets],
        [mesh_in, received, self_near, near, match, base]
        + splits[8:12]
        + [row(process_outbias)]
        + splits[12:16]
        + [row(refine_outbias)],
        [pltpu.VMEM((mesh_slots, width), F32)],
        flops=4 * mesh_slots * square * 3,
        name="refine",
    )


def solution(mesh):
    patch = P(("lat", "lon"), None)
    block = P(("lat", "lon"), None, None)
    feature = P(None, ("lat", "lon"), None)
    return jax.shard_map(
        per_device,
        mesh=mesh,
        in_specs=(P("lat", "lon", None), patch, block, patch, feature, block, patch, feature)
        + (P(),) * 22,
        out_specs=patch,
        check_vma=False,
    )
```

time: 82.4 us -> 67.5 us (0.82)
  Pallas kernels: 0 us -> 47.2 us
  matrix products: 39.9 us -> 0 us
  local copies, waits for them, and re-layouts: 22.9 us -> 1.6 us
  starting transfers between devices: 10.2 us -> 13 us
  other arithmetic: 2.23 us -> 0 us
  waiting for transfers between devices: 6.13 us -> 5.23 us
    pallas_call x0 -> x5, Pallas kernels: none -> 47.2 us  [call(): pl.pallas_call(kernel, out_shape=out_shape, in_specs=[SMEM] * len(scalars...]
    dot_general x16 -> x0, matrix products: 39.9 us -> none  [the longest x14 37 us: matmul(): jnp.dot(left, right, precision=PRECISE, preferred_element_type=jnp.float32)]
    gather x4 -> x0, local copies, waits for them, and re-layouts: 8.62 us -> none  [the longest x2 3.5 us: finish_patch(): receiver_rows = matmul(nodes, weight_receiver)[jnp.maximum(targets, 0)]]
    unnamed x52 -> x4, local copies, waits for them, and re-layouts: 8.24 us -> 1.6 us
    add x2 -> x0, local copies, waits for them, and re-layouts: 4.24 us -> none  [node_block(): return latent + norm_rows(matmul(hidden, weight_output) + bias_output)]
    all_to_all x2, starting transfers between devices: 10.2 us -> 13 us  [exchange(): lax.all_to_all(blocks, ('lat', 'lon'), split_axis=0, concat_axis=0, tiled...]
    reshape x3 -> x0, local copies, waits for them, and re-layouts: 1.78 us -> none  [the longest x1 1.61 us: per_device(): local_grid = grid_latent.reshape(-1, width)]
    add x2 -> x0, other arithmetic: 1.4 us -> none  [node_block(): return latent + norm_rows(matmul(hidden, weight_output) + bias_output)]
  transfers between devices with their start and end apart: 2 -> 2, of which waited for: 2 -> 2; matrix products, arithmetic and copies ran while one was open for 32% -> 0% of each run, Pallas kernels for 0% -> 40%
where the time goes in v1:
time: 67.5 us; the launch traced here: 67.1 us
  Pallas kernels  47.2 us (70%)
  starting transfers between devices  13 us (19%)
  waiting for transfers between devices  5.23 us (8%)
  local copies, waits for them, and re-layouts  1.6 us (2%)
    pallas_call x5, Pallas kernels, call(): pl.pallas_call(kernel, out_shape=out_shape, in_specs=[SMEM] * len(scalars...  47.2 us
    all_to_all x2, starting transfers between devices, exchange(): lax.all_to_all(blocks, ('lat', 'lon'), split_axis=0, concat_axis=0, tiled...  13 us
    all_to_all x2, waiting for transfers between devices, exchange(): lax.all_to_all(blocks, ('lat', 'lon'), split_axis=0, concat_axis=0, tiled...  5.23 us
    unnamed x4, local copies, waits for them, and re-layouts  1.6 us
  transfers between devices with their start and end apart: 2, of which 2 were waited for; matrix products, arithmetic and copies ran while one was open for 0% of the time, Pallas kernels for 40%

profile of v1, /device:TPU:0, one launch (start us, length us, event | category | flops | bytes accessed | tf_op | source)
XLA Modules:
  0.0 67.1 jit_solution(14761222192061495237)
XLA Ops:
  0.0 3.9 %pack.1 = f32[256,512]{1,0:T(8,128)} custom-call(s32[8,32]{1,0:T(8,128)} %bitcast.26, f32[720,512]{1,0:T(8,128)} %bitcast.24), custom_call_target="tpu_custom_call" | custom-call | flops 1000 | bytes 4194304 | tf_op jit(solution)/shard_map/pack/pallas_call | solution.py:277
  3.9 7.3 %all-to-all-start = ((f32[32,8,512]{2,1,0:T(8,128)}), f32[32,8,512]{2,1,0:T(8,128)S(1)}, u32[]{:S(2)}, u32[]{:S(2)}) async-start(f32[32,8,512]{2,1,0:T(8,128)} %bitcast.22), calls=%async_computation | async-start | bytes 1048576 | tf_op jit(solution)/shard_map/all_to_all | solution.py:291
  11.2 15.9 %before.1 = (f32[256,512]{1,0:T(8,128)}, f32[640,512]{1,0:T(8,128)}, f32[256,512]{1,0:T(8,128)}, f32[256,512]{1,0:T(8,128)}, bf16[256,256]{1,0:T(8,128)(2,1)}, /...) custom-call(s32[1,256]{1,0:T(1,128)} %grid_targets.3, ...), custom_call_target="tpu_custom_call" | custom-call | flops 1409286144 | bytes 4194304 | tf_op jit(solution)/shard_map/before/pallas_call | solution.py:277
  27.2 0.3 all-to-all-done
  27.5 0.0 copy-start.1
  27.5 0.8 %copy-done.1 = f32[32,8,512]{2,1,0:T(8,128)} copy-done((f32[32,8,512]{2,1,0:T(8,128)}, f32[32,8,512]{2,1,0:T(8,128)S(1)}, u32[]{:S(2)}) %copy-start.1) | copy-done | bytes 524312
  28.3 6.5 %encode.1 = (f32[256,512]{1,0:T(8,128)}, f32[256,512]{1,0:T(8,128)}) custom-call(f32[256,512]{1,0:T(8,128)} %bitcast.23, f32[256,512]{1,0:T(8,128)} %get-tuple-element.33.received, f32[256,512]{1,0:T(8,128)} %get-tuple-element.34.self_sent, f32[256,512]{1,0:T(8,128)} %get-tuple-element.35.nodes_sent, bf16[256,256]{1,0:T(8,128)(2,1)} %get-tuple-element.36.match, ...), custom_call_target="tpu_custom_call" | custom-call | flops 1610612736 | bytes 4194304 | tf_op jit(solution)/shard_map/encode/pallas_call | solution.py:277
  34.8 5.7 %all-to-all-start.1 = ((f32[32,8,512]{2,1,0:T(8,128)}), f32[32,8,512]{2,1,0:T(8,128)S(1)}, u32[]{:S(2)}, u32[]{:S(2)}) async-start(f32[32,8,512]{2,1,0:T(8,128)} %bitcast.25), calls=%async_computation.1 | async-start | bytes 1048576 | tf_op jit(solution)/shard_map/all_to_all | solution.py:291
  40.5 11.1 %between.1 = (f32[256,512]{1,0:T(8,128)}, f32[256,512]{1,0:T(8,128)}, f32[256,512]{1,0:T(8,128)}, bf16[256,256]{1,0:T(8,128)(2,1)}, f32[640,512]{1,0:T(8,128)}) custom-call(s32[1,256]{1,0:T(1,128)} %mesh_targets_s.3, s32[1,256]{1,0:T(1,128)} %grid_targets.3, s32[1,256]{1,0:T(1,128)} %mesh_targets_s.3, f32[4,1,256]{2,1,0:T(1,128)} %geometry.3, ...), custom_call_target="tpu_custom_call" | custom-call | flops 3422552064 | bytes 4194304 | tf_op jit(solution)/shard_map/between/pallas_call | solution.py:277
  51.7 4.9 %all-to-all-done.1 = f32[32,8,512]{2,1,0:T(8,128)S(1)} async-done(((f32[32,8,512]{2,1,0:T(8,128)}), f32[32,8,512]{2,1,0:T(8,128)S(1)}, u32[]{:S(2)}, u32[]{:S(2)}) %all-to-all-start.1) | async-done | bytes 524320 | tf_op jit(solution)/shard_map/all_to_all | solution.py:291
  56.6 0.0 copy-start
  56.6 0.8 %copy-done = f32[32,8,512]{2,1,0:T(8,128)} copy-done((f32[32,8,512]{2,1,0:T(8,128)}, f32[32,8,512]{2,1,0:T(8,128)S(1)}, u32[]{:S(2)}) %copy-start) | copy-done | bytes 524312
  57.4 9.7 %refine.1 = f32[640,512]{1,0:T(8,128)} custom-call(s32[1,256]{1,0:T(1,128)} %mesh_targets_s.3, f32[256,512]{1,0:T(8,128)} %bitcast.21, f32[256,512]{1,0:T(8,128)} %get-tuple-element.50.received, f32[256,512]{1,0:T(8,128)} %get-tuple-element.51.self_near, f32[256,512]{1,0:T(8,128)} %get-tuple-element.52.near, bf16[256,256]{1,0:T(8,128)(2,1)} %get-tuple-element.53.match, ...), custom_call_target="tpu_custom_call" | custom-call | flops 1610612736 | bytes 4194304 | tf_op jit(solution)/shard_map/refine/pallas_call | solution.py:277
Async XLA Ops:
  3.9 23.6 %all-to-all-start = ((f32[32,8,512]{2,1,0:T(8,128)}), f32[32,8,512]{2,1,0:T(8,128)S(1)}, u32[]{:S(2)}, u32[]{:S(2)}) async-start(f32[32,8,512]{2,1,0:T(8,128)} %bitcast.22), calls=%async_computation | async-start | bytes 1048576 | tf_op jit(solution)/shard_map/all_to_all | solution.py:291
  27.5 0.8 %copy-start.1 = (f32[32,8,512]{2,1,0:T(8,128)}, f32[32,8,512]{2,1,0:T(8,128)S(1)}, u32[]{:S(2)}) copy-start(f32[32,8,512]{2,1,0:T(8,128)S(1)} %all-to-all-done) | copy-start | bytes 1572868
  34.8 21.8 %all-to-all-start.1 = ((f32[32,8,512]{2,1,0:T(8,128)}), f32[32,8,512]{2,1,0:T(8,128)S(1)}, u32[]{:S(2)}, u32[]{:S(2)}) async-start(f32[32,8,512]{2,1,0:T(8,128)} %bitcast.25), calls=%async_computation.1 | async-start | bytes 1048576 | tf_op jit(solution)/shard_map/all_to_all | solution.py:291
  56.6 0.8 %copy-start = (f32[32,8,512]{2,1,0:T(8,128)}, f32[32,8,512]{2,1,0:T(8,128)S(1)}, u32[]{:S(2)}) copy-start(f32[32,8,512]{2,1,0:T(8,128)S(1)} %all-to-all-done.1) | copy-start | bytes 1572868

commit v2 on v1

v2 whole, which is shorter than its diff:
```python
import functools

import jax
import jax.numpy as jnp
from jax import lax
from jax.experimental import pallas as pl
from jax.experimental.pallas import tpu as pltpu
from jax.sharding import PartitionSpec as P

F32 = jnp.float32
BF16 = jnp.bfloat16
VMEM = pl.BlockSpec(memory_space=pltpu.VMEM)
SMEM = pl.BlockSpec(memory_space=pltpu.SMEM)
HBM = pl.BlockSpec(memory_space=pltpu.HBM)


def split(values):
    high = values.astype(BF16)
    low = (values - high.astype(F32)).astype(BF16)
    return high, low


def dot(left, right):
    return jnp.dot(left, right, preferred_element_type=F32)


def dot3(left, high, low):
    left_high, left_low = split(left)
    return dot(left_high, high) + (dot(left_low, high) + dot(left_high, low))


def pick(one_hot, values):
    high, low = split(values)
    return dot(one_hot, high) + dot(one_hot, low)


def silu(values):
    return values * (1.0 / (1.0 + jnp.exp(-values)))


def norm_rows(values):
    average = jnp.mean(values, axis=-1, keepdims=True)
    centred = values - average
    spread = jnp.mean(centred * centred, axis=-1, keepdims=True)
    return centred * lax.rsqrt(spread + 1e-05)


def gather_rows(first, count, row_of, pairs, unroll=16):
    def step(i, carry):
        row = row_of(i)
        for source, target in pairs:
            target[pl.ds(i, 1), :] = source[pl.ds(row, 1), :]
        return carry

    lax.fori_loop(first, first + count, step, 0, unroll=unroll)


def geometry_rows(geometry_ref, weight_ref):
    features, _, slots = geometry_ref.shape
    rows = jnp.concatenate([geometry_ref[k] for k in range(features)], axis=0)
    padded = jnp.concatenate([rows, jnp.zeros((8 - features % 8, slots), F32)], axis=0)
    columns = padded.T
    total = columns[:, 0:1] * weight_ref[0:1, :]
    for k in range(1, features):
        total += columns[:, k : k + 1] * weight_ref[k : k + 1, :]
    return total


def target_matrix(number, targets_ref):
    slots = targets_ref.shape[1]
    nodes = lax.broadcasted_iota(jnp.int32, (number, slots), 0)
    return jnp.where(nodes == targets_ref[...], 1.0, 0.0).astype(F32)


def slot_order(index_ref):
    capacity = index_ref.shape[0]
    bits = capacity.bit_length() - 1
    assert capacity == 1 << bits
    return lambda i: index_ref[i & (capacity - 1), i >> bits]


class Copies:
    def __init__(self, semaphores):
        self.semaphores = semaphores
        self.used = 0

    def start(self, source, target):
        copy = pltpu.make_async_copy(source, target, self.semaphores.at[self.used])
        self.used += 1
        copy.start()
        return copy


def wait(*copies):
    for copy in copies:
        copy.wait()


def pack_kernel(
    rows_in, columns_in, senders_ref, cells_ref, out_ref, cells, out, senders, semaphores
):
    copies = Copies(semaphores)
    load_senders = copies.start(senders_ref, senders)
    load = copies.start(cells_ref, cells)
    shift = 20
    factor = -(-(1 << shift) // columns_in)
    assert all((i * factor) >> shift == i // columns_in for i in range(rows_in * columns_in))
    order = slot_order(senders)

    def row_of(i):
        cell = order(i)
        row = (cell * factor) >> shift
        return (cell - row * columns_in) * rows_in + row

    wait(load_senders, load)
    chunk = out.shape[0] // 4
    stores = []
    for first in range(0, out.shape[0], chunk):
        gather_rows(first, chunk, row_of, [(cells, out)])
        stores.append(
            copies.start(out.at[pl.ds(first, chunk)], out_ref.at[pl.ds(first, chunk)])
        )
    wait(*stores)


def before_kernel(
    grid_targets_s,
    mesh_senders_s,
    grid_targets,
    geometry,
    weight_geometry,
    edge_bias,
    node_bias,
    bias_one,
    bias_two,
    nodes_ref,
    weight_self_ref,
    weight_receiver_ref,
    *refs,
):
    count = 8
    weight_refs, refs = refs[:count], refs[count:]
    inner, refs = refs[:5], refs[5:]
    received_ref, self_all_ref, self_sent_ref, nodes_sent_ref, match_ref = refs[:5]
    split_refs, refs = refs[5 : 2 * count + 1], refs[2 * count + 1 :]
    nodes, weight_self, weight_receiver, weights, refs = *refs[:3], refs[3 : 3 + count], refs[3 + count :]
    received, self_all, self_sent, nodes_sent, match = refs[:5]
    splits, refs = refs[5 : 2 * count + 1], refs[2 * count + 1 :]
    near, table, chosen, semaphores = refs
    copies = Copies(semaphores)
    load_nodes = copies.start(nodes_ref, nodes)
    load_self = copies.start(weight_self_ref, weight_self)
    load_receiver = copies.start(weight_receiver_ref, weight_receiver)
    loads = [copies.start(ref, weight) for ref, weight in zip(weight_refs, weights, strict=True)]
    inner[4][0:1, :] = bias_one[...]
    inner[4][1:2, :] = bias_two[...]
    table[...] = target_matrix(nodes.shape[0], grid_targets)
    stores = []
    wait(load_nodes, load_self)
    self_all[...] = dot3(nodes[...], *split(weight_self[...])) + node_bias[...]
    stores.append(copies.start(self_all, self_all_ref))
    gather_rows(
        0,
        mesh_senders_s.shape[0] * mesh_senders_s.shape[1],
        slot_order(mesh_senders_s),
        [(nodes, nodes_sent), (self_all, self_sent), (table, chosen)],
    )
    match[...] = chosen[...].astype(BF16)
    stores.append(copies.start(self_sent, self_sent_ref))
    stores.append(copies.start(nodes_sent, nodes_sent_ref))
    stores.append(copies.start(match, match_ref))
    gather_rows(
        0, near.shape[0], lambda i: jnp.maximum(grid_targets_s[0, i], 0), [(nodes, near)]
    )
    wait(load_receiver)
    received[...] = (
        dot3(near[...], *split(weight_receiver[...]))
        + geometry_rows(geometry, weight_geometry)
        + edge_bias[...]
    )
    stores.append(copies.start(received, received_ref))
    for k in range(count):
        wait(loads[k])
        if k < 2:
            inner[2 * k][...], inner[2 * k + 1][...] = split(weights[k][...])
        else:
            at = 2 * (k - 2)
            splits[at][...], splits[at + 1][...] = split(weights[k][...])
            stores.append(copies.start(splits[at], split_refs[at]))
            stores.append(copies.start(splits[at + 1], split_refs[at + 1]))
    wait(*stores)


def encode_kernel(
    arrived,
    sender_high,
    sender_low,
    output_high,
    output_low,
    biases,
    received_ref,
    summed_high_ref,
    summed_low_ref,
    self_sent_ref,
    match_ref,
    update_high_ref,
    update_low_ref,
    nodes_sent_ref,
    sent_ref,
    parts_ref,
    received,
    summed_high,
    summed_low,
    self_sent,
    match,
    update_high,
    update_low,
    nodes_sent,
    sent,
    parts,
    semaphores,
):
    copies = Copies(semaphores)
    load_received = copies.start(received_ref, received)
    load_summed_high = copies.start(summed_high_ref, summed_high)
    load_summed_low = copies.start(summed_low_ref, summed_low)
    load_match = copies.start(match_ref, match)
    load_self = copies.start(self_sent_ref, self_sent)
    load_update_high = copies.start(update_high_ref, update_high)
    load_update_low = copies.start(update_low_ref, update_low)
    load_nodes = copies.start(nodes_sent_ref, nodes_sent)
    hidden = dot3(arrived[...], sender_high[...], sender_low[...])
    wait(load_received)
    hidden = silu(hidden + received[...])
    messages = norm_rows(dot3(hidden, output_high[...], output_low[...]) + biases[0:1, :])
    wait(load_summed_high, load_summed_low)
    part = dot3(messages, summed_high[...], summed_low[...])
    parts[...] = part
    store_parts = copies.start(parts, parts_ref)
    wait(load_match, load_self)
    hidden = silu(self_sent[...] + pick(match[...], part))
    wait(load_update_high, load_update_low, load_nodes)
    sent[...] = nodes_sent[...] + norm_rows(
        dot3(hidden, update_high[...], update_low[...]) + biases[1:2, :]
    )
    store_sent = copies.start(sent, sent_ref)
    wait(store_parts, store_sent)


def between_kernel(
    mesh_targets_s,
    grid_targets,
    mesh_targets,
    geometry,
    weight_geometry,
    edge_bias,
    node_bias,
    update_bias,
    refine_bias,
    bias_one,
    sender_high_ref,
    sender_low_ref,
    output_high_ref,
    output_low_ref,
    parts_ref,
    self_all_ref,
    nodes_ref,
    update_high_ref,
    update_low_ref,
    weight_self_ref,
    weight_receiver_ref,
    refine_high_ref,
    refine_low_ref,
    sender_high,
    sender_low,
    output_high,
    output_low,
    biases,
    received_ref,
    self_near_ref,
    near_ref,
    match_ref,
    base_ref,
    parts,
    self_all,
    nodes,
    update_high,
    update_low,
    weight_self,
    weight_receiver,
    refine_high,
    refine_low,
    received,
    self_near,
    near,
    match,
    base,
    encoded,
    self_next,
    table,
    chosen,
    semaphores,
):
    copies = Copies(semaphores)
    load_parts = copies.start(parts_ref, parts)
    load_all = copies.start(self_all_ref, self_all)
    load_update_high = copies.start(update_high_ref, update_high)
    load_update_low = copies.start(update_low_ref, update_low)
    load_nodes = copies.start(nodes_ref, nodes)
    load_self = copies.start(weight_self_ref, weight_self)
    load_receiver = copies.start(weight_receiver_ref, weight_receiver)
    load_refine_high = copies.start(refine_high_ref, refine_high)
    load_refine_low = copies.start(refine_low_ref, refine_low)
    passed = [
        copies.start(sender_high_ref, sender_high),
        copies.start(sender_low_ref, sender_low),
        copies.start(output_high_ref, output_high),
        copies.start(output_low_ref, output_low),
    ]
    stores = []
    biases[0:1, :] = bias_one[...]
    biases[1:2, :] = refine_bias[...]
    one_hot = target_matrix(nodes.shape[0], grid_targets).astype(BF16)
    table[...] = target_matrix(nodes.shape[0], mesh_targets)
    wait(load_parts, load_all)
    hidden = silu(self_all[...] + pick(one_hot, parts[...]))
    wait(load_update_high, load_update_low, load_nodes)
    encoded[...] = nodes[...] + norm_rows(
        dot3(hidden, update_high[...], update_low[...]) + update_bias[...]
    )
    wait(load_self)
    self_next[...] = dot3(encoded[...], *split(weight_self[...])) + node_bias[...]
    gather_rows(
        0,
        near.shape[0],
        lambda i: jnp.maximum(mesh_targets_s[0, i], 0),
        [(encoded, near), (self_next, self_near), (table, chosen)],
    )
    match[...] = chosen[...].astype(BF16)
    stores.append(copies.start(near, near_ref))
    stores.append(copies.start(self_near, self_near_ref))
    stores.append(copies.start(match, match_ref))
    wait(load_receiver)
    received[...] = (
        dot3(near[...], *split(weight_receiver[...]))
        + geometry_rows(geometry, weight_geometry)
        + edge_bias[...]
    )
    stores.append(copies.start(received, received_ref))
    wait(load_refine_high, load_refine_low)
    base[...] = encoded[...] + norm_rows(
        dot3(silu(self_next[...]), refine_high[...], refine_low[...]) + refine_bias[...]
    )
    stores.append(copies.start(base, base_ref))
    wait(*passed, *stores)


def refine_kernel(
    mesh_targets_s,
    arrived,
    sender_high,
    sender_low,
    output_high,
    output_low,
    biases,
    received_ref,
    summed_high_ref,
    summed_low_ref,
    match_ref,
    self_near_ref,
    refine_high_ref,
    refine_low_ref,
    near_ref,
    base_ref,
    out_ref,
    received,
    summed_high,
    summed_low,
    match,
    self_near,
    refine_high,
    refine_low,
    near,
    base,
    rows,
    semaphores,
):
    copies = Copies(semaphores)
    number = base_ref.shape[0]
    load_received = copies.start(received_ref, received)
    load_summed_high = copies.start(summed_high_ref, summed_high)
    load_summed_low = copies.start(summed_low_ref, summed_low)
    load_match = copies.start(match_ref, match)
    load_self = copies.start(self_near_ref, self_near)
    load_refine_high = copies.start(refine_high_ref, refine_high)
    load_refine_low = copies.start(refine_low_ref, refine_low)
    load_near = copies.start(near_ref, near)
    load_base = copies.start(base_ref, base.at[pl.ds(0, number)])
    hidden = dot3(arrived[...], sender_high[...], sender_low[...])
    wait(load_received)
    hidden = silu(hidden + received[...])
    messages = norm_rows(dot3(hidden, output_high[...], output_low[...]) + biases[0:1, :])
    wait(load_summed_high, load_summed_low)
    part = dot3(messages, summed_high[...], summed_low[...])
    wait(load_match, load_self)
    hidden = silu(self_near[...] + pick(match[...], part))
    wait(load_refine_high, load_refine_low, load_near)
    rows[...] = near[...] + norm_rows(
        dot3(hidden, refine_high[...], refine_low[...]) + biases[1:2, :]
    )
    wait(load_base)

    def place(i, carry):
        target = mesh_targets_s[0, i]
        target = jnp.where(target < 0, number, target)
        base[pl.ds(target, 1), :] = rows[pl.ds(i, 1), :]
        return carry

    lax.fori_loop(0, rows.shape[0], place, 0, unroll=16)
    wait(copies.start(base.at[pl.ds(0, number)], out_ref))


def flat(dims, kind=F32):
    return jax.ShapeDtypeStruct(dims, kind)


def call(
    kernel, name, flops, scalars, small, kept, large, results, held=(), scratch=(), direct=()
):
    direct = [pltpu.with_memory_space_constraint(array, pltpu.HBM) for array in direct]
    kept = [pltpu.with_memory_space_constraint(array, pltpu.VMEM) for array in kept]
    large = [pltpu.with_memory_space_constraint(array, pltpu.HBM) for array in large]
    twins = [pltpu.VMEM(array.shape, array.dtype) for array in [*large, *results]]
    twins += list(scratch)
    size = sum(4 * spec.inner_aval.size for spec in twins)
    return pl.pallas_call(
        kernel,
        out_shape=[pltpu.VMEM(array.shape, array.dtype) for array in held]
        + [pltpu.HBM(array.shape, array.dtype) for array in results],
        in_specs=[SMEM] * len(scalars)
        + [VMEM] * (len(small) + len(kept))
        + [HBM] * (len(direct) + len(large)),
        out_specs=[VMEM] * len(held) + [HBM] * len(results),
        scratch_shapes=[
            *twins,
            pltpu.SemaphoreType.DMA((len(direct) + len(large) + len(results) + 8,)),
        ],
        cost_estimate=pl.CostEstimate(flops=flops, bytes_accessed=4 * 2**20, transcendentals=0),
        compiler_params=pltpu.CompilerParams(vmem_limit_bytes=size + 12 * 2**20),
        name=name,
    )(*scalars, *small, *kept, *direct, *large)


def exchange(rows, patches):
    blocks = rows.reshape(patches, -1, rows.shape[1])
    blocks = lax.all_to_all(blocks, ("lat", "lon"), split_axis=0, concat_axis=0, tiled=True)
    return blocks.reshape(rows.shape)


def per_device(
    grid_latent,
    mesh_latent,
    grid_senders,
    grid_targets,
    grid_geometry,
    mesh_senders,
    mesh_targets,
    mesh_geometry,
    encoder_sender,
    encoder_receiver,
    encoder_geometry,
    encoder_bias,
    encoder_output,
    encoder_outbias,
    update_self,
    update_summed,
    update_bias,
    update_output,
    update_outbias,
    process_sender,
    process_receiver,
    process_geometry,
    process_bias,
    process_output,
    process_outbias,
    refine_self,
    refine_summed,
    refine_bias,
    refine_output,
    refine_outbias,
):
    number, width = mesh_latent.shape
    patches = grid_senders.shape[1]
    grid_slots = grid_targets.shape[1]
    mesh_slots = mesh_targets.shape[1]
    rows_in, columns_in = grid_latent.shape[:2]
    square = 2 * width * width
    row = lambda bias: bias.reshape(1, width)
    halves = [flat((width, width), BF16)] * 2

    cells = grid_latent.transpose(1, 0, 2).reshape(rows_in * columns_in, width)
    (packed,) = call(
        functools.partial(pack_kernel, rows_in, columns_in),
        "pack",
        1000,
        [],
        [],
        [],
        [cells],
        [flat((grid_slots, width))],
        scratch=[pltpu.SMEM((grid_slots // patches, patches), jnp.int32)],
        direct=[grid_senders[0].T],
    )
    grid_in = exchange(packed, patches)

    weights = [
        encoder_sender,
        encoder_output,
        update_summed,
        update_output,
        process_sender,
        process_output,
        refine_summed,
        refine_output,
    ]
    (
        *first,
        biases,
        received,
        self_all,
        self_sent,
        nodes_sent,
        match,
        summed_high,
        summed_low,
        update_high,
        update_low,
        sender_high,
        sender_low,
        output_high,
        output_low,
        second_high,
        second_low,
        refine_high,
        refine_low,
    ) = call(
        before_kernel,
        "before",
        (number + grid_slots) * square * 3,
        [grid_targets, mesh_senders[0].T],
        [
            grid_targets,
            grid_geometry,
            encoder_geometry,
            row(encoder_bias),
            row(update_bias),
            row(encoder_outbias),
            row(update_outbias),
        ],
        [],
        [mesh_latent, update_self, encoder_receiver] + weights,
        [
            flat((grid_slots, width)),
            flat((number, width)),
            flat((mesh_slots, width)),
            flat((mesh_slots, width)),
            flat((mesh_slots, grid_slots), BF16),
        ]
        + halves * 6,
        halves * 2 + [flat((8, width))],
        [
            pltpu.VMEM((grid_slots, width), F32),
            pltpu.VMEM((number, grid_slots), F32),
            pltpu.VMEM((mesh_slots, grid_slots), F32),
        ],
    )
    sent, parts = call(
        encode_kernel,
        "encode",
        (3 * grid_slots + mesh_slots) * square * 3,
        [],
        [],
        [grid_in, *first, biases],
        [received, summed_high, summed_low, self_sent, match, update_high, update_low, nodes_sent],
        [flat((mesh_slots, width)), flat((grid_slots, width))],
    )
    mesh_in = exchange(sent, patches)
    *first, biases, received, self_near, near, match, base = call(
        between_kernel,
        "between",
        (3 * number + mesh_slots) * square * 3,
        [mesh_targets],
        [
            grid_targets,
            mesh_targets,
            mesh_geometry,
            process_geometry,
            row(process_bias),
            row(refine_bias),
            row(update_outbias),
            row(refine_outbias),
            row(process_outbias),
        ],
        [],
        [
            parts,
            self_all,
            mesh_latent,
            update_high,
            update_low,
            refine_self,
            process_receiver,
            refine_high,
            refine_low,
        ],
        [
            flat((mesh_slots, width)),
            flat((mesh_slots, width)),
            flat((mesh_slots, width)),
            flat((mesh_slots, mesh_slots), BF16),
            flat((number, width)),
        ],
        halves * 2 + [flat((8, width))],
        [
            pltpu.VMEM((number, width), F32),
            pltpu.VMEM((number, width), F32),
            pltpu.VMEM((number, mesh_slots), F32),
            pltpu.VMEM((mesh_slots, mesh_slots), F32),
        ],
        [sender_high, sender_low, output_high, output_low],
    )
    return refine_call(
        mesh_targets, mesh_in, first, biases, received, second_high, second_low, match, self_near,
        refine_high, refine_low, near, base,
    )


def refine_call(targets, arrived, first, biases, *large):
    base = large[-1]
    number, width = base.shape
    slots = targets.shape[1]
    kept = [pltpu.with_memory_space_constraint(x, pltpu.VMEM) for x in [arrived, *first, biases]]
    large = [pltpu.with_memory_space_constraint(x, pltpu.HBM) for x in large]
    twins = [pltpu.VMEM(x.shape, x.dtype) for x in large[:-1]]
    twins += [pltpu.VMEM((number + 8, width), F32), pltpu.VMEM((slots, width), F32)]
    size = sum(4 * spec.inner_aval.size for spec in twins)
    return pl.pallas_call(
        refine_kernel,
        out_shape=flat((number, width)),
        in_specs=[SMEM] + [VMEM] * len(kept) + [HBM] * len(large),
        out_specs=HBM,
        scratch_shapes=[*twins, pltpu.SemaphoreType.DMA((len(large) + 1,))],
        compiler_params=pltpu.CompilerParams(vmem_limit_bytes=size + 12 * 2**20),
        name="refine",
    )(targets, *kept, *large)


def solution(mesh):
    patch = P(("lat", "lon"), None)
    block = P(("lat", "lon"), None, None)
    feature = P(None, ("lat", "lon"), None)
    return jax.shard_map(
        per_device,
        mesh=mesh,
        in_specs=(P("lat", "lon", None), patch, block, patch, feature, block, patch, feature)
        + (P(),) * 22,
        out_specs=patch,
        check_vma=False,
    )
```

time: 67.5 us -> 58.4 us (0.87)
  Pallas kernels: 47.2 us -> 36.3 us
  waiting for transfers between devices: 5.23 us -> 11.1 us
  starting transfers between devices: 13 us -> 10.1 us
  local copies, waits for them, and re-layouts: 1.6 us -> 0.06 us
    pallas_call x5, Pallas kernels: 47.2 us -> 36.3 us  [the longest x4 29.7 us: call(): pl.pallas_call(kernel, out_shape=[pltpu.VMEM(array.shape, array.dtype) fo...]
    all_to_all x2, waiting for transfers between devices: 5.23 us -> 11.1 us  [exchange(): lax.all_to_all(blocks, ('lat', 'lon'), split_axis=0, concat_axis=0, tiled...]
    all_to_all x2, starting transfers between devices: 13 us -> 10.1 us  [exchange(): lax.all_to_all(blocks, ('lat', 'lon'), split_axis=0, concat_axis=0, tiled...]
    unnamed x4 -> x30, local copies, waits for them, and re-layouts: 1.6 us -> 0.06 us
  transfers between devices with their start and end apart: 2 -> 2, of which waited for: 2 -> 2; matrix products, arithmetic and copies ran while one was open for 0% -> 0% of each run, Pallas kernels for 40% -> 36%
where the time goes in v2:
time: 58.4 us; the launch traced here: 58 us
  Pallas kernels  36.3 us (62%)
  waiting for transfers between devices  11.1 us (19%)
  starting transfers between devices  10.1 us (17%)
    pallas_call x4, Pallas kernels, call(): pl.pallas_call(kernel, out_shape=[pltpu.VMEM(array.shape, array.dtype) fo...  29.7 us
    all_to_all x2, waiting for transfers between devices, exchange(): lax.all_to_all(blocks, ('lat', 'lon'), split_axis=0, concat_axis=0, tiled...  11.1 us
    all_to_all x2, starting transfers between devices, exchange(): lax.all_to_all(blocks, ('lat', 'lon'), split_axis=0, concat_axis=0, tiled...  10.1 us
    pallas_call x1, Pallas kernels, refine_call(): pl.pallas_call(refine_kernel, out_shape=flat((number, width)), in_specs=[...  6.6 us
  transfers between devices with their start and end apart: 2, of which 2 were waited for; matrix products, arithmetic and copies ran while one was open for 0% of the time, Pallas kernels for 36%

profile of v2, /device:TPU:0, one launch (start us, length us, event | category | flops | bytes accessed | tf_op | source)
XLA Modules:
  0.0 58.0 jit_solution(15692518287039288931)
XLA Ops:
  0.0 0.0 copy-start
  0.0 0.0 copy-start.1
  0.0 0.0 copy-start.2
  0.0 0.0 copy-start.3
  0.0 0.0 copy-start.4
  0.0 0.0 copy-start.5
  0.0 0.0 copy-start.6
  0.0 0.0 copy-start.7
  0.0 3.8 %pack.1 = f32[256,512]{1,0:T(8,128)} custom-call(s32[8,32]{1,0:T(8,128)} %bitcast.36, f32[720,512]{1,0:T(8,128)} %bitcast.34), custom_call_target="tpu_custom_call" | custom-call | flops 1000 | bytes 4194304 | tf_op jit(solution)/shard_map/pack/pallas_call | solution.py:436
  3.8 7.3 %all-to-all-start = ((f32[32,8,512]{2,1,0:T(8,128)}), f32[32,8,512]{2,1,0:T(8,128)S(1)}, u32[]{:S(2)}, u32[]{:S(2)}) async-start(f32[32,8,512]{2,1,0:T(8,128)} %bitcast.33), calls=%async_computation | async-start | bytes 1048576 | tf_op jit(solution)/shard_map/all_to_all | solution.py:456
  11.2 0.0 copy-done
  11.2 0.0 copy-done.1
  11.2 0.0 copy-done.2
  11.2 0.0 copy-done.3
  11.2 0.0 copy-done.4
  11.2 0.0 copy-done.5
  11.2 0.0 copy-done.6
  11.2 0.0 copy-done.7
  11.3 10.4 %before.1 = (bf16[512,512]{1,0:T(8,128)(2,1)S(1)}, bf16[512,512]{1,0:T(8,128)(2,1)S(1)}, bf16[512,512]{1,0:T(8,128)(2,1)S(1)}, bf16[512,512]{1,0:T(8,128)(2,1)S(...) custom-call(s32[1,256]{1,0:T(1,128)S(1)} %copy-done.3, ...), custom_call_target="tpu_custom_call" | custom-call | flops 1409286144 | bytes 4194304 | tf_op jit(solution)/shard_map/before/pallas_call | solution.py:436
  21.7 5.7 %all-to-all-done = f32[32,8,512]{2,1,0:T(8,128)S(1)} async-done(((f32[32,8,512]{2,1,0:T(8,128)}), f32[32,8,512]{2,1,0:T(8,128)S(1)}, u32[]{:S(2)}, u32[]{:S(2)}) %all-to-all-start) | async-done | bytes 524320 | tf_op jit(solution)/shard_map/all_to_all | solution.py:456
  27.4 0.0 copy-start.8
  27.4 0.0 copy-start.9
  27.4 0.0 copy-start.10
  27.4 0.0 copy-start.11
  27.4 0.0 copy-start.12
  27.4 0.0 copy-start.13
  27.4 0.0 copy-start.14
  27.5 4.9 %encode.1 = (f32[256,512]{1,0:T(8,128)}, f32[256,512]{1,0:T(8,128)}) custom-call(f32[256,512]{1,0:T(8,128)S(1)} %bitcast.22, bf16[512,512]{1,0:T(8,128)(2,1)S(1)} %get-tuple-element.39.sender_high, bf16[512,512]{1,0:T(8,128)(2,1)S(1)} %get-tuple-element.40.sender_low, bf16[512,512]{1,0:T(8,128)(2,1)S(1)} %get-tuple-element.41.output_high, ...), custom_call_target="tpu_custom_call" | custom-call | flops 1610612736 | bytes 4194304 | tf_op jit(solution)/shard_map/encode/pallas_call | solution.py:436
  32.4 2.8 %all-to-all-start.1 = ((f32[32,8,512]{2,1,0:T(8,128)}), f32[32,8,512]{2,1,0:T(8,128)S(1)}, u32[]{:S(2)}, u32[]{:S(2)}) async-start(f32[32,8,512]{2,1,0:T(8,128)} %bitcast.35), calls=%async_computation.1 | async-start | bytes 1048576 | tf_op jit(solution)/shard_map/all_to_all | solution.py:456
  35.2 0.0 copy-done.8
  35.2 0.0 copy-done.9
  35.2 0.0 copy-done.10
  35.2 0.0 copy-done.11
  35.2 0.0 copy-done.12
  35.2 0.0 copy-done.13
  35.2 0.0 copy-done.14
  35.3 10.6 %between.1 = (bf16[512,512]{1,0:T(8,128)(2,1)S(1)}, bf16[512,512]{1,0:T(8,128)(2,1)S(1)}, bf16[512,512]{1,0:T(8,128)(2,1)S(1)}, bf16[512,512]{1,0:T(8,128)(2,1)S...) custom-call(s32[1,256]{1,0:T(1,128)S(1)} %copy-done.8, ...), custom_call_target="tpu_custom_call" | custom-call | flops 3422552064 | bytes 4194304 | tf_op jit(solution)/shard_map/between/pallas_call | solution.py:436
  45.9 5.4 %all-to-all-done.1 = f32[32,8,512]{2,1,0:T(8,128)S(1)} async-done(((f32[32,8,512]{2,1,0:T(8,128)}), f32[32,8,512]{2,1,0:T(8,128)S(1)}, u32[]{:S(2)}, u32[]{:S(2)}) %all-to-all-start.1) | async-done | bytes 524320 | tf_op jit(solution)/shard_map/all_to_all | solution.py:456
  51.2 6.6 %refine.1 = f32[640,512]{1,0:T(8,128)} custom-call(s32[1,256]{1,0:T(1,128)S(1)} %copy-done.8, f32[256,512]{1,0:T(8,128)S(1)} %bitcast.21, bf16[512,512]{1,0:T(8,128)(2,1)S(1)} %get-tuple-element.61.sender_high, bf16[512,512]{1,0:T(8,128)(2,1)S(1)} %get-tuple-element.62.sender_low, bf16[512,512]{1,0:T(8,128)(2,1)S(1)} %get-tuple-element.63.output_high, ...), custom_call_target="tpu_custom_call" | custom-call | tf_op jit(solution)/shard_map/refine/pallas_call | solution.py:647
Async XLA Ops:
  0.0 11.2 %copy-start = (f32[4,512]{1,0:T(4,128)S(1)}, f32[4,512]{1,0:T(4,128)}, u32[]{:S(2)}) copy-start(f32[4,512]{1,0:T(4,128)} %weight_geometry.2) | copy-start | bytes 24580
  0.0 11.2 %copy-start.1 = (s32[1,32,8]{1,2,0:T(8,128)S(1)}, s32[1,32,8]{1,2,0:T(8,128)}, u32[]{:S(2)}) copy-start(s32[1,32,8]{1,2,0:T(8,128)} %param.35) | copy-start | bytes 3076
  0.0 11.2 %copy-start.2 = (f32[4,1,256]{2,1,0:T(1,128)S(1)}, f32[4,1,256]{2,1,0:T(1,128)}, u32[]{:S(2)}) copy-start(f32[4,1,256]{2,1,0:T(1,128)} %geometry.2) | copy-start | bytes 12292
  0.0 11.2 %copy-start.3 = (s32[1,256]{1,0:T(1,128)S(1)}, s32[1,256]{1,0:T(1,128)}, u32[]{:S(2)}) copy-start(s32[1,256]{1,0:T(1,128)} %grid_targets.3) | copy-start | bytes 3076
  0.0 11.2 %copy-start.4 = (f32[512]{0:T(512)S(1)}, f32[512]{0:T(512)}, u32[]{:S(2)}) copy-start(f32[512]{0:T(512)} %param.41) | copy-start | bytes 6148
  0.0 11.2 %copy-start.5 = (f32[512]{0:T(512)S(1)}, f32[512]{0:T(512)}, u32[]{:S(2)}) copy-start(f32[512]{0:T(512)} %param.46) | copy-start | bytes 6148
  0.0 11.2 %copy-start.6 = (f32[512]{0:T(512)S(1)}, f32[512]{0:T(512)}, u32[]{:S(2)}) copy-start(f32[512]{0:T(512)} %param.43) | copy-start | bytes 6148
  0.0 11.2 %copy-start.7 = (f32[512]{0:T(512)S(1)}, f32[512]{0:T(512)}, u32[]{:S(2)}) copy-start(f32[512]{0:T(512)} %param.48) | copy-start | bytes 6148
  3.8 23.6 %all-to-all-start = ((f32[32,8,512]{2,1,0:T(8,128)}), f32[32,8,512]{2,1,0:T(8,128)S(1)}, u32[]{:S(2)}, u32[]{:S(2)}) async-start(f32[32,8,512]{2,1,0:T(8,128)} %bitcast.33), calls=%async_computation | async-start | bytes 1048576 | tf_op jit(solution)/shard_map/all_to_all | solution.py:456
  27.4 7.8 %copy-start.8 = (s32[1,256]{1,0:T(1,128)S(1)}, s32[1,256]{1,0:T(1,128)}, u32[]{:S(2)}) copy-start(s32[1,256]{1,0:T(1,128)} %mesh_targets_s.3) | copy-start | bytes 3076
  27.4 7.8 %copy-start.9 = (f32[4,512]{1,0:T(4,128)S(1)}, f32[4,512]{1,0:T(4,128)}, u32[]{:S(2)}) copy-start(f32[4,512]{1,0:T(4,128)} %weight_geometry.3) | copy-start | bytes 24580
  27.4 7.8 %copy-start.10 = (f32[4,1,256]{2,1,0:T(1,128)S(1)}, f32[4,1,256]{2,1,0:T(1,128)}, u32[]{:S(2)}) copy-start(f32[4,1,256]{2,1,0:T(1,128)} %geometry.3) | copy-start | bytes 12292
  27.4 7.8 %copy-start.11 = (f32[512]{0:T(512)S(1)}, f32[512]{0:T(512)}, u32[]{:S(2)}) copy-start(f32[512]{0:T(512)} %param.52) | copy-start | bytes 6148
  27.4 7.8 %copy-start.12 = (f32[512]{0:T(512)S(1)}, f32[512]{0:T(512)}, u32[]{:S(2)}) copy-start(f32[512]{0:T(512)} %param.57) | copy-start | bytes 6148
  27.4 7.8 %copy-start.13 = (f32[512]{0:T(512)S(1)}, f32[512]{0:T(512)}, u32[]{:S(2)}) copy-start(f32[512]{0:T(512)} %param.59) | copy-start | bytes 6148
  27.4 7.8 %copy-start.14 = (f32[512]{0:T(512)S(1)}, f32[512]{0:T(512)}, u32[]{:S(2)}) copy-start(f32[512]{0:T(512)} %param.54) | copy-start | bytes 6148
  32.4 18.9 %all-to-all-start.1 = ((f32[32,8,512]{2,1,0:T(8,128)}), f32[32,8,512]{2,1,0:T(8,128)S(1)}, u32[]{:S(2)}, u32[]{:S(2)}) async-start(f32[32,8,512]{2,1,0:T(8,128)} %bitcast.35), calls=%async_computation.1 | async-start | bytes 1048576 | tf_op jit(solution)/shard_map/all_to_all | solution.py:456

commit v3 on v2

--- a/solution.py
+++ b/solution.py
@@ -35,14 +35,20 @@
 
 
 def silu(values):
-    return values * (1.0 / (1.0 + jnp.exp(-values)))
-
-
-def norm_rows(values):
-    average = jnp.mean(values, axis=-1, keepdims=True)
-    centred = values - average
-    spread = jnp.mean(centred * centred, axis=-1, keepdims=True)
-    return centred * lax.rsqrt(spread + 1e-05)
+    half = 0.5 * values
+    return half + half * jnp.tanh(half)
+
+
+def centre(values):
+    return values - jnp.mean(values, axis=-1, keepdims=True)
+
+
+def scale(centred):
+    return lax.rsqrt(jnp.mean(centred * centred, axis=-1, keepdims=True) + 1e-05)
+
+
+def norm_centred(centred):
+    return centred * scale(centred)
 
 
 def gather_rows(first, count, row_of, pairs, unroll=16):
@@ -52,7 +58,11 @@
             target[pl.ds(i, 1), :] = source[pl.ds(row, 1), :]
         return carry
 
-    lax.fori_loop(first, first + count, step, 0, unroll=unroll)
+    if count <= unroll:
+        for i in range(first, first + count):
+            step(i, 0)
+    else:
+        lax.fori_loop(first, first + count, step, 0, unroll=unroll)
 
 
 def geometry_rows(geometry_ref, weight_ref):
@@ -94,6 +104,10 @@
 def wait(*copies):
     for copy in copies:
         copy.wait()
+
+
+def started():
+    pl.delay(1)
 
 
 def pack_kernel(
@@ -116,7 +130,7 @@
     chunk = out.shape[0] // 4
     stores = []
     for first in range(0, out.shape[0], chunk):
-        gather_rows(first, chunk, row_of, [(cells, out)])
+        gather_rows(first, chunk, row_of, [(cells, out)], 64)
         stores.append(
             copies.start(out.at[pl.ds(first, chunk)], out_ref.at[pl.ds(first, chunk)])
         )
@@ -140,20 +154,22 @@
 ):
     count = 8
     weight_refs, refs = refs[:count], refs[count:]
-    inner, refs = refs[:5], refs[5:]
-    received_ref, self_all_ref, self_sent_ref, nodes_sent_ref, match_ref = refs[:5]
-    split_refs, refs = refs[5 : 2 * count + 1], refs[2 * count + 1 :]
+    inner, refs = refs[:6], refs[6:]
+    self_all_ref, self_sent_ref, nodes_sent_ref, match_ref = refs[:4]
+    split_refs, refs = refs[4 : 2 * count], refs[2 * count :]
     nodes, weight_self, weight_receiver, weights, refs = *refs[:3], refs[3 : 3 + count], refs[3 + count :]
-    received, self_all, self_sent, nodes_sent, match = refs[:5]
-    splits, refs = refs[5 : 2 * count + 1], refs[2 * count + 1 :]
+    self_all, self_sent, nodes_sent, match = refs[:4]
+    splits, refs = refs[4 : 2 * count], refs[2 * count :]
     near, table, chosen, semaphores = refs
     copies = Copies(semaphores)
     load_nodes = copies.start(nodes_ref, nodes)
     load_self = copies.start(weight_self_ref, weight_self)
     load_receiver = copies.start(weight_receiver_ref, weight_receiver)
     loads = [copies.start(ref, weight) for ref, weight in zip(weight_refs, weights, strict=True)]
-    inner[4][0:1, :] = bias_one[...]
-    inner[4][1:2, :] = bias_two[...]
+    started()
+    received, biases = inner[4:]
+    biases[0:1, :] = centre(bias_one[...])
+    biases[1:2, :] = centre(bias_two[...])
     table[...] = target_matrix(nodes.shape[0], grid_targets)
     stores = []
     wait(load_nodes, load_self)
@@ -178,17 +194,24 @@
         + geometry_rows(geometry, weight_geometry)
         + edge_bias[...]
     )
-    stores.append(copies.start(received, received_ref))
     for k in range(count):
         wait(loads[k])
+        weight = weights[k][...]
+        if k % 2:
+            weight = centre(weight)
         if k < 2:
-            inner[2 * k][...], inner[2 * k + 1][...] = split(weights[k][...])
+            inner[2 * k][...], inner[2 * k + 1][...] = split(weight)
         else:
             at = 2 * (k - 2)
-            splits[at][...], splits[at + 1][...] = split(weights[k][...])
+            splits[at][...], splits[at + 1][...] = split(weight)
             stores.append(copies.start(splits[at], split_refs[at]))
             stores.append(copies.start(splits[at + 1], split_refs[at + 1]))
     wait(*stores)
+
+
+def edges(arrived, sender_high, sender_low, received, output_high, output_low, bias):
+    hidden = silu(dot3(arrived[...], sender_high[...], sender_low[...]) + received[...])
+    return dot3(hidden, output_high[...], output_low[...]) + bias
 
 
 def encode_kernel(
@@ -197,22 +220,21 @@
     sender_low,
     output_high,
     output_low,
+    received,
     biases,
-    received_ref,
     summed_high_ref,
     summed_low_ref,
+    match_ref,
     self_sent_ref,
-    match_ref,
     update_high_ref,
     update_low_ref,
     nodes_sent_ref,
     sent_ref,
     parts_ref,
-    received,
     summed_high,
     summed_low,
+    match,
     self_sent,
-    match,
     update_high,
     update_low,
     nodes_sent,
@@ -221,7 +243,6 @@
     semaphores,
 ):
     copies = Copies(semaphores)
-    load_received = copies.start(received_ref, received)
     load_summed_high = copies.start(summed_high_ref, summed_high)
     load_summed_low = copies.start(summed_low_ref, summed_low)
     load_match = copies.start(match_ref, match)
@@ -229,18 +250,18 @@
     load_update_high = copies.start(update_high_ref, update_high)
     load_update_low = copies.start(update_low_ref, update_low)
     load_nodes = copies.start(nodes_sent_ref, nodes_sent)
-    hidden = dot3(arrived[...], sender_high[...], sender_low[...])
-    wait(load_received)
-    hidden = silu(hidden + received[...])
-    messages = norm_rows(dot3(hidden, output_high[...], output_low[...]) + biases[0:1, :])
+    started()
+    rows = edges(
+        arrived, sender_high, sender_low, received, output_high, output_low, biases[0:1, :]
+    )
     wait(load_summed_high, load_summed_low)
-    part = dot3(messages, summed_high[...], summed_low[...])
+    part = dot3(rows, summed_high[...], summed_low[...]) * scale(rows)
     parts[...] = part
     store_parts = copies.start(parts, parts_ref)
     wait(load_match, load_self)
     hidden = silu(self_sent[...] + pick(match[...], part))
     wait(load_update_high, load_update_low, load_nodes)
-    sent[...] = nodes_sent[...] + norm_rows(
+    sent[...] = nodes_sent[...] + norm_centred(
         dot3(hidden, update_high[...], update_low[...]) + biases[1:2, :]
     )
     store_sent = copies.start(sent, sent_ref)
@@ -275,12 +296,13 @@
     sender_low,
     output_high,
     output_low,
+    received,
     biases,
-    received_ref,
     self_near_ref,
-    near_ref,
+    normed_ref,
     match_ref,
     base_ref,
+    firsts_ref,
     parts,
     self_all,
     nodes,
@@ -290,13 +312,15 @@
     weight_receiver,
     refine_high,
     refine_low,
-    received,
     self_near,
-    near,
+    normed_near,
     match,
     base,
+    firsts,
+    near,
     encoded,
     self_next,
+    normed,
     table,
     chosen,
     semaphores,
@@ -317,107 +341,122 @@
         copies.start(output_high_ref, output_high),
         copies.start(output_low_ref, output_low),
     ]
+    started()
     stores = []
-    biases[0:1, :] = bias_one[...]
-    biases[1:2, :] = refine_bias[...]
+    biases[0:1, :] = centre(bias_one[...])
+    biases[1:2, :] = centre(refine_bias[...])
     one_hot = target_matrix(nodes.shape[0], grid_targets).astype(BF16)
-    table[...] = target_matrix(nodes.shape[0], mesh_targets)
+    table[...] = target_matrix(table.shape[0], mesh_targets)
+    number = nodes.shape[0]
+
+    def node_or_empty(i):
+        target = mesh_targets_s[0, i]
+        return jnp.where(target < 0, number, target)
+
     wait(load_parts, load_all)
     hidden = silu(self_all[...] + pick(one_hot, parts[...]))
     wait(load_update_high, load_update_low, load_nodes)
-    encoded[...] = nodes[...] + norm_rows(
-        dot3(hidden, update_high[...], update_low[...]) + update_bias[...]
+    encoded[...] = nodes[...] + norm_centred(
+        dot3(hidden, update_high[...], update_low[...]) + centre(update_bias[...])
     )
     wait(load_self)
     self_next[...] = dot3(encoded[...], *split(weight_self[...])) + node_bias[...]
+    wait(load_refine_high, load_refine_low)
+    normed[...] = norm_centred(
+        dot3(silu(self_next[...]), refine_high[...], refine_low[...]) + centre(refine_bias[...])
+    )
+    base[...] = encoded[...] + normed[...]
+    stores.append(copies.start(base, base_ref))
     gather_rows(
         0,
         near.shape[0],
         lambda i: jnp.maximum(mesh_targets_s[0, i], 0),
-        [(encoded, near), (self_next, self_near), (table, chosen)],
-    )
-    match[...] = chosen[...].astype(BF16)
-    stores.append(copies.start(near, near_ref))
+        [(encoded, near), (self_next, self_near), (normed, normed_near)],
+    )
+    gather_rows(0, near.shape[0], node_or_empty, [(table, chosen)])
+    slots = near.shape[0]
+    same = chosen[...]
+    match[...] = same.astype(BF16)
+    earlier = lax.broadcasted_iota(jnp.int32, (slots, slots), 0) < lax.broadcasted_iota(
+        jnp.int32, (slots, slots), 1
+    )
+    repeats = jnp.sum(jnp.where(earlier, same, 0.0), axis=0, keepdims=True)
+    firsts[...] = jnp.where(repeats == 0.0, table[0:number, :], 0.0).astype(BF16)
     stores.append(copies.start(self_near, self_near_ref))
+    stores.append(copies.start(normed_near, normed_ref))
     stores.append(copies.start(match, match_ref))
+    stores.append(copies.start(firsts, firsts_ref))
     wait(load_receiver)
     received[...] = (
         dot3(near[...], *split(weight_receiver[...]))
         + geometry_rows(geometry, weight_geometry)
         + edge_bias[...]
     )
-    stores.append(copies.start(received, received_ref))
-    wait(load_refine_high, load_refine_low)
-    base[...] = encoded[...] + norm_rows(
-        dot3(silu(self_next[...]), refine_high[...], refine_low[...]) + refine_bias[...]
-    )
-    stores.append(copies.start(base, base_ref))
     wait(*passed, *stores)
 
 
 def refine_kernel(
-    mesh_targets_s,
     arrived,
     sender_high,
     sender_low,
     output_high,
     output_low,
+    received,
     biases,
-    received_ref,
     summed_high_ref,
     summed_low_ref,
     match_ref,
     self_near_ref,
     refine_high_ref,
     refine_low_ref,
-    near_ref,
+    normed_ref,
+    firsts_ref,
     base_ref,
     out_ref,
-    received,
     summed_high,
     summed_low,
     match,
     self_near,
     refine_high,
     refine_low,
-    near,
+    normed,
+    firsts,
     base,
-    rows,
+    out,
     semaphores,
 ):
     copies = Copies(semaphores)
-    number = base_ref.shape[0]
-    load_received = copies.start(received_ref, received)
     load_summed_high = copies.start(summed_high_ref, summed_high)
     load_summed_low = copies.start(summed_low_ref, summed_low)
     load_match = copies.start(match_ref, match)
     load_self = copies.start(self_near_ref, self_near)
     load_refine_high = copies.start(refine_high_ref, refine_high)
     load_refine_low = copies.start(refine_low_ref, refine_low)
-    load_near = copies.start(near_ref, near)
-    load_base = copies.start(base_ref, base.at[pl.ds(0, number)])
-    hidden = dot3(arrived[...], sender_high[...], sender_low[...])
-    wait(load_received)
-    hidden = silu(hidden + received[...])
-    messages = norm_rows(dot3(hidden, output_high[...], output_low[...]) + biases[0:1, :])
+    load_normed = copies.start(normed_ref, normed)
+    load_firsts = copies.start(firsts_ref, firsts)
+    load_base = copies.start(base_ref, base)
+    started()
+    rows = edges(
+        arrived, sender_high, sender_low, received, output_high, output_low, biases[0:1, :]
+    )
     wait(load_summed_high, load_summed_low)
-    part = dot3(messages, summed_high[...], summed_low[...])
+    part = dot3(rows, summed_high[...], summed_low[...]) * scale(rows)
     wait(load_match, load_self)
     hidden = silu(self_near[...] + pick(match[...], part))
-    wait(load_refine_high, load_refine_low, load_near)
-    rows[...] = near[...] + norm_rows(
-        dot3(hidden, refine_high[...], refine_low[...]) + biases[1:2, :]
-    )
-    wait(load_base)
-
-    def place(i, carry):
-        target = mesh_targets_s[0, i]
-        target = jnp.where(target < 0, number, target)
-        base[pl.ds(target, 1), :] = rows[pl.ds(i, 1), :]
-        return carry
-
-    lax.fori_loop(0, rows.shape[0], place, 0, unroll=16)
-    wait(copies.start(base.at[pl.ds(0, number)], out_ref))
+    wait(load_refine_high, load_refine_low, load_normed)
+    change = norm_centred(dot3(hidden, refine_high[...], refine_low[...]) + biases[1:2, :])
+    high, low = split(change - normed[...])
+    wait(load_firsts, load_base)
+    number = out.shape[0]
+    chunk = number // 2
+    stores = []
+    for first in range(0, number, chunk):
+        at = pl.ds(first, chunk)
+        out[at, :] = base[at, :] + (dot(firsts[at, :], high) + dot(firsts[at, :], low))
+        stores.append(copies.start(out.at[at], out_ref.at[at]))
+        if first + chunk < number:
+            started()
+    wait(*stores)
 
 
 def flat(dims, kind=F32):
@@ -525,8 +564,6 @@
     ]
     (
         *first,
-        biases,
-        received,
         self_all,
         self_sent,
         nodes_sent,
@@ -560,14 +597,13 @@
         [],
         [mesh_latent, update_self, encoder_receiver] + weights,
         [
-            flat((grid_slots, width)),
             flat((number, width)),
             flat((mesh_slots, width)),
             flat((mesh_slots, width)),
             flat((mesh_slots, grid_slots), BF16),
         ]
         + halves * 6,
-        halves * 2 + [flat((8, width))],
+        halves * 2 + [flat((grid_slots, width)), flat((8, width))],
         [
             pltpu.VMEM((grid_slots, width), F32),
             pltpu.VMEM((number, grid_slots), F32),
@@ -580,12 +616,12 @@
         (3 * grid_slots + mesh_slots) * square * 3,
         [],
         [],
-        [grid_in, *first, biases],
-        [received, summed_high, summed_low, self_sent, match, update_high, update_low, nodes_sent],
+        [grid_in, *first],
+        [summed_high, summed_low, match, self_sent, update_high, update_low, nodes_sent],
         [flat((mesh_slots, width)), flat((grid_slots, width))],
     )
     mesh_in = exchange(sent, patches)
-    *first, biases, received, self_near, near, match, base = call(
+    *first, self_near, normed, match, base, firsts = call(
         between_kernel,
         "between",
         (3 * number + mesh_slots) * square * 3,
@@ -616,43 +652,42 @@
         [
             flat((mesh_slots, width)),
             flat((mesh_slots, width)),
-            flat((mesh_slots, width)),
             flat((mesh_slots, mesh_slots), BF16),
             flat((number, width)),
+            flat((number, mesh_slots), BF16),
         ],
-        halves * 2 + [flat((8, width))],
+        halves * 2 + [flat((mesh_slots, width)), flat((8, width))],
         [
+            pltpu.VMEM((mesh_slots, width), F32),
             pltpu.VMEM((number, width), F32),
             pltpu.VMEM((number, width), F32),
-            pltpu.VMEM((number, mesh_slots), F32),
+            pltpu.VMEM((number, width), F32),
+            pltpu.VMEM((number + 8, mesh_slots), F32),
             pltpu.VMEM((mesh_slots, mesh_slots), F32),
         ],
         [sender_high, sender_low, output_high, output_low],
     )
-    return refine_call(
-        mesh_targets, mesh_in, first, biases, received, second_high, second_low, match, self_near,
-        refine_high, refine_low, near, base,
-    )
-
-
-def refine_call(targets, arrived, first, biases, *large):
-    base = large[-1]
-    number, width = base.shape
-    slots = targets.shape[1]
-    kept = [pltpu.with_memory_space_constraint(x, pltpu.VMEM) for x in [arrived, *first, biases]]
-    large = [pltpu.with_memory_space_constraint(x, pltpu.HBM) for x in large]
-    twins = [pltpu.VMEM(x.shape, x.dtype) for x in large[:-1]]
-    twins += [pltpu.VMEM((number + 8, width), F32), pltpu.VMEM((slots, width), F32)]
-    size = sum(4 * spec.inner_aval.size for spec in twins)
-    return pl.pallas_call(
+    (out,) = call(
         refine_kernel,
-        out_shape=flat((number, width)),
-        in_specs=[SMEM] + [VMEM] * len(kept) + [HBM] * len(large),
-        out_specs=HBM,
-        scratch_shapes=[*twins, pltpu.SemaphoreType.DMA((len(large) + 1,))],
-        compiler_params=pltpu.CompilerParams(vmem_limit_bytes=size + 12 * 2**20),
-        name="refine",
-    )(targets, *kept, *large)
+        "refine",
+        4 * mesh_slots * square * 3,
+        [],
+        [],
+        [mesh_in, *first],
+        [
+            second_high,
+            second_low,
+            match,
+            self_near,
+            refine_high,
+            refine_low,
+            normed,
+            firsts,
+            base,
+        ],
+        [flat((number, width))],
+    )
+    return out
 
 
 def solution(mesh):

time: 58.4 us -> 54.5 us (0.933)
  Pallas kernels: 36.3 us -> 32.4 us
    pallas_call x1 -> x0, Pallas kernels: 6.6 us -> none  [refine_call(): pl.pallas_call(refine_kernel, out_shape=flat((number, width)), in_specs=[...]
    pallas_call x4 -> x5, Pallas kernels: 29.7 us -> 32.4 us  [call(): pl.pallas_call(kernel, out_shape=[pltpu.VMEM(array.shape, array.dtype) fo...]
  transfers between devices with their start and end apart: 2 -> 2, of which waited for: 2 -> 2; matrix products, arithmetic and copies ran while one was open for 0% -> 0% of each run, Pallas kernels for 36% -> 39%
where the time goes in v3:
time: 54.5 us; the launch traced here: 54.1 us
  Pallas kernels  32.4 us (59%)
  waiting for transfers between devices  11.1 us (20%)
  starting transfers between devices  10.1 us (19%)
    pallas_call x5, Pallas kernels, call(): pl.pallas_call(kernel, out_shape=[pltpu.VMEM(array.shape, array.dtype) fo...  32.4 us
    all_to_all x2, waiting for transfers between devices, exchange(): lax.all_to_all(blocks, ('lat', 'lon'), split_axis=0, concat_axis=0, tiled...  11.1 us
    all_to_all x2, starting transfers between devices, exchange(): lax.all_to_all(blocks, ('lat', 'lon'), split_axis=0, concat_axis=0, tiled...  10.1 us
  transfers between devices with their start and end apart: 2, of which 2 were waited for; matrix products, arithmetic and copies ran while one was open for 0% of the time, Pallas kernels for 39%

profile of v3, /device:TPU:0, one launch (start us, length us, event | category | flops | bytes accessed | tf_op | source)
XLA Modules:
  0.0 54.1 jit_solution(15809128024823489139)
XLA Ops:
  0.0 0.0 copy-start
  0.0 0.0 copy-start.1
  0.0 0.0 copy-start.2
  0.0 0.0 copy-start.3
  0.0 0.0 copy-start.4
  0.0 0.0 copy-start.5
  0.0 0.0 copy-start.6
  0.0 0.0 copy-start.7
  0.0 3.0 %pack.1 = f32[256,512]{1,0:T(8,128)} custom-call(s32[8,32]{1,0:T(8,128)} %bitcast.36, f32[720,512]{1,0:T(8,128)} %bitcast.34), custom_call_target="tpu_custom_call" | custom-call | flops 1000 | bytes 4194304 | tf_op jit(solution)/shard_map/pack/pallas_call | solution.py:475
  3.1 7.3 %all-to-all-start = ((f32[32,8,512]{2,1,0:T(8,128)}), f32[32,8,512]{2,1,0:T(8,128)S(1)}, u32[]{:S(2)}, u32[]{:S(2)}) async-start(f32[32,8,512]{2,1,0:T(8,128)} %bitcast.33), calls=%async_computation | async-start | bytes 1048576 | tf_op jit(solution)/shard_map/all_to_all | solution.py:495
  10.4 0.0 copy-done
  10.4 0.0 copy-done.1
  10.4 0.0 copy-done.2
  10.5 0.0 copy-done.3
  10.5 0.0 copy-done.4
  10.5 0.0 copy-done.5
  10.5 0.0 copy-done.6
  10.5 0.0 copy-done.7
  10.5 10.5 %before.1 = (bf16[512,512]{1,0:T(8,128)(2,1)S(1)}, bf16[512,512]{1,0:T(8,128)(2,1)S(1)}, bf16[512,512]{1,0:T(8,128)(2,1)S(1)}, bf16[512,512]{1,0:T(8,128)(2,1)S(...) custom-call(s32[1,256]{1,0:T(1,128)S(1)} %copy-done.3, ...), custom_call_target="tpu_custom_call" | custom-call | flops 1409286144 | bytes 4194304 | tf_op jit(solution)/shard_map/before/pallas_call | solution.py:475
  21.0 5.6 %all-to-all-done = f32[32,8,512]{2,1,0:T(8,128)S(1)} async-done(((f32[32,8,512]{2,1,0:T(8,128)}), f32[32,8,512]{2,1,0:T(8,128)S(1)}, u32[]{:S(2)}, u32[]{:S(2)}) %all-to-all-start) | async-done | bytes 524320 | tf_op jit(solution)/shard_map/all_to_all | solution.py:495
  26.7 0.0 copy-start.8
  26.7 0.0 copy-start.9
  26.7 0.0 copy-start.10
  26.7 0.0 copy-start.11
  26.7 0.0 copy-start.12
  26.7 0.0 copy-start.13
  26.7 0.0 copy-start.14
  26.7 3.9 %encode.1 = (f32[256,512]{1,0:T(8,128)}, f32[256,512]{1,0:T(8,128)}) custom-call(f32[256,512]{1,0:T(8,128)S(1)} %bitcast.22, bf16[512,512]{1,0:T(8,128)(2,1)S(1)} %get-tuple-element.40.sender_high, bf16[512,512]{1,0:T(8,128)(2,1)S(1)} %get-tuple-element.41.sender_low, bf16[512,512]{1,0:T(8,128)(2,1)S(1)} %get-tuple-element.42.output_high, ...), custom_call_target="tpu_custom_call" | custom-call | flops 1610612736 | bytes 4194304 | tf_op jit(solution)/shard_map/encode/pallas_call | solution.py:475
  30.6 2.8 %all-to-all-start.1 = ((f32[32,8,512]{2,1,0:T(8,128)}), f32[32,8,512]{2,1,0:T(8,128)S(1)}, u32[]{:S(2)}, u32[]{:S(2)}) async-start(f32[32,8,512]{2,1,0:T(8,128)} %bitcast.35), calls=%async_computation.1 | async-start | bytes 1048576 | tf_op jit(solution)/shard_map/all_to_all | solution.py:495
  33.4 0.0 copy-done.8
  33.4 0.0 copy-done.9
  33.4 0.0 copy-done.10
  33.4 0.0 copy-done.11
  33.4 0.0 copy-done.12
  33.5 0.0 copy-done.13
  33.5 0.0 copy-done.14
  33.5 10.5 %between.1 = (bf16[512,512]{1,0:T(8,128)(2,1)S(1)}, bf16[512,512]{1,0:T(8,128)(2,1)S(1)}, bf16[512,512]{1,0:T(8,128)(2,1)S(1)}, bf16[512,512]{1,0:T(8,128)(2,1)S...) custom-call(s32[1,256]{1,0:T(1,128)S(1)} %copy-done.14, ...), custom_call_target="tpu_custom_call" | custom-call | flops 3422552064 | bytes 4194304 | tf_op jit(solution)/shard_map/between/pallas_call | solution.py:475
  44.0 5.5 %all-to-all-done.1 = f32[32,8,512]{2,1,0:T(8,128)S(1)} async-done(((f32[32,8,512]{2,1,0:T(8,128)}), f32[32,8,512]{2,1,0:T(8,128)S(1)}, u32[]{:S(2)}, u32[]{:S(2)}) %all-to-all-start.1) | async-done | bytes 524320 | tf_op jit(solution)/shard_map/all_to_all | solution.py:495
  49.5 4.5 %refine.1 = f32[640,512]{1,0:T(8,128)} custom-call(f32[256,512]{1,0:T(8,128)S(1)} %bitcast.21, bf16[512,512]{1,0:T(8,128)(2,1)S(1)} %get-tuple-element.62.sender_high, bf16[512,512]{1,0:T(8,128)(2,1)S(1)} %get-tuple-element.63.sender_low, bf16[512,512]{1,0:T(8,128)(2,1)S(1)} %get-tuple-element.64.output_high, ...), custom_call_target="tpu_custom_call" | custom-call | flops 1610612736 | bytes 4194304 | tf_op jit(solution)/shard_map/refine/pallas_call | solution.py:475
Async XLA Ops:
  0.0 10.4 %copy-start = (f32[4,512]{1,0:T(4,128)S(1)}, f32[4,512]{1,0:T(4,128)}, u32[]{:S(2)}) copy-start(f32[4,512]{1,0:T(4,128)} %weight_geometry.2) | copy-start | bytes 24580
  0.0 10.4 %copy-start.1 = (s32[1,32,8]{1,2,0:T(8,128)S(1)}, s32[1,32,8]{1,2,0:T(8,128)}, u32[]{:S(2)}) copy-start(s32[1,32,8]{1,2,0:T(8,128)} %param.35) | copy-start | bytes 3076
  0.0 10.4 %copy-start.2 = (f32[4,1,256]{2,1,0:T(1,128)S(1)}, f32[4,1,256]{2,1,0:T(1,128)}, u32[]{:S(2)}) copy-start(f32[4,1,256]{2,1,0:T(1,128)} %geometry.2) | copy-start | bytes 12292
  0.0 10.5 %copy-start.3 = (s32[1,256]{1,0:T(1,128)S(1)}, s32[1,256]{1,0:T(1,128)}, u32[]{:S(2)}) copy-start(s32[1,256]{1,0:T(1,128)} %grid_targets.3) | copy-start | bytes 3076
  0.0 10.5 %copy-start.4 = (f32[512]{0:T(512)S(1)}, f32[512]{0:T(512)}, u32[]{:S(2)}) copy-start(f32[512]{0:T(512)} %param.41) | copy-start | bytes 6148
  0.0 10.5 %copy-start.5 = (f32[512]{0:T(512)S(1)}, f32[512]{0:T(512)}, u32[]{:S(2)}) copy-start(f32[512]{0:T(512)} %param.46) | copy-start | bytes 6148
  0.0 10.5 %copy-start.6 = (f32[512]{0:T(512)S(1)}, f32[512]{0:T(512)}, u32[]{:S(2)}) copy-start(f32[512]{0:T(512)} %param.43) | copy-start | bytes 6148
  0.0 10.5 %copy-start.7 = (f32[512]{0:T(512)S(1)}, f32[512]{0:T(512)}, u32[]{:S(2)}) copy-start(f32[512]{0:T(512)} %param.48) | copy-start | bytes 6148
  3.1 23.6 %all-to-all-start = ((f32[32,8,512]{2,1,0:T(8,128)}), f32[32,8,512]{2,1,0:T(8,128)S(1)}, u32[]{:S(2)}, u32[]{:S(2)}) async-start(f32[32,8,512]{2,1,0:T(8,128)} %bitcast.33), calls=%async_computation | async-start | bytes 1048576 | tf_op jit(solution)/shard_map/all_to_all | solution.py:495
  26.7 6.7 %copy-start.8 = (f32[4,512]{1,0:T(4,128)S(1)}, f32[4,512]{1,0:T(4,128)}, u32[]{:S(2)}) copy-start(f32[4,512]{1,0:T(4,128)} %weight_geometry.3) | copy-start | bytes 24580
  26.7 6.8 %copy-start.9 = (f32[4,1,256]{2,1,0:T(1,128)S(1)}, f32[4,1,256]{2,1,0:T(1,128)}, u32[]{:S(2)}) copy-start(f32[4,1,256]{2,1,0:T(1,128)} %geometry.3) | copy-start | bytes 12292
  26.7 6.8 %copy-start.10 = (f32[512]{0:T(512)S(1)}, f32[512]{0:T(512)}, u32[]{:S(2)}) copy-start(f32[512]{0:T(512)} %param.52) | copy-start | bytes 6148
  26.7 6.8 %copy-start.11 = (f32[512]{0:T(512)S(1)}, f32[512]{0:T(512)}, u32[]{:S(2)}) copy-start(f32[512]{0:T(512)} %param.57) | copy-start | bytes 6148
  26.7 6.8 %copy-start.12 = (f32[512]{0:T(512)S(1)}, f32[512]{0:T(512)}, u32[]{:S(2)}) copy-start(f32[512]{0:T(512)} %param.59) | copy-start | bytes 6148
  26.7 6.8 %copy-start.13 = (f32[512]{0:T(512)S(1)}, f32[512]{0:T(512)}, u32[]{:S(2)}) copy-start(f32[512]{0:T(512)} %param.54) | copy-start | bytes 6148
  26.7 6.8 %copy-start.14 = (s32[1,256]{1,0:T(1,128)S(1)}, s32[1,256]{1,0:T(1,128)}, u32[]{:S(2)}) copy-start(s32[1,256]{1,0:T(1,128)} %mesh_targets.1) | copy-start | bytes 3076
  30.6 18.9 %all-to-all-start.1 = ((f32[32,8,512]{2,1,0:T(8,128)}), f32[32,8,512]{2,1,0:T(8,128)S(1)}, u32[]{:S(2)}, u32[]{:S(2)}) async-start(f32[32,8,512]{2,1,0:T(8,128)} %bitcast.35), calls=%async_computation.1 | async-start | bytes 1048576 | tf_op jit(solution)/shard_map/all_to_all | solution.py:495

commit v4 on v3

--- a/solution.py
+++ b/solution.py
@@ -58,7 +58,7 @@
             target[pl.ds(i, 1), :] = source[pl.ds(row, 1), :]
         return carry
 
-    if count <= unroll:
+    if count <= 256:
         for i in range(first, first + count):
             step(i, 0)
     else:
@@ -130,11 +130,16 @@
     chunk = out.shape[0] // 4
     stores = []
     for first in range(0, out.shape[0], chunk):
-        gather_rows(first, chunk, row_of, [(cells, out)], 64)
+        gather_rows(first, chunk, row_of, [(cells, out)])
         stores.append(
             copies.start(out.at[pl.ds(first, chunk)], out_ref.at[pl.ds(first, chunk)])
         )
     wait(*stores)
+
+
+def rows_of(*biases):
+    width = biases[0].shape[1]
+    return jnp.concatenate([*biases, jnp.zeros((8 - len(biases), width), F32)], axis=0)
 
 
 def before_kernel(
@@ -145,46 +150,112 @@
     weight_geometry,
     edge_bias,
     node_bias,
-    bias_one,
-    bias_two,
+    output_bias,
+    update_bias,
+    output_bias_2,
+    refine_bias,
     nodes_ref,
     weight_self_ref,
     weight_receiver_ref,
-    *refs,
+    output_ref,
+    summed_ref,
+    sender_ref,
+    update_ref,
+    sender_ref_2,
+    output_ref_2,
+    summed_ref_2,
+    refine_ref,
+    sender_high,
+    sender_low,
+    merged_high,
+    merged_low,
+    received,
+    biases,
+    self_all_ref,
+    self_sent_ref,
+    nodes_sent_ref,
+    match_ref,
+    output_high_ref,
+    onward_high_ref,
+    onward_low_ref,
+    update_high_ref,
+    update_low_ref,
+    merged_high_ref_2,
+    merged_low_ref_2,
+    output_high_ref_2,
+    refine_high_ref,
+    refine_low_ref,
+    biases_ref_2,
+    nodes,
+    weight_self,
+    weight_receiver,
+    output,
+    summed,
+    sender,
+    update,
+    sender_2,
+    output_2,
+    summed_2,
+    refine,
+    self_all,
+    self_sent,
+    nodes_sent,
+    match,
+    output_high,
+    onward_high,
+    onward_low,
+    update_high,
+    update_low,
+    merged_high_2,
+    merged_low_2,
+    output_high_2,
+    refine_high,
+    refine_low,
+    biases_2,
+    near,
+    picked,
+    table,
+    chosen,
+    semaphores,
 ):
-    count = 8
-    weight_refs, refs = refs[:count], refs[count:]
-    inner, refs = refs[:6], refs[6:]
-    self_all_ref, self_sent_ref, nodes_sent_ref, match_ref = refs[:4]
-    split_refs, refs = refs[4 : 2 * count], refs[2 * count :]
-    nodes, weight_self, weight_receiver, weights, refs = *refs[:3], refs[3 : 3 + count], refs[3 + count :]
-    self_all, self_sent, nodes_sent, match = refs[:4]
-    splits, refs = refs[4 : 2 * count], refs[2 * count :]
-    near, table, chosen, semaphores = refs
     copies = Copies(semaphores)
     load_nodes = copies.start(nodes_ref, nodes)
     load_self = copies.start(weight_self_ref, weight_self)
+    load_output = copies.start(output_ref, output)
+    load_summed = copies.start(summed_ref, summed)
     load_receiver = copies.start(weight_receiver_ref, weight_receiver)
-    loads = [copies.start(ref, weight) for ref, weight in zip(weight_refs, weights, strict=True)]
+    load_sender = copies.start(sender_ref, sender)
+    load_update = copies.start(update_ref, update)
+    load_sender_2 = copies.start(sender_ref_2, sender_2)
+    load_output_2 = copies.start(output_ref_2, output_2)
+    load_summed_2 = copies.start(summed_ref_2, summed_2)
+    load_refine = copies.start(refine_ref, refine)
     started()
-    received, biases = inner[4:]
-    biases[0:1, :] = centre(bias_one[...])
-    biases[1:2, :] = centre(bias_two[...])
+    stores = []
+
+    def store(*pairs):
+        stores.extend(copies.start(source, target) for source, target in pairs)
+
     table[...] = target_matrix(nodes.shape[0], grid_targets)
-    stores = []
     wait(load_nodes, load_self)
     self_all[...] = dot3(nodes[...], *split(weight_self[...])) + node_bias[...]
-    stores.append(copies.start(self_all, self_all_ref))
+    store((self_all, self_all_ref))
     gather_rows(
         0,
-        mesh_senders_s.shape[0] * mesh_senders_s.shape[1],
+        picked.shape[0],
         slot_order(mesh_senders_s),
-        [(nodes, nodes_sent), (self_all, self_sent), (table, chosen)],
+        [(nodes, picked), (self_all, self_sent), (table, chosen)],
     )
     match[...] = chosen[...].astype(BF16)
-    stores.append(copies.start(self_sent, self_sent_ref))
-    stores.append(copies.start(nodes_sent, nodes_sent_ref))
-    stores.append(copies.start(match, match_ref))
+    store((self_sent, self_sent_ref), (match, match_ref))
+    wait(load_output, load_summed)
+    centred = centre(output[...])
+    high, low = split(summed[...])
+    merged_high[...], merged_low[...] = split(dot3(centred, high, low))
+    output_high[...] = centred.astype(BF16)
+    store((output_high, output_high_ref))
+    first_bias = centre(output_bias[...])
+    first_bias_on = dot3(rows_of(first_bias), high, low)[0:1, :]
     gather_rows(
         0, near.shape[0], lambda i: jnp.maximum(grid_targets_s[0, i], 0), [(nodes, near)]
     )
@@ -194,75 +265,102 @@
         + geometry_rows(geometry, weight_geometry)
         + edge_bias[...]
     )
-    for k in range(count):
-        wait(loads[k])
-        weight = weights[k][...]
-        if k % 2:
-            weight = centre(weight)
-        if k < 2:
-            inner[2 * k][...], inner[2 * k + 1][...] = split(weight)
-        else:
-            at = 2 * (k - 2)
-            splits[at][...], splits[at + 1][...] = split(weight)
-            stores.append(copies.start(splits[at], split_refs[at]))
-            stores.append(copies.start(splits[at + 1], split_refs[at + 1]))
+    wait(load_sender)
+    sender_high[...], sender_low[...] = split(sender[...])
+    wait(load_update, load_sender_2)
+    centred = centre(update[...])
+    update_high[...], update_low[...] = split(centred)
+    high, low = split(sender_2[...])
+    onward_high[...], onward_low[...] = split(dot3(centred, high, low))
+    nodes_sent[...] = dot3(picked[...], high, low)
+    store(
+        (update_high, update_high_ref),
+        (update_low, update_low_ref),
+        (onward_high, onward_high_ref),
+        (onward_low, onward_low_ref),
+        (nodes_sent, nodes_sent_ref),
+    )
+    second_bias = centre(update_bias[...])
+    second_bias_on = dot3(rows_of(second_bias), high, low)[0:1, :]
+    biases[...] = rows_of(first_bias, first_bias_on, second_bias, second_bias_on)
+    wait(load_output_2, load_summed_2, load_refine)
+    centred = centre(output_2[...])
+    high, low = split(summed_2[...])
+    merged_high_2[...], merged_low_2[...] = split(dot3(centred, high, low))
+    output_high_2[...] = centred.astype(BF16)
+    third_bias = centre(output_bias_2[...])
+    third_bias_on = dot3(rows_of(third_bias), high, low)[0:1, :]
+    biases_2[...] = rows_of(third_bias, third_bias_on, centre(refine_bias[...]))
+    refine_high[...], refine_low[...] = split(centre(refine[...]))
+    store(
+        (merged_high_2, merged_high_ref_2),
+        (merged_low_2, merged_low_ref_2),
+        (output_high_2, output_high_ref_2),
+        (refine_high, refine_high_ref),
+        (refine_low, refine_low_ref),
+        (biases_2, biases_ref_2),
+    )
     wait(*stores)
 
 
-def edges(arrived, sender_high, sender_low, received, output_high, output_low, bias):
-    hidden = silu(dot3(arrived[...], sender_high[...], sender_low[...]) + received[...])
-    return dot3(hidden, output_high[...], output_low[...]) + bias
+def edges(hidden, merged_high, merged_low, output_high, bias, bias_on):
+    hidden_high, hidden_low = split(hidden)
+    high = merged_high[...]
+    total = dot(hidden_high, high) + (
+        dot(hidden_low, high) + dot(hidden_high, merged_low[...])
+    )
+    return (total + bias_on) * scale(dot(hidden_high, output_high[...]) + bias)
 
 
 def encode_kernel(
     arrived,
     sender_high,
     sender_low,
-    output_high,
-    output_low,
+    merged_high,
+    merged_low,
     received,
     biases,
-    summed_high_ref,
-    summed_low_ref,
+    output_high_ref,
     match_ref,
     self_sent_ref,
+    onward_high_ref,
+    onward_low_ref,
     update_high_ref,
-    update_low_ref,
     nodes_sent_ref,
     sent_ref,
     parts_ref,
-    summed_high,
-    summed_low,
+    output_high,
     match,
     self_sent,
+    onward_high,
+    onward_low,
     update_high,
-    update_low,
     nodes_sent,
     sent,
     parts,
     semaphores,
 ):
     copies = Copies(semaphores)
-    load_summed_high = copies.start(summed_high_ref, summed_high)
-    load_summed_low = copies.start(summed_low_ref, summed_low)
+    load_output = copies.start(output_high_ref, output_high)
     load_match = copies.start(match_ref, match)
     load_self = copies.start(self_sent_ref, self_sent)
-    load_update_high = copies.start(update_high_ref, update_high)
-    load_update_low = copies.start(update_low_ref, update_low)
+    load_onward_high = copies.start(onward_high_ref, onward_high)
+    load_onward_low = copies.start(onward_low_ref, onward_low)
+    load_update = copies.start(update_high_ref, update_high)
     load_nodes = copies.start(nodes_sent_ref, nodes_sent)
     started()
-    rows = edges(
-        arrived, sender_high, sender_low, received, output_high, output_low, biases[0:1, :]
-    )
-    wait(load_summed_high, load_summed_low)
-    part = dot3(rows, summed_high[...], summed_low[...]) * scale(rows)
+    hidden = silu(dot3(arrived[...], sender_high[...], sender_low[...]) + received[...])
+    wait(load_output)
+    part = edges(
+        hidden, merged_high, merged_low, output_high, biases[0:1, :], biases[1:2, :]
+    )
     parts[...] = part
     store_parts = copies.start(parts, parts_ref)
     wait(load_match, load_self)
     hidden = silu(self_sent[...] + pick(match[...], part))
-    wait(load_update_high, load_update_low, load_nodes)
-    sent[...] = nodes_sent[...] + norm_centred(
-        dot3(hidden, update_high[...], update_low[...]) + biases[1:2, :]
+    wait(load_onward_high, load_onward_low, load_update, load_nodes)
+    sent[...] = nodes_sent[...] + edges(
+        hidden, onward_high, onward_low, update_high, biases[2:3, :], biases[3:4, :]
     )
     store_sent = copies.start(sent, sent_ref)
     wait(store_parts, store_sent)
@@ -278,11 +376,10 @@
     node_bias,
     update_bias,
     refine_bias,
-    bias_one,
-    sender_high_ref,
-    sender_low_ref,
+    merged_high_ref,
+    merged_low_ref,
     output_high_ref,
-    output_low_ref,
+    biases_ref,
     parts_ref,
     self_all_ref,
     nodes_ref,
@@ -292,15 +389,14 @@
     weight_receiver_ref,
     refine_high_ref,
     refine_low_ref,
-    sender_high,
-    sender_low,
+    merged_high,
+    merged_low,
     output_high,
-    output_low,
     received,
+    self_near,
+    match,
     biases,
-    self_near_ref,
     normed_ref,
-    match_ref,
     base_ref,
     firsts_ref,
     parts,
@@ -312,9 +408,7 @@
     weight_receiver,
     refine_high,
     refine_low,
-    self_near,
     normed_near,
-    match,
     base,
     firsts,
     near,
@@ -336,15 +430,13 @@
     load_refine_high = copies.start(refine_high_ref, refine_high)
     load_refine_low = copies.start(refine_low_ref, refine_low)
     passed = [
-        copies.start(sender_high_ref, sender_high),
-        copies.start(sender_low_ref, sender_low),
+        copies.start(merged_high_ref, merged_high),
+        copies.start(merged_low_ref, merged_low),
         copies.start(output_high_ref, output_high),
-        copies.start(output_low_ref, output_low),
+        copies.start(biases_ref, biases),
     ]
     started()
     stores = []
-    biases[0:1, :] = centre(bias_one[...])
-    biases[1:2, :] = centre(refine_bias[...])
     one_hot = target_matrix(nodes.shape[0], grid_targets).astype(BF16)
     table[...] = target_matrix(table.shape[0], mesh_targets)
     number = nodes.shape[0]
@@ -382,9 +474,7 @@
     )
     repeats = jnp.sum(jnp.where(earlier, same, 0.0), axis=0, keepdims=True)
     firsts[...] = jnp.where(repeats == 0.0, table[0:number, :], 0.0).astype(BF16)
-    stores.append(copies.start(self_near, self_near_ref))
     stores.append(copies.start(normed_near, normed_ref))
-    stores.append(copies.start(match, match_ref))
     stores.append(copies.start(firsts, firsts_ref))
     wait(load_receiver)
     received[...] = (
@@ -397,26 +487,19 @@
 
 def refine_kernel(
     arrived,
-    sender_high,
-    sender_low,
+    merged_high,
+    merged_low,
     output_high,
-    output_low,
     received,
+    self_near,
+    match,
     biases,
-    summed_high_ref,
-    summed_low_ref,
-    match_ref,
-    self_near_ref,
     refine_high_ref,
     refine_low_ref,
     normed_ref,
     firsts_ref,
     base_ref,
     out_ref,
-    summed_high,
-    summed_low,
-    match,
-    self_near,
     refine_high,
     refine_low,
     normed,
@@ -426,25 +509,23 @@
     semaphores,
 ):
     copies = Copies(semaphores)
-    load_summed_high = copies.start(summed_high_ref, summed_high)
-    load_summed_low = copies.start(summed_low_ref, summed_low)
-    load_match = copies.start(match_ref, match)
-    load_self = copies.start(self_near_ref, self_near)
     load_refine_high = copies.start(refine_high_ref, refine_high)
     load_refine_low = copies.start(refine_low_ref, refine_low)
     load_normed = copies.start(normed_ref, normed)
     load_firsts = copies.start(firsts_ref, firsts)
     load_base = copies.start(base_ref, base)
     started()
-    rows = edges(
-        arrived, sender_high, sender_low, received, output_high, output_low, biases[0:1, :]
-    )
-    wait(load_summed_high, load_summed_low)
-    part = dot3(rows, summed_high[...], summed_low[...]) * scale(rows)
-    wait(load_match, load_self)
+    part = edges(
+        silu(arrived[...] + received[...]),
+        merged_high,
+        merged_low,
+        output_high,
+        biases[0:1, :],
+        biases[1:2, :],
+    )
     hidden = silu(self_near[...] + pick(match[...], part))
     wait(load_refine_high, load_refine_low, load_normed)
-    change = norm_centred(dot3(hidden, refine_high[...], refine_low[...]) + biases[1:2, :])
+    change = norm_centred(dot3(hidden, refine_high[...], refine_low[...]) + biases[2:3, :])
     high, low = split(change - normed[...])
     wait(load_firsts, load_base)
     number = out.shape[0]
@@ -552,34 +633,23 @@
     )
     grid_in = exchange(packed, patches)
 
-    weights = [
-        encoder_sender,
-        encoder_output,
-        update_summed,
-        update_output,
-        process_sender,
-        process_output,
-        refine_summed,
-        refine_output,
-    ]
     (
         *first,
         self_all,
         self_sent,
         nodes_sent,
         match,
-        summed_high,
-        summed_low,
+        output_high,
+        onward_high,
+        onward_low,
         update_high,
         update_low,
-        sender_high,
-        sender_low,
-        output_high,
-        output_low,
+        merged_high,
+        merged_low,
         second_high,
-        second_low,
         refine_high,
         refine_low,
+        biases,
     ) = call(
         before_kernel,
         "before",
@@ -593,19 +663,35 @@
             row(update_bias),
             row(encoder_outbias),
             row(update_outbias),
-        ],
-        [],
-        [mesh_latent, update_self, encoder_receiver] + weights,
+            row(process_outbias),
+            row(refine_outbias),
+        ],
+        [],
+        [
+            mesh_latent,
+            update_self,
+            encoder_receiver,
+            encoder_output,
+            update_summed,
+            encoder_sender,
+            update_output,
+            process_sender,
+            process_output,
+            refine_summed,
+            refine_output,
+        ],
         [
             flat((number, width)),
             flat((mesh_slots, width)),
             flat((mesh_slots, width)),
             flat((mesh_slots, grid_slots), BF16),
         ]
-        + halves * 6,
+        + halves * 5
+        + [flat((8, width))],
         halves * 2 + [flat((grid_slots, width)), flat((8, width))],
         [
             pltpu.VMEM((grid_slots, width), F32),
+            pltpu.VMEM((mesh_slots, width), F32),
             pltpu.VMEM((number, grid_slots), F32),
             pltpu.VMEM((mesh_slots, grid_slots), F32),
         ],
@@ -617,11 +703,11 @@
         [],
         [],
         [grid_in, *first],
-        [summed_high, summed_low, match, self_sent, update_high, update_low, nodes_sent],
+        [output_high, match, self_sent, onward_high, onward_low, update_high, nodes_sent],
         [flat((mesh_slots, width)), flat((grid_slots, width))],
     )
     mesh_in = exchange(sent, patches)
-    *first, self_near, normed, match, base, firsts = call(
+    *first, normed, base, firsts = call(
         between_kernel,
         "between",
         (3 * number + mesh_slots) * square * 3,
@@ -635,7 +721,6 @@
             row(refine_bias),
             row(update_outbias),
             row(refine_outbias),
-            row(process_outbias),
         ],
         [],
         [
@@ -651,12 +736,17 @@
         ],
         [
             flat((mesh_slots, width)),
+            flat((number, width)),
+            flat((number, mesh_slots), BF16),
+        ],
+        [
+            *halves,
+            halves[0],
+            flat((mesh_slots, width)),
             flat((mesh_slots, width)),
             flat((mesh_slots, mesh_slots), BF16),
-            flat((number, width)),
-            flat((number, mesh_slots), BF16),
-        ],
-        halves * 2 + [flat((mesh_slots, width)), flat((8, width))],
+            flat((8, width)),
+        ],
         [
             pltpu.VMEM((mesh_slots, width), F32),
             pltpu.VMEM((number, width), F32),
@@ -665,7 +755,7 @@
             pltpu.VMEM((number + 8, mesh_slots), F32),
             pltpu.VMEM((mesh_slots, mesh_slots), F32),
         ],
-        [sender_high, sender_low, output_high, output_low],
+        [merged_high, merged_low, second_high, biases],
     )
     (out,) = call(
         refine_kernel,
@@ -675,10 +765,6 @@
         [],
         [mesh_in, *first],
         [
-            second_high,
-            second_low,
-            match,
-            self_near,
             refine_high,
             refine_low,
             normed,

time: 54.5 us -> 53.8 us (0.987)
  Pallas kernels: 32.4 us -> 30.9 us
  waiting for transfers between devices: 11.1 us -> 12 us
    pallas_call x5, Pallas kernels: 32.4 us -> 30.9 us  [call(): pl.pallas_call(kernel, out_shape=[pltpu.VMEM(array.shape, array.dtype) fo...]
    all_to_all x2, waiting for transfers between devices: 11.1 us -> 12 us  [exchange(): lax.all_to_all(blocks, ('lat', 'lon'), split_axis=0, concat_axis=0, tiled...]
  transfers between devices with their start and end apart: 2 -> 2, of which waited for: 2 -> 2; matrix products, arithmetic and copies ran while one was open for 0% -> 0% of each run, Pallas kernels for 39% -> 38%
where the time goes in v4:
time: 53.8 us; the launch traced here: 53.4 us
  Pallas kernels  30.9 us (57%)
  waiting for transfers between devices  12 us (22%)
  starting transfers between devices  10.1 us (19%)
    pallas_call x5, Pallas kernels, call(): pl.pallas_call(kernel, out_shape=[pltpu.VMEM(array.shape, array.dtype) fo...  30.9 us
    all_to_all x2, waiting for transfers between devices, exchange(): lax.all_to_all(blocks, ('lat', 'lon'), split_axis=0, concat_axis=0, tiled...  12 us
    all_to_all x2, starting transfers between devices, exchange(): lax.all_to_all(blocks, ('lat', 'lon'), split_axis=0, concat_axis=0, tiled...  10.1 us
  transfers between devices with their start and end apart: 2, of which 2 were waited for; matrix products, arithmetic and copies ran while one was open for 0% of the time, Pallas kernels for 38%

profile of v4, /device:TPU:0, one launch (start us, length us, event | category | flops | bytes accessed | tf_op | source)
XLA Modules:
  0.0 53.4 jit_solution(6833168720141468466)
XLA Ops:
  0.0 0.0 copy-start
  0.0 0.0 copy-start.1
  0.0 0.0 copy-start.2
  0.0 0.0 copy-start.3
  0.0 0.0 copy-start.4
  0.0 0.0 copy-start.5
  0.0 0.0 copy-start.6
  0.0 0.0 copy-start.7
  0.0 0.0 copy-start.8
  0.1 0.0 copy-start.9
  0.1 3.0 %pack.1 = f32[256,512]{1,0:T(8,128)} custom-call(s32[8,32]{1,0:T(8,128)} %bitcast.37, f32[720,512]{1,0:T(8,128)} %bitcast.35), custom_call_target="tpu_custom_call" | custom-call | flops 1000 | bytes 4194304 | tf_op jit(solution)/shard_map/pack/pallas_call | solution.py:556
  3.1 7.3 %all-to-all-start = ((f32[32,8,512]{2,1,0:T(8,128)}), f32[32,8,512]{2,1,0:T(8,128)S(1)}, u32[]{:S(2)}, u32[]{:S(2)}) async-start(f32[32,8,512]{2,1,0:T(8,128)} %bitcast.34), calls=%async_computation | async-start | bytes 1048576 | tf_op jit(solution)/shard_map/all_to_all | solution.py:576
  10.4 0.0 copy-done
  10.4 0.0 copy-done.1
  10.4 0.0 copy-done.2
  10.5 0.0 copy-done.3
  10.5 0.0 copy-done.4
  10.5 0.0 copy-done.5
  10.5 0.0 copy-done.6
  10.5 0.0 copy-done.7
  10.5 0.0 copy-done.8
  10.5 0.0 copy-done.9
  10.5 11.1 %before.1 = (bf16[512,512]{1,0:T(8,128)(2,1)S(1)}, bf16[512,512]{1,0:T(8,128)(2,1)S(1)}, bf16[512,512]{1,0:T(8,128)(2,1)S(1)}, bf16[512,512]{1,0:T(8,128)(2,1)S(...) custom-call(s32[1,256]{1,0:T(1,128)S(1)} %copy-done.3, ...), custom_call_target="tpu_custom_call" | custom-call | flops 1409286144 | bytes 4194304 | tf_op jit(solution)/shard_map/before/pallas_call | solution.py:556
  21.6 5.0 %all-to-all-done = f32[32,8,512]{2,1,0:T(8,128)S(1)} async-done(((f32[32,8,512]{2,1,0:T(8,128)}), f32[32,8,512]{2,1,0:T(8,128)S(1)}, u32[]{:S(2)}, u32[]{:S(2)}) %all-to-all-start) | async-done | bytes 524320 | tf_op jit(solution)/shard_map/all_to_all | solution.py:576
  26.7 0.0 copy-start.10
  26.7 0.0 copy-start.11
  26.7 0.0 copy-start.12
  26.7 0.0 copy-start.13
  26.7 0.0 copy-start.14
  26.7 4.0 %encode.1 = (f32[256,512]{1,0:T(8,128)}, f32[256,512]{1,0:T(8,128)}) custom-call(f32[256,512]{1,0:T(8,128)S(1)} %bitcast.21, bf16[512,512]{1,0:T(8,128)(2,1)S(1)} %get-tuple-element.38.sender_high, bf16[512,512]{1,0:T(8,128)(2,1)S(1)} %get-tuple-element.39.sender_low, bf16[512,512]{1,0:T(8,128)(2,1)S(1)} %get-tuple-element.40.merged_high, ...), custom_call_target="tpu_custom_call" | custom-call | flops 1610612736 | bytes 4194304 | tf_op jit(solution)/shard_map/encode/pallas_call | solution.py:556
  30.7 2.8 %all-to-all-start.1 = ((f32[32,8,512]{2,1,0:T(8,128)}), f32[32,8,512]{2,1,0:T(8,128)S(1)}, u32[]{:S(2)}, u32[]{:S(2)}) async-start(f32[32,8,512]{2,1,0:T(8,128)} %bitcast.36), calls=%async_computation.1 | async-start | bytes 1048576 | tf_op jit(solution)/shard_map/all_to_all | solution.py:576
  33.5 0.0 copy-done.10
  33.6 0.0 copy-done.11
  33.6 0.0 copy-done.12
  33.6 0.0 copy-done.13
  33.6 0.0 copy-done.14
  33.6 9.1 %between.1 = (bf16[512,512]{1,0:T(8,128)(2,1)S(1)}, bf16[512,512]{1,0:T(8,128)(2,1)S(1)}, bf16[512,512]{1,0:T(8,128)(2,1)S(1)}, f32[256,512]{1,0:T(8,128)S(1)}, ...) custom-call(s32[1,256]{1,0:T(1,128)S(1)} %copy-done.14, ...), custom_call_target="tpu_custom_call" | custom-call | flops 3422552064 | bytes 4194304 | tf_op jit(solution)/shard_map/between/pallas_call | solution.py:556
  42.7 6.9 %all-to-all-done.1 = f32[32,8,512]{2,1,0:T(8,128)S(1)} async-done(((f32[32,8,512]{2,1,0:T(8,128)}), f32[32,8,512]{2,1,0:T(8,128)S(1)}, u32[]{:S(2)}, u32[]{:S(2)}) %all-to-all-start.1) | async-done | bytes 524320 | tf_op jit(solution)/shard_map/all_to_all | solution.py:576
  49.6 3.7 %refine.1 = f32[640,512]{1,0:T(8,128)} custom-call(f32[256,512]{1,0:T(8,128)S(1)} %bitcast.22, bf16[512,512]{1,0:T(8,128)(2,1)S(1)} %get-tuple-element.61.merged_high, bf16[512,512]{1,0:T(8,128)(2,1)S(1)} %get-tuple-element.62.merged_low, bf16[512,512]{1,0:T(8,128)(2,1)S(1)} %get-tuple-element.63.output_high, f32[256,512]{1,0:T(8,128)S(1)} %get-tuple-element.64.received, ...), custom_call_target="tpu_custom_call" | custom-call | flops 1610612736 | bytes 4194304 | tf_op jit(solution)/shard_map/refine/pallas_call | solution.py:556
Async XLA Ops:
  0.0 10.4 %copy-start = (f32[4,512]{1,0:T(4,128)S(1)}, f32[4,512]{1,0:T(4,128)}, u32[]{:S(2)}) copy-start(f32[4,512]{1,0:T(4,128)} %weight_geometry.2) | copy-start | bytes 24580
  0.0 10.4 %copy-start.1 = (s32[1,32,8]{1,2,0:T(8,128)S(1)}, s32[1,32,8]{1,2,0:T(8,128)}, u32[]{:S(2)}) copy-start(s32[1,32,8]{1,2,0:T(8,128)} %param.35) | copy-start | bytes 3076
  0.0 10.4 %copy-start.2 = (f32[4,1,256]{2,1,0:T(1,128)S(1)}, f32[4,1,256]{2,1,0:T(1,128)}, u32[]{:S(2)}) copy-start(f32[4,1,256]{2,1,0:T(1,128)} %geometry.2) | copy-start | bytes 12292
  0.0 10.4 %copy-start.3 = (s32[1,256]{1,0:T(1,128)S(1)}, s32[1,256]{1,0:T(1,128)}, u32[]{:S(2)}) copy-start(s32[1,256]{1,0:T(1,128)} %grid_targets.3) | copy-start | bytes 3076
  0.0 10.5 %copy-start.4 = (f32[512]{0:T(512)S(1)}, f32[512]{0:T(512)}, u32[]{:S(2)}) copy-start(f32[512]{0:T(512)} %param.41) | copy-start | bytes 6148
  0.0 10.5 %copy-start.5 = (f32[512]{0:T(512)S(1)}, f32[512]{0:T(512)}, u32[]{:S(2)}) copy-start(f32[512]{0:T(512)} %param.46) | copy-start | bytes 6148
  0.0 10.5 %copy-start.6 = (f32[512]{0:T(512)S(1)}, f32[512]{0:T(512)}, u32[]{:S(2)}) copy-start(f32[512]{0:T(512)} %param.43) | copy-start | bytes 6148
  0.0 10.5 %copy-start.7 = (f32[512]{0:T(512)S(1)}, f32[512]{0:T(512)}, u32[]{:S(2)}) copy-start(f32[512]{0:T(512)} %param.54) | copy-start | bytes 6148
  0.0 10.5 %copy-start.8 = (f32[512]{0:T(512)S(1)}, f32[512]{0:T(512)}, u32[]{:S(2)}) copy-start(f32[512]{0:T(512)} %param.48) | copy-start | bytes 6148
  0.1 10.5 %copy-start.9 = (f32[512]{0:T(512)S(1)}, f32[512]{0:T(512)}, u32[]{:S(2)}) copy-start(f32[512]{0:T(512)} %param.59) | copy-start | bytes 6148
  3.1 23.6 %all-to-all-start = ((f32[32,8,512]{2,1,0:T(8,128)}), f32[32,8,512]{2,1,0:T(8,128)S(1)}, u32[]{:S(2)}, u32[]{:S(2)}) async-start(f32[32,8,512]{2,1,0:T(8,128)} %bitcast.34), calls=%async_computation | async-start | bytes 1048576 | tf_op jit(solution)/shard_map/all_to_all | solution.py:576
  26.7 6.9 %copy-start.10 = (f32[4,512]{1,0:T(4,128)S(1)}, f32[4,512]{1,0:T(4,128)}, u32[]{:S(2)}) copy-start(f32[4,512]{1,0:T(4,128)} %weight_geometry.3) | copy-start | bytes 24580
  26.7 6.9 %copy-start.11 = (f32[4,1,256]{2,1,0:T(1,128)S(1)}, f32[4,1,256]{2,1,0:T(1,128)}, u32[]{:S(2)}) copy-start(f32[4,1,256]{2,1,0:T(1,128)} %geometry.3) | copy-start | bytes 12292
  26.7 6.9 %copy-start.12 = (f32[512]{0:T(512)S(1)}, f32[512]{0:T(512)}, u32[]{:S(2)}) copy-start(f32[512]{0:T(512)} %param.52) | copy-start | bytes 6148
  26.7 6.9 %copy-start.13 = (f32[512]{0:T(512)S(1)}, f32[512]{0:T(512)}, u32[]{:S(2)}) copy-start(f32[512]{0:T(512)} %param.57) | copy-start | bytes 6148
  26.7 6.9 %copy-start.14 = (s32[1,256]{1,0:T(1,128)S(1)}, s32[1,256]{1,0:T(1,128)}, u32[]{:S(2)}) copy-start(s32[1,256]{1,0:T(1,128)} %mesh_targets.1) | copy-start | bytes 3076
  30.7 18.9 %all-to-all-start.1 = ((f32[32,8,512]{2,1,0:T(8,128)}), f32[32,8,512]{2,1,0:T(8,128)S(1)}, u32[]{:S(2)}, u32[]{:S(2)}) async-start(f32[32,8,512]{2,1,0:T(8,128)} %bitcast.36), calls=%async_computation.1 | async-start | bytes 1048576 | tf_op jit(solution)/shard_map/all_to_all | solution.py:576

commit v5 on v4

--- a/solution.py
+++ b/solution.py
@@ -303,12 +303,13 @@
     wait(*stores)
 
 
-def edges(hidden, merged_high, merged_low, output_high, bias, bias_on):
+def edges(hidden, merged_high, merged_low, output_high, bias, bias_on, loads=()):
     hidden_high, hidden_low = split(hidden)
     high = merged_high[...]
     total = dot(hidden_high, high) + (
         dot(hidden_low, high) + dot(hidden_high, merged_low[...])
     )
+    wait(*loads)
     return (total + bias_on) * scale(dot(hidden_high, output_high[...]) + bias)
 
 
@@ -350,9 +351,8 @@
     load_nodes = copies.start(nodes_sent_ref, nodes_sent)
     started()
     hidden = silu(dot3(arrived[...], sender_high[...], sender_low[...]) + received[...])
-    wait(load_output)
     part = edges(
-        hidden, merged_high, merged_low, output_high, biases[0:1, :], biases[1:2, :]
+        hidden, merged_high, merged_low, output_high, biases[0:1, :], biases[1:2, :], [load_output]
     )
     parts[...] = part
     store_parts = copies.start(parts, parts_ref)
@@ -524,10 +524,10 @@
         biases[1:2, :],
     )
     hidden = silu(self_near[...] + pick(match[...], part))
-    wait(load_refine_high, load_refine_low, load_normed)
+    wait(load_refine_high, load_refine_low)
     change = norm_centred(dot3(hidden, refine_high[...], refine_low[...]) + biases[2:3, :])
+    wait(load_normed, load_firsts, load_base)
     high, low = split(change - normed[...])
-    wait(load_firsts, load_base)
     number = out.shape[0]
     chunk = number // 2
     stores = []
@@ -535,8 +535,6 @@
         at = pl.ds(first, chunk)
         out[at, :] = base[at, :] + (dot(firsts[at, :], high) + dot(firsts[at, :], low))
         stores.append(copies.start(out.at[at], out_ref.at[at]))
-        if first + chunk < number:
-            started()
     wait(*stores)
 
 

time: 53.8 us -> 53.2 us (0.989)
  Pallas kernels: 30.9 us -> 30.3 us
    pallas_call x5, Pallas kernels: 30.9 us -> 30.3 us  [call(): pl.pallas_call(kernel, out_shape=[pltpu.VMEM(array.shape, array.dtype) fo...]
where the time goes in v5:
time: 53.2 us; the launch traced here: 52.8 us
  Pallas kernels  30.3 us (57%)
  waiting for transfers between devices  12 us (23%)
  starting transfers between devices  10.1 us (19%)
    pallas_call x5, Pallas kernels, call(): pl.pallas_call(kernel, out_shape=[pltpu.VMEM(array.shape, array.dtype) fo...  30.3 us
    all_to_all x2, waiting for transfers between devices, exchange(): lax.all_to_all(blocks, ('lat', 'lon'), split_axis=0, concat_axis=0, tiled...  12 us
    all_to_all x2, starting transfers between devices, exchange(): lax.all_to_all(blocks, ('lat', 'lon'), split_axis=0, concat_axis=0, tiled...  10.1 us
  transfers between devices with their start and end apart: 2, of which 2 were waited for; matrix products, arithmetic and copies ran while one was open for 0% of the time, Pallas kernels for 38%

profile of v5, /device:TPU:0, one launch (start us, length us, event | category | flops | bytes accessed | tf_op | source)
XLA Modules:
  0.0 52.8 jit_solution(18011059911363560071)
XLA Ops:
  0.0 0.0 copy-start
  0.0 0.0 copy-start.1
  0.0 0.0 copy-start.2
  0.0 0.0 copy-start.3
  0.0 0.0 copy-start.4
  0.0 0.0 copy-start.5
  0.0 0.0 copy-start.6
  0.0 0.0 copy-start.7
  0.0 0.0 copy-start.8
  0.1 0.0 copy-start.9
  0.1 3.0 %pack.1 = f32[256,512]{1,0:T(8,128)} custom-call(s32[8,32]{1,0:T(8,128)} %bitcast.37, f32[720,512]{1,0:T(8,128)} %bitcast.35), custom_call_target="tpu_custom_call" | custom-call | flops 1000 | bytes 4194304 | tf_op jit(solution)/shard_map/pack/pallas_call | solution.py:554
  3.1 7.3 %all-to-all-start = ((f32[32,8,512]{2,1,0:T(8,128)}), f32[32,8,512]{2,1,0:T(8,128)S(1)}, u32[]{:S(2)}, u32[]{:S(2)}) async-start(f32[32,8,512]{2,1,0:T(8,128)} %bitcast.34), calls=%async_computation | async-start | bytes 1048576 | tf_op jit(solution)/shard_map/all_to_all | solution.py:574
  10.4 0.0 copy-done
  10.4 0.0 copy-done.1
  10.4 0.0 copy-done.2
  10.5 0.0 copy-done.3
  10.5 0.0 copy-done.4
  10.5 0.0 copy-done.5
  10.5 0.0 copy-done.6
  10.5 0.0 copy-done.7
  10.5 0.0 copy-done.8
  10.5 0.0 copy-done.9
  10.5 11.1 %before.1 = (bf16[512,512]{1,0:T(8,128)(2,1)S(1)}, bf16[512,512]{1,0:T(8,128)(2,1)S(1)}, bf16[512,512]{1,0:T(8,128)(2,1)S(1)}, bf16[512,512]{1,0:T(8,128)(2,1)S(...) custom-call(s32[1,256]{1,0:T(1,128)S(1)} %copy-done.3, ...), custom_call_target="tpu_custom_call" | custom-call | flops 1409286144 | bytes 4194304 | tf_op jit(solution)/shard_map/before/pallas_call | solution.py:554
  21.6 5.0 %all-to-all-done = f32[32,8,512]{2,1,0:T(8,128)S(1)} async-done(((f32[32,8,512]{2,1,0:T(8,128)}), f32[32,8,512]{2,1,0:T(8,128)S(1)}, u32[]{:S(2)}, u32[]{:S(2)}) %all-to-all-start) | async-done | bytes 524320 | tf_op jit(solution)/shard_map/all_to_all | solution.py:574
  26.7 0.0 copy-start.10
  26.7 0.0 copy-start.11
  26.7 0.0 copy-start.12
  26.7 0.0 copy-start.13
  26.7 0.0 copy-start.14
  26.7 3.7 %encode.1 = (f32[256,512]{1,0:T(8,128)}, f32[256,512]{1,0:T(8,128)}) custom-call(f32[256,512]{1,0:T(8,128)S(1)} %bitcast.21, bf16[512,512]{1,0:T(8,128)(2,1)S(1)} %get-tuple-element.38.sender_high, bf16[512,512]{1,0:T(8,128)(2,1)S(1)} %get-tuple-element.39.sender_low, bf16[512,512]{1,0:T(8,128)(2,1)S(1)} %get-tuple-element.40.merged_high, ...), custom_call_target="tpu_custom_call" | custom-call | flops 1610612736 | bytes 4194304 | tf_op jit(solution)/shard_map/encode/pallas_call | solution.py:554
  30.4 2.8 %all-to-all-start.1 = ((f32[32,8,512]{2,1,0:T(8,128)}), f32[32,8,512]{2,1,0:T(8,128)S(1)}, u32[]{:S(2)}, u32[]{:S(2)}) async-start(f32[32,8,512]{2,1,0:T(8,128)} %bitcast.36), calls=%async_computation.1 | async-start | bytes 1048576 | tf_op jit(solution)/shard_map/all_to_all | solution.py:574
  33.2 0.0 copy-done.10
  33.2 0.0 copy-done.11
  33.2 0.0 copy-done.12
  33.2 0.0 copy-done.13
  33.2 0.0 copy-done.14
  33.2 9.1 %between.1 = (bf16[512,512]{1,0:T(8,128)(2,1)S(1)}, bf16[512,512]{1,0:T(8,128)(2,1)S(1)}, bf16[512,512]{1,0:T(8,128)(2,1)S(1)}, f32[256,512]{1,0:T(8,128)S(1)}, ...) custom-call(s32[1,256]{1,0:T(1,128)S(1)} %copy-done.14, ...), custom_call_target="tpu_custom_call" | custom-call | flops 3422552064 | bytes 4194304 | tf_op jit(solution)/shard_map/between/pallas_call | solution.py:554
  42.3 6.9 %all-to-all-done.1 = f32[32,8,512]{2,1,0:T(8,128)S(1)} async-done(((f32[32,8,512]{2,1,0:T(8,128)}), f32[32,8,512]{2,1,0:T(8,128)S(1)}, u32[]{:S(2)}, u32[]{:S(2)}) %all-to-all-start.1) | async-done | bytes 524320 | tf_op jit(solution)/shard_map/all_to_all | solution.py:574
  49.2 3.4 %refine.1 = f32[640,512]{1,0:T(8,128)} custom-call(f32[256,512]{1,0:T(8,128)S(1)} %bitcast.22, bf16[512,512]{1,0:T(8,128)(2,1)S(1)} %get-tuple-element.61.merged_high, bf16[512,512]{1,0:T(8,128)(2,1)S(1)} %get-tuple-element.62.merged_low, bf16[512,512]{1,0:T(8,128)(2,1)S(1)} %get-tuple-element.63.output_high, f32[256,512]{1,0:T(8,128)S(1)} %get-tuple-element.64.received, ...), custom_call_target="tpu_custom_call" | custom-call | flops 1610612736 | bytes 4194304 | tf_op jit(solution)/shard_map/refine/pallas_call | solution.py:554
Async XLA Ops:
  0.0 10.4 %copy-start = (f32[4,512]{1,0:T(4,128)S(1)}, f32[4,512]{1,0:T(4,128)}, u32[]{:S(2)}) copy-start(f32[4,512]{1,0:T(4,128)} %weight_geometry.2) | copy-start | bytes 24580
  0.0 10.4 %copy-start.1 = (s32[1,32,8]{1,2,0:T(8,128)S(1)}, s32[1,32,8]{1,2,0:T(8,128)}, u32[]{:S(2)}) copy-start(s32[1,32,8]{1,2,0:T(8,128)} %param.35) | copy-start | bytes 3076
  0.0 10.4 %copy-start.2 = (f32[4,1,256]{2,1,0:T(1,128)S(1)}, f32[4,1,256]{2,1,0:T(1,128)}, u32[]{:S(2)}) copy-start(f32[4,1,256]{2,1,0:T(1,128)} %geometry.2) | copy-start | bytes 12292
  0.0 10.4 %copy-start.3 = (s32[1,256]{1,0:T(1,128)S(1)}, s32[1,256]{1,0:T(1,128)}, u32[]{:S(2)}) copy-start(s32[1,256]{1,0:T(1,128)} %grid_targets.3) | copy-start | bytes 3076
  0.0 10.5 %copy-start.4 = (f32[512]{0:T(512)S(1)}, f32[512]{0:T(512)}, u32[]{:S(2)}) copy-start(f32[512]{0:T(512)} %param.41) | copy-start | bytes 6148
  0.0 10.5 %copy-start.5 = (f32[512]{0:T(512)S(1)}, f32[512]{0:T(512)}, u32[]{:S(2)}) copy-start(f32[512]{0:T(512)} %param.46) | copy-start | bytes 6148
  0.0 10.5 %copy-start.6 = (f32[512]{0:T(512)S(1)}, f32[512]{0:T(512)}, u32[]{:S(2)}) copy-start(f32[512]{0:T(512)} %param.43) | copy-start | bytes 6148
  0.0 10.5 %copy-start.7 = (f32[512]{0:T(512)S(1)}, f32[512]{0:T(512)}, u32[]{:S(2)}) copy-start(f32[512]{0:T(512)} %param.54) | copy-start | bytes 6148
  0.0 10.5 %copy-start.8 = (f32[512]{0:T(512)S(1)}, f32[512]{0:T(512)}, u32[]{:S(2)}) copy-start(f32[512]{0:T(512)} %param.48) | copy-start | bytes 6148
  0.1 10.5 %copy-start.9 = (f32[512]{0:T(512)S(1)}, f32[512]{0:T(512)}, u32[]{:S(2)}) copy-start(f32[512]{0:T(512)} %param.59) | copy-start | bytes 6148
  3.1 23.6 %all-to-all-start = ((f32[32,8,512]{2,1,0:T(8,128)}), f32[32,8,512]{2,1,0:T(8,128)S(1)}, u32[]{:S(2)}, u32[]{:S(2)}) async-start(f32[32,8,512]{2,1,0:T(8,128)} %bitcast.34), calls=%async_computation | async-start | bytes 1048576 | tf_op jit(solution)/shard_map/all_to_all | solution.py:574
  26.7 6.5 %copy-start.10 = (f32[4,512]{1,0:T(4,128)S(1)}, f32[4,512]{1,0:T(4,128)}, u32[]{:S(2)}) copy-start(f32[4,512]{1,0:T(4,128)} %weight_geometry.3) | copy-start | bytes 24580
  26.7 6.5 %copy-start.11 = (f32[4,1,256]{2,1,0:T(1,128)S(1)}, f32[4,1,256]{2,1,0:T(1,128)}, u32[]{:S(2)}) copy-start(f32[4,1,256]{2,1,0:T(1,128)} %geometry.3) | copy-start | bytes 12292
  26.7 6.5 %copy-start.12 = (f32[512]{0:T(512)S(1)}, f32[512]{0:T(512)}, u32[]{:S(2)}) copy-start(f32[512]{0:T(512)} %param.52) | copy-start | bytes 6148
  26.7 6.5 %copy-start.13 = (f32[512]{0:T(512)S(1)}, f32[512]{0:T(512)}, u32[]{:S(2)}) copy-start(f32[512]{0:T(512)} %param.57) | copy-start | bytes 6148
  26.7 6.5 %copy-start.14 = (s32[1,256]{1,0:T(1,128)S(1)}, s32[1,256]{1,0:T(1,128)}, u32[]{:S(2)}) copy-start(s32[1,256]{1,0:T(1,128)} %mesh_targets.1) | copy-start | bytes 3076
  30.4 18.9 %all-to-all-start.1 = ((f32[32,8,512]{2,1,0:T(8,128)}), f32[32,8,512]{2,1,0:T(8,128)S(1)}, u32[]{:S(2)}, u32[]{:S(2)}) async-start(f32[32,8,512]{2,1,0:T(8,128)} %bitcast.36), calls=%async_computation.1 | async-start | bytes 1048576 | tf_op jit(solution)/shard_map/all_to_all | solution.py:574

commit v6 on v5

--- a/solution.py
+++ b/solution.py
@@ -111,29 +111,35 @@
 
 
 def pack_kernel(
-    rows_in, columns_in, senders_ref, cells_ref, out_ref, cells, out, senders, semaphores
+    rows_in,
+    columns_in,
+    senders_ref,
+    cells_ref,
+    out_ref,
+    cells,
+    out,
+    senders,
+    senders_s,
+    semaphores,
 ):
     copies = Copies(semaphores)
     load_senders = copies.start(senders_ref, senders)
-    load = copies.start(cells_ref, cells)
+    load_cells = copies.start(cells_ref, cells)
     shift = 20
     factor = -(-(1 << shift) // columns_in)
     assert all((i * factor) >> shift == i // columns_in for i in range(rows_in * columns_in))
-    order = slot_order(senders)
-
-    def row_of(i):
-        cell = order(i)
-        row = (cell * factor) >> shift
-        return (cell - row * columns_in) * rows_in + row
-
-    wait(load_senders, load)
-    chunk = out.shape[0] // 4
+    wait(load_senders)
+    cell = senders[...]
+    row = (cell * factor) >> shift
+    senders[...] = (cell - row * columns_in) * rows_in + row
+    wait(copies.start(senders, senders_s), load_cells)
+    chunk = out.shape[0] // 2
     stores = []
     for first in range(0, out.shape[0], chunk):
-        gather_rows(first, chunk, row_of, [(cells, out)])
-        stores.append(
-            copies.start(out.at[pl.ds(first, chunk)], out_ref.at[pl.ds(first, chunk)])
-        )
+        gather_rows(first, chunk, slot_order(senders_s), [(cells, out)])
+        at = pl.ds(first, chunk)
+        stores.append(copies.start(out.at[at], out_ref.at[at]))
+        started()
     wait(*stores)
 
 
@@ -626,7 +632,10 @@
         [],
         [cells],
         [flat((grid_slots, width))],
-        scratch=[pltpu.SMEM((grid_slots // patches, patches), jnp.int32)],
+        scratch=[
+            pltpu.VMEM((grid_slots // patches, patches), jnp.int32),
+            pltpu.SMEM((grid_slots // patches, patches), jnp.int32),
+        ],
         direct=[grid_senders[0].T],
     )
     grid_in = exchange(packed, patches)

time: 53.2 us -> 52.9 us (level)
  no operation moved by 1% of the time
where the time goes in v6:
time: 52.9 us; the launch traced here: 52.5 us
  Pallas kernels  30 us (57%)
  waiting for transfers between devices  12 us (23%)
  starting transfers between devices  10.1 us (19%)
    pallas_call x5, Pallas kernels, call(): pl.pallas_call(kernel, out_shape=[pltpu.VMEM(array.shape, array.dtype) fo...  30 us
    all_to_all x2, waiting for transfers between devices, exchange(): lax.all_to_all(blocks, ('lat', 'lon'), split_axis=0, concat_axis=0, tiled...  12 us
    all_to_all x2, starting transfers between devices, exchange(): lax.all_to_all(blocks, ('lat', 'lon'), split_axis=0, concat_axis=0, tiled...  10.1 us
  transfers between devices with their start and end apart: 2, of which 2 were waited for; matrix products, arithmetic and copies ran while one was open for 0% of the time, Pallas kernels for 38%

profile of v6, /device:TPU:0, one launch (start us, length us, event | category | flops | bytes accessed | tf_op | source)
XLA Modules:
  0.0 52.5 jit_solution(8833329868120218365)
XLA Ops:
  0.0 0.0 copy-start
  0.0 0.0 copy-start.1
  0.0 0.0 copy-start.2
  0.0 0.0 copy-start.3
  0.0 0.0 copy-start.4
  0.0 0.0 copy-start.5
  0.0 0.0 copy-start.6
  0.0 0.0 copy-start.7
  0.0 0.0 copy-start.8
  0.1 0.0 copy-start.9
  0.1 2.7 %pack.1 = f32[256,512]{1,0:T(8,128)} custom-call(s32[8,32]{1,0:T(8,128)} %bitcast.37, f32[720,512]{1,0:T(8,128)} %bitcast.35), custom_call_target="tpu_custom_call" | custom-call | flops 1000 | bytes 4194304 | tf_op jit(solution)/shard_map/pack/pallas_call | solution.py:560
  2.8 7.3 %all-to-all-start = ((f32[32,8,512]{2,1,0:T(8,128)}), f32[32,8,512]{2,1,0:T(8,128)S(1)}, u32[]{:S(2)}, u32[]{:S(2)}) async-start(f32[32,8,512]{2,1,0:T(8,128)} %bitcast.34), calls=%async_computation | async-start | bytes 1048576 | tf_op jit(solution)/shard_map/all_to_all | solution.py:580
  10.1 0.0 copy-done
  10.1 0.0 copy-done.1
  10.1 0.0 copy-done.2
  10.1 0.0 copy-done.3
  10.2 0.0 copy-done.4
  10.2 0.0 copy-done.5
  10.2 0.0 copy-done.6
  10.2 0.0 copy-done.7
  10.2 0.0 copy-done.8
  10.2 0.0 copy-done.9
  10.2 11.1 %before.1 = (bf16[512,512]{1,0:T(8,128)(2,1)S(1)}, bf16[512,512]{1,0:T(8,128)(2,1)S(1)}, bf16[512,512]{1,0:T(8,128)(2,1)S(1)}, bf16[512,512]{1,0:T(8,128)(2,1)S(...) custom-call(s32[1,256]{1,0:T(1,128)S(1)} %copy-done.3, ...), custom_call_target="tpu_custom_call" | custom-call | flops 1409286144 | bytes 4194304 | tf_op jit(solution)/shard_map/before/pallas_call | solution.py:560
  21.3 5.0 %all-to-all-done = f32[32,8,512]{2,1,0:T(8,128)S(1)} async-done(((f32[32,8,512]{2,1,0:T(8,128)}), f32[32,8,512]{2,1,0:T(8,128)S(1)}, u32[]{:S(2)}, u32[]{:S(2)}) %all-to-all-start) | async-done | bytes 524320 | tf_op jit(solution)/shard_map/all_to_all | solution.py:580
  26.3 0.0 copy-start.10
  26.3 0.0 copy-start.11
  26.3 0.0 copy-start.12
  26.4 0.0 copy-start.13
  26.4 0.0 copy-start.14
  26.4 3.7 %encode.1 = (f32[256,512]{1,0:T(8,128)}, f32[256,512]{1,0:T(8,128)}) custom-call(f32[256,512]{1,0:T(8,128)S(1)} %bitcast.21, bf16[512,512]{1,0:T(8,128)(2,1)S(1)} %get-tuple-element.38.sender_high, bf16[512,512]{1,0:T(8,128)(2,1)S(1)} %get-tuple-element.39.sender_low, bf16[512,512]{1,0:T(8,128)(2,1)S(1)} %get-tuple-element.40.merged_high, ...), custom_call_target="tpu_custom_call" | custom-call | flops 1610612736 | bytes 4194304 | tf_op jit(solution)/shard_map/encode/pallas_call | solution.py:560
  30.0 2.8 %all-to-all-start.1 = ((f32[32,8,512]{2,1,0:T(8,128)}), f32[32,8,512]{2,1,0:T(8,128)S(1)}, u32[]{:S(2)}, u32[]{:S(2)}) async-start(f32[32,8,512]{2,1,0:T(8,128)} %bitcast.36), calls=%async_computation.1 | async-start | bytes 1048576 | tf_op jit(solution)/shard_map/all_to_all | solution.py:580
  32.9 0.0 copy-done.10
  32.9 0.0 copy-done.11
  32.9 0.0 copy-done.12
  32.9 0.0 copy-done.13
  32.9 0.0 copy-done.14
  32.9 9.1 %between.1 = (bf16[512,512]{1,0:T(8,128)(2,1)S(1)}, bf16[512,512]{1,0:T(8,128)(2,1)S(1)}, bf16[512,512]{1,0:T(8,128)(2,1)S(1)}, f32[256,512]{1,0:T(8,128)S(1)}, ...) custom-call(s32[1,256]{1,0:T(1,128)S(1)} %copy-done.14, ...), custom_call_target="tpu_custom_call" | custom-call | flops 3422552064 | bytes 4194304 | tf_op jit(solution)/shard_map/between/pallas_call | solution.py:560
  42.0 6.9 %all-to-all-done.1 = f32[32,8,512]{2,1,0:T(8,128)S(1)} async-done(((f32[32,8,512]{2,1,0:T(8,128)}), f32[32,8,512]{2,1,0:T(8,128)S(1)}, u32[]{:S(2)}, u32[]{:S(2)}) %all-to-all-start.1) | async-done | bytes 524320 | tf_op jit(solution)/shard_map/all_to_all | solution.py:580
  48.9 3.4 %refine.1 = f32[640,512]{1,0:T(8,128)} custom-call(f32[256,512]{1,0:T(8,128)S(1)} %bitcast.22, bf16[512,512]{1,0:T(8,128)(2,1)S(1)} %get-tuple-element.61.merged_high, bf16[512,512]{1,0:T(8,128)(2,1)S(1)} %get-tuple-element.62.merged_low, bf16[512,512]{1,0:T(8,128)(2,1)S(1)} %get-tuple-element.63.output_high, f32[256,512]{1,0:T(8,128)S(1)} %get-tuple-element.64.received, ...), custom_call_target="tpu_custom_call" | custom-call | flops 1610612736 | bytes 4194304 | tf_op jit(solution)/shard_map/refine/pallas_call | solution.py:560
Async XLA Ops:
  0.0 10.1 %copy-start = (f32[4,512]{1,0:T(4,128)S(1)}, f32[4,512]{1,0:T(4,128)}, u32[]{:S(2)}) copy-start(f32[4,512]{1,0:T(4,128)} %weight_geometry.2) | copy-start | bytes 24580
  0.0 10.1 %copy-start.1 = (s32[1,32,8]{1,2,0:T(8,128)S(1)}, s32[1,32,8]{1,2,0:T(8,128)}, u32[]{:S(2)}) copy-start(s32[1,32,8]{1,2,0:T(8,128)} %param.35) | copy-start | bytes 3076
  0.0 10.1 %copy-start.2 = (f32[4,1,256]{2,1,0:T(1,128)S(1)}, f32[4,1,256]{2,1,0:T(1,128)}, u32[]{:S(2)}) copy-start(f32[4,1,256]{2,1,0:T(1,128)} %geometry.2) | copy-start | bytes 12292
  0.0 10.1 %copy-start.3 = (s32[1,256]{1,0:T(1,128)S(1)}, s32[1,256]{1,0:T(1,128)}, u32[]{:S(2)}) copy-start(s32[1,256]{1,0:T(1,128)} %grid_targets.3) | copy-start | bytes 3076
  0.0 10.1 %copy-start.4 = (f32[512]{0:T(512)S(1)}, f32[512]{0:T(512)}, u32[]{:S(2)}) copy-start(f32[512]{0:T(512)} %param.41) | copy-start | bytes 6148
  0.0 10.1 %copy-start.5 = (f32[512]{0:T(512)S(1)}, f32[512]{0:T(512)}, u32[]{:S(2)}) copy-start(f32[512]{0:T(512)} %param.46) | copy-start | bytes 6148
  0.0 10.1 %copy-start.6 = (f32[512]{0:T(512)S(1)}, f32[512]{0:T(512)}, u32[]{:S(2)}) copy-start(f32[512]{0:T(512)} %param.43) | copy-start | bytes 6148
  0.0 10.1 %copy-start.7 = (f32[512]{0:T(512)S(1)}, f32[512]{0:T(512)}, u32[]{:S(2)}) copy-start(f32[512]{0:T(512)} %param.54) | copy-start | bytes 6148
  0.0 10.1 %copy-start.8 = (f32[512]{0:T(512)S(1)}, f32[512]{0:T(512)}, u32[]{:S(2)}) copy-start(f32[512]{0:T(512)} %param.48) | copy-start | bytes 6148
  0.1 10.1 %copy-start.9 = (f32[512]{0:T(512)S(1)}, f32[512]{0:T(512)}, u32[]{:S(2)}) copy-start(f32[512]{0:T(512)} %param.59) | copy-start | bytes 6148
  2.8 23.6 %all-to-all-start = ((f32[32,8,512]{2,1,0:T(8,128)}), f32[32,8,512]{2,1,0:T(8,128)S(1)}, u32[]{:S(2)}, u32[]{:S(2)}) async-start(f32[32,8,512]{2,1,0:T(8,128)} %bitcast.34), calls=%async_computation | async-start | bytes 1048576 | tf_op jit(solution)/shard_map/all_to_all | solution.py:580
  26.3 6.5 %copy-start.10 = (f32[4,512]{1,0:T(4,128)S(1)}, f32[4,512]{1,0:T(4,128)}, u32[]{:S(2)}) copy-start(f32[4,512]{1,0:T(4,128)} %weight_geometry.3) | copy-start | bytes 24580
  26.3 6.5 %copy-start.11 = (f32[4,1,256]{2,1,0:T(1,128)S(1)}, f32[4,1,256]{2,1,0:T(1,128)}, u32[]{:S(2)}) copy-start(f32[4,1,256]{2,1,0:T(1,128)} %geometry.3) | copy-start | bytes 12292
  26.3 6.5 %copy-start.12 = (f32[512]{0:T(512)S(1)}, f32[512]{0:T(512)}, u32[]{:S(2)}) copy-start(f32[512]{0:T(512)} %param.52) | copy-start | bytes 6148
  26.4 6.5 %copy-start.13 = (f32[512]{0:T(512)S(1)}, f32[512]{0:T(512)}, u32[]{:S(2)}) copy-start(f32[512]{0:T(512)} %param.57) | copy-start | bytes 6148
  26.4 6.5 %copy-start.14 = (s32[1,256]{1,0:T(1,128)S(1)}, s32[1,256]{1,0:T(1,128)}, u32[]{:S(2)}) copy-start(s32[1,256]{1,0:T(1,128)} %mesh_targets.1) | copy-start | bytes 3076
  30.0 18.9 %all-to-all-start.1 = ((f32[32,8,512]{2,1,0:T(8,128)}), f32[32,8,512]{2,1,0:T(8,128)S(1)}, u32[]{:S(2)}, u32[]{:S(2)}) async-start(f32[32,8,512]{2,1,0:T(8,128)} %bitcast.36), calls=%async_computation.1 | async-start | bytes 1048576 | tf_op jit(solution)/shard_map/all_to_all | solution.py:580

commit v7 on v6

--- a/solution.py
+++ b/solution.py
@@ -174,14 +174,14 @@
     sender_high,
     sender_low,
     merged_high,
-    merged_low,
+    output_high,
     received,
     biases,
     self_all_ref,
     self_sent_ref,
     nodes_sent_ref,
     match_ref,
-    output_high_ref,
+    merged_low_ref,
     onward_high_ref,
     onward_low_ref,
     update_high_ref,
@@ -207,7 +207,7 @@
     self_sent,
     nodes_sent,
     match,
-    output_high,
+    merged_low,
     onward_high,
     onward_low,
     update_high,
@@ -259,7 +259,7 @@
     high, low = split(summed[...])
     merged_high[...], merged_low[...] = split(dot3(centred, high, low))
     output_high[...] = centred.astype(BF16)
-    store((output_high, output_high_ref))
+    store((merged_low, merged_low_ref))
     first_bias = centre(output_bias[...])
     first_bias_on = dot3(rows_of(first_bias), high, low)[0:1, :]
     gather_rows(
@@ -309,14 +309,13 @@
     wait(*stores)
 
 
-def edges(hidden, merged_high, merged_low, output_high, bias, bias_on, loads=()):
+def edges(hidden, merged_high, merged_low, output_high, bias, bias_on, load_low=()):
     hidden_high, hidden_low = split(hidden)
+    normed = scale(dot(hidden_high, output_high[...]) + bias)
     high = merged_high[...]
-    total = dot(hidden_high, high) + (
-        dot(hidden_low, high) + dot(hidden_high, merged_low[...])
-    )
-    wait(*loads)
-    return (total + bias_on) * scale(dot(hidden_high, output_high[...]) + bias)
+    total = dot(hidden_high, high) + dot(hidden_low, high)
+    wait(*load_low)
+    return (total + dot(hidden_high, merged_low[...]) + bias_on) * normed
 
 
 def encode_kernel(
@@ -324,10 +323,10 @@
     sender_high,
     sender_low,
     merged_high,
-    merged_low,
+    output_high,
     received,
     biases,
-    output_high_ref,
+    merged_low_ref,
     match_ref,
     self_sent_ref,
     onward_high_ref,
@@ -336,7 +335,7 @@
     nodes_sent_ref,
     sent_ref,
     parts_ref,
-    output_high,
+    merged_low,
     match,
     self_sent,
     onward_high,
@@ -348,7 +347,7 @@
     semaphores,
 ):
     copies = Copies(semaphores)
-    load_output = copies.start(output_high_ref, output_high)
+    load_merged = copies.start(merged_low_ref, merged_low)
     load_match = copies.start(match_ref, match)
     load_self = copies.start(self_sent_ref, self_sent)
     load_onward_high = copies.start(onward_high_ref, onward_high)
@@ -358,15 +357,24 @@
     started()
     hidden = silu(dot3(arrived[...], sender_high[...], sender_low[...]) + received[...])
     part = edges(
-        hidden, merged_high, merged_low, output_high, biases[0:1, :], biases[1:2, :], [load_output]
+        hidden, merged_high, merged_low, output_high, biases[0:1, :], biases[1:2, :], [load_merged]
     )
     parts[...] = part
     store_parts = copies.start(parts, parts_ref)
     wait(load_match, load_self)
     hidden = silu(self_sent[...] + pick(match[...], part))
-    wait(load_onward_high, load_onward_low, load_update, load_nodes)
-    sent[...] = nodes_sent[...] + edges(
-        hidden, onward_high, onward_low, update_high, biases[2:3, :], biases[3:4, :]
+    wait(load_onward_high, load_update)
+    sent[...] = (
+        edges(
+            hidden,
+            onward_high,
+            onward_low,
+            update_high,
+            biases[2:3, :],
+            biases[3:4, :],
+            [load_onward_low, load_nodes],
+        )
+        + nodes_sent[...]
     )
     store_sent = copies.start(sent, sent_ref)
     wait(store_parts, store_sent)
@@ -646,7 +654,7 @@
         self_sent,
         nodes_sent,
         match,
-        output_high,
+        first_low,
         onward_high,
         onward_low,
         update_high,
@@ -710,7 +718,7 @@
         [],
         [],
         [grid_in, *first],
-        [output_high, match, self_sent, onward_high, onward_low, update_high, nodes_sent],
+        [first_low, match, self_sent, onward_high, onward_low, update_high, nodes_sent],
         [flat((mesh_slots, width)), flat((grid_slots, width))],
     )
     mesh_in = exchange(sent, patches)

time: 52.9 us -> 52.7 us (level)
  transfers between devices with their start and end apart: 2 -> 2, of which waited for: 2 -> 2; matrix products, arithmetic and copies ran while one was open for 0% -> 0% of each run, Pallas kernels for 38% -> 39%
where the time goes in v7:
time: 52.7 us; the launch traced here: 52.3 us
  Pallas kernels  29.8 us (57%)
  waiting for transfers between devices  11.9 us (23%)
  starting transfers between devices  10.1 us (19%)
    pallas_call x5, Pallas kernels, call(): pl.pallas_call(kernel, out_shape=[pltpu.VMEM(array.shape, array.dtype) fo...  29.8 us
    all_to_all x2, waiting for transfers between devices, exchange(): lax.all_to_all(blocks, ('lat', 'lon'), split_axis=0, concat_axis=0, tiled...  11.9 us
    all_to_all x2, starting transfers between devices, exchange(): lax.all_to_all(blocks, ('lat', 'lon'), split_axis=0, concat_axis=0, tiled...  10.1 us
  transfers between devices with their start and end apart: 2, of which 2 were waited for; matrix products, arithmetic and copies ran while one was open for 0% of the time, Pallas kernels for 39%

profile of v7, /device:TPU:0, one launch (start us, length us, event | category | flops | bytes accessed | tf_op | source)
XLA Modules:
  0.0 52.3 jit_solution(6279237449853064929)
XLA Ops:
  0.0 0.0 copy-start
  0.0 0.0 copy-start.1
  0.0 0.0 copy-start.2
  0.0 0.0 copy-start.3
  0.0 0.0 copy-start.4
  0.0 0.0 copy-start.5
  0.0 0.0 copy-start.6
  0.0 0.0 copy-start.7
  0.0 0.0 copy-start.8
  0.1 0.0 copy-start.9
  0.1 2.7 %pack.1 = f32[256,512]{1,0:T(8,128)} custom-call(s32[8,32]{1,0:T(8,128)} %bitcast.37, f32[720,512]{1,0:T(8,128)} %bitcast.35), custom_call_target="tpu_custom_call" | custom-call | flops 1000 | bytes 4194304 | tf_op jit(solution)/shard_map/pack/pallas_call | solution.py:568
  2.8 7.3 %all-to-all-start = ((f32[32,8,512]{2,1,0:T(8,128)}), f32[32,8,512]{2,1,0:T(8,128)S(1)}, u32[]{:S(2)}, u32[]{:S(2)}) async-start(f32[32,8,512]{2,1,0:T(8,128)} %bitcast.34), calls=%async_computation | async-start | bytes 1048576 | tf_op jit(solution)/shard_map/all_to_all | solution.py:588
  10.1 0.0 copy-done
  10.1 0.0 copy-done.1
  10.1 0.0 copy-done.2
  10.1 0.0 copy-done.3
  10.2 0.0 copy-done.4
  10.2 0.0 copy-done.5
  10.2 0.0 copy-done.6
  10.2 0.0 copy-done.7
  10.2 0.0 copy-done.8
  10.2 0.0 copy-done.9
  10.2 11.1 %before.1 = (bf16[512,512]{1,0:T(8,128)(2,1)S(1)}, bf16[512,512]{1,0:T(8,128)(2,1)S(1)}, bf16[512,512]{1,0:T(8,128)(2,1)S(1)}, bf16[512,512]{1,0:T(8,128)(2,1)S(...) custom-call(s32[1,256]{1,0:T(1,128)S(1)} %copy-done.3, ...), custom_call_target="tpu_custom_call" | custom-call | flops 1409286144 | bytes 4194304 | tf_op jit(solution)/shard_map/before/pallas_call | solution.py:568
  21.3 5.0 %all-to-all-done = f32[32,8,512]{2,1,0:T(8,128)S(1)} async-done(((f32[32,8,512]{2,1,0:T(8,128)}), f32[32,8,512]{2,1,0:T(8,128)S(1)}, u32[]{:S(2)}, u32[]{:S(2)}) %all-to-all-start) | async-done | bytes 524320 | tf_op jit(solution)/shard_map/all_to_all | solution.py:588
  26.3 0.0 copy-start.10
  26.3 0.0 copy-start.11
  26.3 0.0 copy-start.12
  26.4 0.0 copy-start.13
  26.4 0.0 copy-start.14
  26.4 3.5 %encode.1 = (f32[256,512]{1,0:T(8,128)}, f32[256,512]{1,0:T(8,128)}) custom-call(f32[256,512]{1,0:T(8,128)S(1)} %bitcast.21, bf16[512,512]{1,0:T(8,128)(2,1)S(1)} %get-tuple-element.38.sender_high, bf16[512,512]{1,0:T(8,128)(2,1)S(1)} %get-tuple-element.39.sender_low, bf16[512,512]{1,0:T(8,128)(2,1)S(1)} %get-tuple-element.40.merged_high, ...), custom_call_target="tpu_custom_call" | custom-call | flops 1610612736 | bytes 4194304 | tf_op jit(solution)/shard_map/encode/pallas_call | solution.py:568
  29.9 2.8 %all-to-all-start.1 = ((f32[32,8,512]{2,1,0:T(8,128)}), f32[32,8,512]{2,1,0:T(8,128)S(1)}, u32[]{:S(2)}, u32[]{:S(2)}) async-start(f32[32,8,512]{2,1,0:T(8,128)} %bitcast.36), calls=%async_computation.1 | async-start | bytes 1048576 | tf_op jit(solution)/shard_map/all_to_all | solution.py:588
  32.7 0.0 copy-done.10
  32.7 0.0 copy-done.11
  32.7 0.0 copy-done.12
  32.7 0.0 copy-done.13
  32.7 0.0 copy-done.14
  32.7 9.1 %between.1 = (bf16[512,512]{1,0:T(8,128)(2,1)S(1)}, bf16[512,512]{1,0:T(8,128)(2,1)S(1)}, bf16[512,512]{1,0:T(8,128)(2,1)S(1)}, f32[256,512]{1,0:T(8,128)S(1)}, ...) custom-call(s32[1,256]{1,0:T(1,128)S(1)} %copy-done.14, ...), custom_call_target="tpu_custom_call" | custom-call | flops 3422552064 | bytes 4194304 | tf_op jit(solution)/shard_map/between/pallas_call | solution.py:568
  41.8 6.9 %all-to-all-done.1 = f32[32,8,512]{2,1,0:T(8,128)S(1)} async-done(((f32[32,8,512]{2,1,0:T(8,128)}), f32[32,8,512]{2,1,0:T(8,128)S(1)}, u32[]{:S(2)}, u32[]{:S(2)}) %all-to-all-start.1) | async-done | bytes 524320 | tf_op jit(solution)/shard_map/all_to_all | solution.py:588
  48.7 3.4 %refine.1 = f32[640,512]{1,0:T(8,128)} custom-call(f32[256,512]{1,0:T(8,128)S(1)} %bitcast.22, bf16[512,512]{1,0:T(8,128)(2,1)S(1)} %get-tuple-element.61.merged_high, bf16[512,512]{1,0:T(8,128)(2,1)S(1)} %get-tuple-element.62.merged_low, bf16[512,512]{1,0:T(8,128)(2,1)S(1)} %get-tuple-element.63.output_high, f32[256,512]{1,0:T(8,128)S(1)} %get-tuple-element.64.received, ...), custom_call_target="tpu_custom_call" | custom-call | flops 1610612736 | bytes 4194304 | tf_op jit(solution)/shard_map/refine/pallas_call | solution.py:568
Async XLA Ops:
  0.0 10.1 %copy-start = (f32[4,512]{1,0:T(4,128)S(1)}, f32[4,512]{1,0:T(4,128)}, u32[]{:S(2)}) copy-start(f32[4,512]{1,0:T(4,128)} %weight_geometry.2) | copy-start | bytes 24580
  0.0 10.1 %copy-start.1 = (s32[1,32,8]{1,2,0:T(8,128)S(1)}, s32[1,32,8]{1,2,0:T(8,128)}, u32[]{:S(2)}) copy-start(s32[1,32,8]{1,2,0:T(8,128)} %param.35) | copy-start | bytes 3076
  0.0 10.1 %copy-start.2 = (f32[4,1,256]{2,1,0:T(1,128)S(1)}, f32[4,1,256]{2,1,0:T(1,128)}, u32[]{:S(2)}) copy-start(f32[4,1,256]{2,1,0:T(1,128)} %geometry.2) | copy-start | bytes 12292
  0.0 10.1 %copy-start.3 = (s32[1,256]{1,0:T(1,128)S(1)}, s32[1,256]{1,0:T(1,128)}, u32[]{:S(2)}) copy-start(s32[1,256]{1,0:T(1,128)} %grid_targets.3) | copy-start | bytes 3076
  0.0 10.1 %copy-start.4 = (f32[512]{0:T(512)S(1)}, f32[512]{0:T(512)}, u32[]{:S(2)}) copy-start(f32[512]{0:T(512)} %param.41) | copy-start | bytes 6148
  0.0 10.1 %copy-start.5 = (f32[512]{0:T(512)S(1)}, f32[512]{0:T(512)}, u32[]{:S(2)}) copy-start(f32[512]{0:T(512)} %param.46) | copy-start | bytes 6148
  0.0 10.1 %copy-start.6 = (f32[512]{0:T(512)S(1)}, f32[512]{0:T(512)}, u32[]{:S(2)}) copy-start(f32[512]{0:T(512)} %param.43) | copy-start | bytes 6148
  0.0 10.1 %copy-start.7 = (f32[512]{0:T(512)S(1)}, f32[512]{0:T(512)}, u32[]{:S(2)}) copy-start(f32[512]{0:T(512)} %param.54) | copy-start | bytes 6148
  0.0 10.1 %copy-start.8 = (f32[512]{0:T(512)S(1)}, f32[512]{0:T(512)}, u32[]{:S(2)}) copy-start(f32[512]{0:T(512)} %param.48) | copy-start | bytes 6148
  0.1 10.1 %copy-start.9 = (f32[512]{0:T(512)S(1)}, f32[512]{0:T(512)}, u32[]{:S(2)}) copy-start(f32[512]{0:T(512)} %param.59) | copy-start | bytes 6148
  2.8 23.6 %all-to-all-start = ((f32[32,8,512]{2,1,0:T(8,128)}), f32[32,8,512]{2,1,0:T(8,128)S(1)}, u32[]{:S(2)}, u32[]{:S(2)}) async-start(f32[32,8,512]{2,1,0:T(8,128)} %bitcast.34), calls=%async_computation | async-start | bytes 1048576 | tf_op jit(solution)/shard_map/all_to_all | solution.py:588
  26.3 6.3 %copy-start.10 = (f32[4,512]{1,0:T(4,128)S(1)}, f32[4,512]{1,0:T(4,128)}, u32[]{:S(2)}) copy-start(f32[4,512]{1,0:T(4,128)} %weight_geometry.3) | copy-start | bytes 24580
  26.3 6.3 %copy-start.11 = (f32[4,1,256]{2,1,0:T(1,128)S(1)}, f32[4,1,256]{2,1,0:T(1,128)}, u32[]{:S(2)}) copy-start(f32[4,1,256]{2,1,0:T(1,128)} %geometry.3) | copy-start | bytes 12292
  26.3 6.4 %copy-start.12 = (f32[512]{0:T(512)S(1)}, f32[512]{0:T(512)}, u32[]{:S(2)}) copy-start(f32[512]{0:T(512)} %param.52) | copy-start | bytes 6148
  26.4 6.4 %copy-start.13 = (f32[512]{0:T(512)S(1)}, f32[512]{0:T(512)}, u32[]{:S(2)}) copy-start(f32[512]{0:T(512)} %param.57) | copy-start | bytes 6148
  26.4 6.4 %copy-start.14 = (s32[1,256]{1,0:T(1,128)S(1)}, s32[1,256]{1,0:T(1,128)}, u32[]{:S(2)}) copy-start(s32[1,256]{1,0:T(1,128)} %mesh_targets.1) | copy-start | bytes 3076
  29.9 18.9 %all-to-all-start.1 = ((f32[32,8,512]{2,1,0:T(8,128)}), f32[32,8,512]{2,1,0:T(8,128)S(1)}, u32[]{:S(2)}, u32[]{:S(2)}) async-start(f32[32,8,512]{2,1,0:T(8,128)} %bitcast.36), calls=%async_computation.1 | async-start | bytes 1048576 | tf_op jit(solution)/shard_map/all_to_all | solution.py:588

commit v8 on v7

--- a/solution.py
+++ b/solution.py
@@ -10,7 +10,6 @@
 F32 = jnp.float32
 BF16 = jnp.bfloat16
 VMEM = pl.BlockSpec(memory_space=pltpu.VMEM)
-SMEM = pl.BlockSpec(memory_space=pltpu.SMEM)
 HBM = pl.BlockSpec(memory_space=pltpu.HBM)
 
 
@@ -223,6 +222,7 @@
     table,
     chosen,
     semaphores,
+    pending,
 ):
     copies = Copies(semaphores)
     load_nodes = copies.start(nodes_ref, nodes)
@@ -237,6 +237,7 @@
     load_summed_2 = copies.start(summed_ref_2, summed_2)
     load_refine = copies.start(refine_ref, refine)
     started()
+    wait(*pending)
     stores = []
 
     def store(*pairs):
@@ -432,6 +433,7 @@
     table,
     chosen,
     semaphores,
+    pending,
 ):
     copies = Copies(semaphores)
     load_parts = copies.start(parts_ref, parts)
@@ -450,6 +452,7 @@
         copies.start(biases_ref, biases),
     ]
     started()
+    wait(*pending)
     stores = []
     one_hot = target_matrix(nodes.shape[0], grid_targets).astype(BF16)
     table[...] = target_matrix(table.shape[0], mesh_targets)
@@ -559,28 +562,41 @@
 def call(
     kernel, name, flops, scalars, small, kept, large, results, held=(), scratch=(), direct=()
 ):
-    direct = [pltpu.with_memory_space_constraint(array, pltpu.HBM) for array in direct]
+    hbm = lambda arrays: [pltpu.with_memory_space_constraint(x, pltpu.HBM) for x in arrays]
+    ahead = hbm([*scalars, *small])
     kept = [pltpu.with_memory_space_constraint(array, pltpu.VMEM) for array in kept]
-    large = [pltpu.with_memory_space_constraint(array, pltpu.HBM) for array in large]
+    direct = hbm(direct)
+    large = hbm(large)
+    landing = [pltpu.SMEM(x.shape, x.dtype) for x in scalars]
+    landing += [pltpu.VMEM(x.shape, x.dtype) for x in small]
     twins = [pltpu.VMEM(array.shape, array.dtype) for array in [*large, *results]]
     twins += list(scratch)
     size = sum(4 * spec.inner_aval.size for spec in twins)
+    count = len(ahead)
+
+    def with_pending(*refs):
+        *landed, semaphores = refs[len(refs) - count - 1 :]
+        copies = Copies(semaphores)
+        pending = [copies.start(*pair) for pair in zip(refs[:count], landed, strict=True)]
+        kernel(*landed, *refs[count : len(refs) - count - 1], pending)
+
+    if count:
+        landing.append(pltpu.SemaphoreType.DMA((count,)))
     return pl.pallas_call(
-        kernel,
+        with_pending if count else kernel,
         out_shape=[pltpu.VMEM(array.shape, array.dtype) for array in held]
         + [pltpu.HBM(array.shape, array.dtype) for array in results],
-        in_specs=[SMEM] * len(scalars)
-        + [VMEM] * (len(small) + len(kept))
-        + [HBM] * (len(direct) + len(large)),
+        in_specs=[HBM] * count + [VMEM] * len(kept) + [HBM] * (len(direct) + len(large)),
         out_specs=[VMEM] * len(held) + [HBM] * len(results),
         scratch_shapes=[
             *twins,
             pltpu.SemaphoreType.DMA((len(direct) + len(large) + len(results) + 8,)),
+            *landing,
         ],
         cost_estimate=pl.CostEstimate(flops=flops, bytes_accessed=4 * 2**20, transcendentals=0),
         compiler_params=pltpu.CompilerParams(vmem_limit_bytes=size + 12 * 2**20),
         name=name,
-    )(*scalars, *small, *kept, *direct, *large)
+    )(*ahead, *kept, *direct, *large)
 
 
 def exchange(rows, patches):

time: 52.7 us -> 52.5 us (level)
  Pallas kernels: 29.8 us -> 33.1 us
  waiting for transfers between devices: 11.9 us -> 8.64 us
    pallas_call x5, Pallas kernels: 29.8 us -> 33.1 us  [call(): pl.pallas_call(with_pending if count else kernel, out_shape=[pltpu.VMEM(a...]
    all_to_all x2, waiting for transfers between devices: 11.9 us -> 8.64 us  [exchange(): lax.all_to_all(blocks, ('lat', 'lon'), split_axis=0, concat_axis=0, tiled...]
  transfers between devices with their start and end apart: 2 -> 2, of which waited for: 2 -> 2; matrix products, arithmetic and copies ran while one was open for 0% -> 0% of each run, Pallas kernels for 39% -> 45%
where the time goes in v8:
time: 52.5 us; the launch traced here: 52.2 us
  Pallas kernels  33.1 us (63%)
  starting transfers between devices  10.2 us (19%)
  waiting for transfers between devices  8.64 us (16%)
    pallas_call x5, Pallas kernels, call(): pl.pallas_call(with_pending if count else kernel, out_shape=[pltpu.VMEM(a...  33.1 us
    all_to_all x2, starting transfers between devices, exchange(): lax.all_to_all(blocks, ('lat', 'lon'), split_axis=0, concat_axis=0, tiled...  10.2 us
    all_to_all x2, waiting for transfers between devices, exchange(): lax.all_to_all(blocks, ('lat', 'lon'), split_axis=0, concat_axis=0, tiled...  8.64 us
  transfers between devices with their start and end apart: 2, of which 2 were waited for; matrix products, arithmetic and copies ran while one was open for 0% of the time, Pallas kernels for 45%

profile of v8, /device:TPU:0, one launch (start us, length us, event | category | flops | bytes accessed | tf_op | source)
XLA Modules:
  0.0 52.2 jit_solution(9334327361429964068)
XLA Ops:
  0.0 2.6 %pack.1 = f32[256,512]{1,0:T(8,128)} custom-call(s32[8,32]{1,0:T(8,128)} %bitcast.26, f32[720,512]{1,0:T(8,128)} %bitcast.24), custom_call_target="tpu_custom_call" | custom-call | flops 1000 | bytes 4194304 | tf_op jit(solution)/shard_map/pack/pallas_call | solution.py:585
  2.6 7.3 %all-to-all-start = ((f32[32,8,512]{2,1,0:T(8,128)}), f32[32,8,512]{2,1,0:T(8,128)S(1)}, u32[]{:S(2)}, u32[]{:S(2)}) async-start(f32[32,8,512]{2,1,0:T(8,128)} %bitcast.23), calls=%async_computation | async-start | bytes 1048576 | tf_op jit(solution)/shard_map/all_to_all | solution.py:604
  10.0 13.1 %before.1 = (bf16[512,512]{1,0:T(8,128)(2,1)S(1)}, bf16[512,512]{1,0:T(8,128)(2,1)S(1)}, bf16[512,512]{1,0:T(8,128)(2,1)S(1)}, bf16[512,512]{1,0:T(8,128)(2,1)S(...) custom-call(s32[1,256]{1,0:T(1,128)} %refs_1_.1, ...), custom_call_target="tpu_custom_call" | custom-call | flops 1409286144 | bytes 4194304 | tf_op jit(solution)/shard_map/before/pallas_call | solution.py:585
  23.0 3.2 %all-to-all-done = f32[32,8,512]{2,1,0:T(8,128)S(1)} async-done(((f32[32,8,512]{2,1,0:T(8,128)}), f32[32,8,512]{2,1,0:T(8,128)S(1)}, u32[]{:S(2)}, u32[]{:S(2)}) %all-to-all-start) | async-done | bytes 524320 | tf_op jit(solution)/shard_map/all_to_all | solution.py:604
  26.2 3.5 %encode.1 = (f32[256,512]{1,0:T(8,128)}, f32[256,512]{1,0:T(8,128)}) custom-call(f32[256,512]{1,0:T(8,128)S(1)} %bitcast.21, bf16[512,512]{1,0:T(8,128)(2,1)S(1)} %get-tuple-element.38.sender_high, bf16[512,512]{1,0:T(8,128)(2,1)S(1)} %get-tuple-element.39.sender_low, bf16[512,512]{1,0:T(8,128)(2,1)S(1)} %get-tuple-element.40.merged_high, ...), custom_call_target="tpu_custom_call" | custom-call | flops 1610612736 | bytes 4194304 | tf_op jit(solution)/shard_map/encode/pallas_call | solution.py:585
  29.7 2.9 %all-to-all-start.1 = ((f32[32,8,512]{2,1,0:T(8,128)}), f32[32,8,512]{2,1,0:T(8,128)S(1)}, u32[]{:S(2)}, u32[]{:S(2)}) async-start(f32[32,8,512]{2,1,0:T(8,128)} %bitcast.25), calls=%async_computation.1 | async-start | bytes 1048576 | tf_op jit(solution)/shard_map/all_to_all | solution.py:604
  32.5 10.6 %between.1 = (bf16[512,512]{1,0:T(8,128)(2,1)S(1)}, bf16[512,512]{1,0:T(8,128)(2,1)S(1)}, bf16[512,512]{1,0:T(8,128)(2,1)S(1)}, f32[256,512]{1,0:T(8,128)S(1)}, ...) custom-call(s32[1,256]{1,0:T(1,128)} %refs_2_.3, ...), custom_call_target="tpu_custom_call" | custom-call | flops 3422552064 | bytes 4194304 | tf_op jit(solution)/shard_map/between/pallas_call | solution.py:585
  43.1 5.5 %all-to-all-done.1 = f32[32,8,512]{2,1,0:T(8,128)S(1)} async-done(((f32[32,8,512]{2,1,0:T(8,128)}), f32[32,8,512]{2,1,0:T(8,128)S(1)}, u32[]{:S(2)}, u32[]{:S(2)}) %all-to-all-start.1) | async-done | bytes 524320 | tf_op jit(solution)/shard_map/all_to_all | solution.py:604
  48.6 3.4 %refine.1 = f32[640,512]{1,0:T(8,128)} custom-call(f32[256,512]{1,0:T(8,128)S(1)} %bitcast.22, bf16[512,512]{1,0:T(8,128)(2,1)S(1)} %get-tuple-element.61.merged_high, bf16[512,512]{1,0:T(8,128)(2,1)S(1)} %get-tuple-element.62.merged_low, bf16[512,512]{1,0:T(8,128)(2,1)S(1)} %get-tuple-element.63.output_high, f32[256,512]{1,0:T(8,128)S(1)} %get-tuple-element.64.received, ...), custom_call_target="tpu_custom_call" | custom-call | flops 1610612736 | bytes 4194304 | tf_op jit(solution)/shard_map/refine/pallas_call | solution.py:585
Async XLA Ops:
  2.6 23.6 %all-to-all-start = ((f32[32,8,512]{2,1,0:T(8,128)}), f32[32,8,512]{2,1,0:T(8,128)S(1)}, u32[]{:S(2)}, u32[]{:S(2)}) async-start(f32[32,8,512]{2,1,0:T(8,128)} %bitcast.23), calls=%async_computation | async-start | bytes 1048576 | tf_op jit(solution)/shard_map/all_to_all | solution.py:604
  29.7 18.9 %all-to-all-start.1 = ((f32[32,8,512]{2,1,0:T(8,128)}), f32[32,8,512]{2,1,0:T(8,128)S(1)}, u32[]{:S(2)}, u32[]{:S(2)}) async-start(f32[32,8,512]{2,1,0:T(8,128)} %bitcast.25), calls=%async_computation.1 | async-start | bytes 1048576 | tf_op jit(solution)/shard_map/all_to_all | solution.py:604

commit v9 on v8

--- a/solution.py
+++ b/solution.py
@@ -237,15 +237,16 @@
     load_summed_2 = copies.start(summed_ref_2, summed_2)
     load_refine = copies.start(refine_ref, refine)
     started()
-    wait(*pending)
     stores = []
 
     def store(*pairs):
         stores.extend(copies.start(source, target) for source, target in pairs)
 
+    wait(load_nodes, load_self)
+    self_all[...] = dot3(nodes[...], *split(weight_self[...]))
+    wait(*pending)
+    self_all[...] = self_all[...] + node_bias[...]
     table[...] = target_matrix(nodes.shape[0], grid_targets)
-    wait(load_nodes, load_self)
-    self_all[...] = dot3(nodes[...], *split(weight_self[...])) + node_bias[...]
     store((self_all, self_all_ref))
     gather_rows(
         0,

time: 52.5 us -> 52.5 us (level)
  waiting for transfers between devices: 8.64 us -> 9.95 us
  Pallas kernels: 33.1 us -> 31.8 us
    all_to_all x2, waiting for transfers between devices: 8.64 us -> 9.95 us  [exchange(): lax.all_to_all(blocks, ('lat', 'lon'), split_axis=0, concat_axis=0, tiled...]
    pallas_call x5, Pallas kernels: 33.1 us -> 31.8 us  [call(): pl.pallas_call(with_pending if count else kernel, out_shape=[pltpu.VMEM(a...]
  transfers between devices with their start and end apart: 2 -> 2, of which waited for: 2 -> 2; matrix products, arithmetic and copies ran while one was open for 0% -> 0% of each run, Pallas kernels for 45% -> 43%
where the time goes in v9:
time: 52.5 us; the launch traced here: 52.1 us
  Pallas kernels  31.8 us (61%)
  starting transfers between devices  10.1 us (19%)
  waiting for transfers between devices  9.95 us (19%)
    pallas_call x5, Pallas kernels, call(): pl.pallas_call(with_pending if count else kernel, out_shape=[pltpu.VMEM(a...  31.8 us
    all_to_all x2, starting transfers between devices, exchange(): lax.all_to_all(blocks, ('lat', 'lon'), split_axis=0, concat_axis=0, tiled...  10.1 us
    all_to_all x2, waiting for transfers between devices, exchange(): lax.all_to_all(blocks, ('lat', 'lon'), split_axis=0, concat_axis=0, tiled...  9.95 us
  transfers between devices with their start and end apart: 2, of which 2 were waited for; matrix products, arithmetic and copies ran while one was open for 0% of the time, Pallas kernels for 43%

profile of v9, /device:TPU:0, one launch (start us, length us, event | category | flops | bytes accessed | tf_op | source)
XLA Modules:
  0.0 52.1 jit_solution(16209481125114355035)
XLA Ops:
  0.0 2.6 %pack.1 = f32[256,512]{1,0:T(8,128)} custom-call(s32[8,32]{1,0:T(8,128)} %bitcast.26, f32[720,512]{1,0:T(8,128)} %bitcast.24), custom_call_target="tpu_custom_call" | custom-call | flops 1000 | bytes 4194304 | tf_op jit(solution)/shard_map/pack/pallas_call | solution.py:586
  2.6 7.3 %all-to-all-start = ((f32[32,8,512]{2,1,0:T(8,128)}), f32[32,8,512]{2,1,0:T(8,128)S(1)}, u32[]{:S(2)}, u32[]{:S(2)}) async-start(f32[32,8,512]{2,1,0:T(8,128)} %bitcast.23), calls=%async_computation | async-start | bytes 1048576 | tf_op jit(solution)/shard_map/all_to_all | solution.py:605
  10.0 11.7 %before.1 = (bf16[512,512]{1,0:T(8,128)(2,1)S(1)}, bf16[512,512]{1,0:T(8,128)(2,1)S(1)}, bf16[512,512]{1,0:T(8,128)(2,1)S(1)}, bf16[512,512]{1,0:T(8,128)(2,1)S(...) custom-call(s32[1,256]{1,0:T(1,128)} %refs_1_.1, ...), custom_call_target="tpu_custom_call" | custom-call | flops 1409286144 | bytes 4194304 | tf_op jit(solution)/shard_map/before/pallas_call | solution.py:586
  21.7 4.5 %all-to-all-done = f32[32,8,512]{2,1,0:T(8,128)S(1)} async-done(((f32[32,8,512]{2,1,0:T(8,128)}), f32[32,8,512]{2,1,0:T(8,128)S(1)}, u32[]{:S(2)}, u32[]{:S(2)}) %all-to-all-start) | async-done | bytes 524320 | tf_op jit(solution)/shard_map/all_to_all | solution.py:605
  26.2 3.5 %encode.1 = (f32[256,512]{1,0:T(8,128)}, f32[256,512]{1,0:T(8,128)}) custom-call(f32[256,512]{1,0:T(8,128)S(1)} %bitcast.21, bf16[512,512]{1,0:T(8,128)(2,1)S(1)} %get-tuple-element.38.sender_high, bf16[512,512]{1,0:T(8,128)(2,1)S(1)} %get-tuple-element.39.sender_low, bf16[512,512]{1,0:T(8,128)(2,1)S(1)} %get-tuple-element.40.merged_high, ...), custom_call_target="tpu_custom_call" | custom-call | flops 1610612736 | bytes 4194304 | tf_op jit(solution)/shard_map/encode/pallas_call | solution.py:586
  29.7 2.8 %all-to-all-start.1 = ((f32[32,8,512]{2,1,0:T(8,128)}), f32[32,8,512]{2,1,0:T(8,128)S(1)}, u32[]{:S(2)}, u32[]{:S(2)}) async-start(f32[32,8,512]{2,1,0:T(8,128)} %bitcast.25), calls=%async_computation.1 | async-start | bytes 1048576 | tf_op jit(solution)/shard_map/all_to_all | solution.py:605
  32.5 10.6 %between.1 = (bf16[512,512]{1,0:T(8,128)(2,1)S(1)}, bf16[512,512]{1,0:T(8,128)(2,1)S(1)}, bf16[512,512]{1,0:T(8,128)(2,1)S(1)}, f32[256,512]{1,0:T(8,128)S(1)}, ...) custom-call(s32[1,256]{1,0:T(1,128)} %refs_2_.3, ...), custom_call_target="tpu_custom_call" | custom-call | flops 3422552064 | bytes 4194304 | tf_op jit(solution)/shard_map/between/pallas_call | solution.py:586
  43.0 5.5 %all-to-all-done.1 = f32[32,8,512]{2,1,0:T(8,128)S(1)} async-done(((f32[32,8,512]{2,1,0:T(8,128)}), f32[32,8,512]{2,1,0:T(8,128)S(1)}, u32[]{:S(2)}, u32[]{:S(2)}) %all-to-all-start.1) | async-done | bytes 524320 | tf_op jit(solution)/shard_map/all_to_all | solution.py:605
  48.5 3.4 %refine.1 = f32[640,512]{1,0:T(8,128)} custom-call(f32[256,512]{1,0:T(8,128)S(1)} %bitcast.22, bf16[512,512]{1,0:T(8,128)(2,1)S(1)} %get-tuple-element.61.merged_high, bf16[512,512]{1,0:T(8,128)(2,1)S(1)} %get-tuple-element.62.merged_low, bf16[512,512]{1,0:T(8,128)(2,1)S(1)} %get-tuple-element.63.output_high, f32[256,512]{1,0:T(8,128)S(1)} %get-tuple-element.64.received, ...), custom_call_target="tpu_custom_call" | custom-call | flops 1610612736 | bytes 4194304 | tf_op jit(solution)/shard_map/refine/pallas_call | solution.py:586
Async XLA Ops:
  2.6 23.6 %all-to-all-start = ((f32[32,8,512]{2,1,0:T(8,128)}), f32[32,8,512]{2,1,0:T(8,128)S(1)}, u32[]{:S(2)}, u32[]{:S(2)}) async-start(f32[32,8,512]{2,1,0:T(8,128)} %bitcast.23), calls=%async_computation | async-start | bytes 1048576 | tf_op jit(solution)/shard_map/all_to_all | solution.py:605
  29.7 18.9 %all-to-all-start.1 = ((f32[32,8,512]{2,1,0:T(8,128)}), f32[32,8,512]{2,1,0:T(8,128)S(1)}, u32[]{:S(2)}, u32[]{:S(2)}) async-start(f32[32,8,512]{2,1,0:T(8,128)} %bitcast.25), calls=%async_computation.1 | async-start | bytes 1048576 | tf_op jit(solution)/shard_map/all_to_all | solution.py:605
